TPU v7x, 256 devices: a 4x2x16 block of a 4x16x16 slice. The times are simulated.
256 devices in a mesh: grp: 2 (over y), slab: 32 (over z, core), ang: 4 (over x).
Axes of the slice: x: 4, y: 2, z: 16, core: 2. Of those that a mesh axis runs over, the one named last changes fastest.
The devices are a block of a 4x16x16 slice.
Arguments:
- volume: bfloat16 [128, 256, 1024], P(('grp', 'slab')), parts along dimension 0, may hold values from -6 to 6
- ray_weights: bfloat16 [8, 1024, 1024], P('ang'), may hold values from -0.0234375 to 0.0234375
- row_offsets: int32 [8, 64], P('ang'), may hold values from 0 to 8
- measured: float32 [16, 256, 1024], P(('grp', 'ang'), 'slab'), parts along dimension 0, may hold values from -6 to 6
- shifts: float32 [16], P(('grp', 'ang')), parts along dimension 0, may hold values from -4 to 4
Outputs:
- updated_volume: bfloat16 [128, 256, 1024], P(('grp', 'slab')), parts along dimension 0
- last_residual: float32 [16, 256, 1024], P(('grp', 'ang'), 'slab'), parts along dimension 0
- shift_slope: float32 [16], P(('grp', 'ang')), parts along dimension 0
There are 2 independent parts, one for each index of `grp`. A program takes and returns all parts, laid end to end along the dimension named above; an argument that names none is the same for every part. Nothing has to cross between parts.
All inputs are finite; a program needn't handle non-finite values.
Results may differ from a plain program's by a relative error of at most 0.006.
Values may be sent and summed in bfloat16 or wider, within the bound.
No kernel may reach another device: no remote copies, remote signals or barrier semaphores. Data moves between devices by JAX's collectives and lax.ppermute only.
A program may use at most 128 MiB of HBM per device.

v0:
```python
import math

import jax
import jax.numpy as jnp
from jax import lax
from jax.sharding import Mesh
from jax.sharding import PartitionSpec as P

Y = 256
X = 1024
U = 1024
OFF = 8
ROUNDS = 2
SLAB = ("slab_0", "slab_1")
GRP_SLAB = ("grp", "slab_0", "slab_1")


step_size = 0.5


def own_block(tiles, axes, order):
    lengths = [lax.axis_size(a) for a in axes]
    tiles = tiles.reshape(*lengths, *tiles.shape[1:])
    tiles = tiles.transpose(*order, *range(len(axes), tiles.ndim))
    tiles = tiles.reshape(-1, *tiles.shape[len(axes) :])
    for k in order:
        tiles = lax.psum_scatter(tiles, axes[k], scatter_dimension=0, tiled=True)
    return tiles[0]


def in_blocks(shard, dim, length):
    lengths = shard.shape
    tiles = shard.reshape(*lengths[:dim], length, lengths[dim] // length, *lengths[dim + 1 :])
    return jnp.moveaxis(tiles, dim, 0)


def summed_rows(shard, axes, order, dim):
    length = lax.axis_size(axes)
    return own_block(in_blocks(shard, dim, length), axes, order)


def in_order(tiles, dim):
    lengths = list(tiles.shape[1:])
    lengths[dim] *= tiles.shape[0]
    return jnp.moveaxis(tiles, 0, dim).reshape(lengths)


def stacked_from(shard, axes, order):
    tiles = shard
    for k in order:
        tiles = lax.all_gather(tiles, axes[k])
    done = order[::-1]
    back = [done.index(k) for k in range(len(axes))]
    tiles = tiles.transpose(*back, *range(len(axes), tiles.ndim))
    return tiles.reshape(-1, *shard.shape)


def gather_axes(shard, axes, order, dim):
    return in_order(stacked_from(shard, axes, order), dim)


def from_everyone(shard, axis):
    copies = jnp.broadcast_to(shard, (lax.axis_size(axis), *shard.shape))
    return lax.all_to_all(copies, axis, split_axis=0, concat_axis=0, tiled=True)


def over_copies(shard, axis):
    return from_everyone(shard, axis).sum(axis=0)


def move_down(products, tilt_table):
    base = jnp.zeros((products.shape[1] + OFF, U), jnp.float32)
    placed = jax.vmap(
        lambda block, shift_rows: lax.dynamic_update_slice(base, block, (shift_rows, jnp.int32(0)))
    )(products, tilt_table)
    return jnp.sum(placed, axis=0)


def backproject(extended, tilt_table, ray_weights, band_rows):
    slices_count = tilt_table.shape[1]
    running = jnp.zeros((slices_count * band_rows, X), jnp.float32)
    for angle_index in range(ray_weights.shape[0]):
        source = extended[angle_index]
        picked = jax.vmap(
            lambda shift_rows: lax.dynamic_slice(source, (shift_rows, jnp.int32(0)), (band_rows, U))
        )(tilt_table[angle_index])
        running = running + lax.dot_general(
            picked.reshape(slices_count * band_rows, U),
            ray_weights[angle_index],
            (((1,), (1,)), ((), ())),
            preferred_element_type=jnp.float32,
        )
    return running


def apply_update(current, running):
    partial_value = lax.optimization_barrier(running.reshape(current.shape).astype(jnp.bfloat16))
    partial_wide = partial_value.astype(jnp.float32)
    gradient = lax.psum(partial_wide, "ang")
    renewed = (current.astype(jnp.float32) - step_size * gradient).astype(jnp.bfloat16)
    return renewed


def per_device(volume, ray_weights, row_offsets, measured, shifts):
    angles_here = ray_weights.shape[0]
    band_rows = measured.shape[1]
    highest = lax.Precision.HIGHEST
    numbers = lax.iota(jnp.int32, U)
    turns = numbers[:, None] * numbers[None, :] % U
    radians = turns.astype(jnp.float32) * (2.0 * math.pi / U)
    cosine = jnp.cos(radians)
    sine = jnp.sin(radians)
    signed = jnp.where(numbers <= (U - 1) // 2, numbers, numbers - U)
    omega = signed.astype(jnp.float32) * (2.0 * math.pi / U)
    flat_rows = measured.reshape(angles_here * band_rows, U)
    real_part = jnp.dot(flat_rows, cosine, precision=highest).reshape(angles_here, band_rows, U)
    imag_part = -jnp.dot(flat_rows, sine, precision=highest).reshape(angles_here, band_rows, U)
    phase = omega[None, None, :] * shifts[:, None, None]
    turned_real = real_part * jnp.cos(phase) + imag_part * jnp.sin(phase)
    turned_imag = imag_part * jnp.cos(phase) - real_part * jnp.sin(phase)
    first_half = jnp.concatenate([turned_real, omega * turned_imag], axis=0).reshape(-1, U)
    second_half = jnp.concatenate([turned_imag, -omega * turned_real], axis=0).reshape(-1, U)
    inverse = (
        jnp.dot(first_half, cosine, precision=highest)
        - jnp.dot(second_half, sine, precision=highest)
    ) / U
    inverse = inverse.reshape(2, angles_here, band_rows, U)
    shifted = inverse[0]
    slope_field = inverse[1]
    projection = shifted
    residual = shifted
    current = volume
    slices_here = volume.shape[0]
    tilt_table = lax.dynamic_slice_in_dim(
        row_offsets, lax.axis_index(SLAB) * slices_here, slices_here, 1
    )
    for round_index in range(ROUNDS):
        flattened = current.reshape(slices_here * Y, X)
        partials = jnp.stack(
            [
                move_down(
                    jnp.dot(
                        flattened, ray_weights[angle_index], preferred_element_type=jnp.float32
                    ).reshape(slices_here, Y, U),
                    tilt_table[angle_index],
                )[:Y]
                for angle_index in range(angles_here)
            ]
        )
        projection = summed_rows(partials, SLAB, (1, 0), 1)
        residual = projection - shifted
        rounded = residual.astype(jnp.bfloat16)
        gathered = gather_axes(rounded, SLAB, (0, 1), 1)
        extended = jnp.concatenate(
            [gathered, jnp.zeros((angles_here, OFF, U), jnp.bfloat16)], axis=1
        )
        running = backproject(extended, tilt_table, ray_weights, Y)
        current = apply_update(current, running)
    local_dot = jnp.sum(projection * slope_field, axis=(1, 2))
    shift_slope = over_copies(local_dot, SLAB) / math.sqrt(Y * U)
    return (current, residual, shift_slope)


def solution(mesh):
    split = Mesh(
        mesh.devices.reshape(mesh.shape["grp"], 16, 2, mesh.shape["ang"]),
        ("grp", "slab_0", "slab_1", "ang"),
    )
    placed = (
        P(GRP_SLAB, None, None),
        P("ang", None, None),
        P("ang", None),
        P(("grp", "ang"), SLAB, None),
        P(("grp", "ang")),
    )
    return jax.shard_map(
        per_device,
        mesh=split,
        in_specs=placed,
        out_specs=(P(GRP_SLAB, None, None), P(("grp", "ang"), SLAB, None), P(("grp", "ang"))),
        check_vma=False,
    )
```

profile of v0, /device:TPU:40, one launch (start us, length us, event | category | flops | bytes accessed | tf_op | source)
XLA Modules:
  0.0 536.4 jit_solution(7147799609888639398)
XLA Ops:
  7.3 4.7 fusion.16
  12.0 2.6 fusion.8
  15.2 18.0 %while.12 = (s32[]{:T(128)}, f32[2,264,1024]{2,1,0:T(8,128)S(1)}, s32[2,3]{1,0:T(2,128)S(1)}, f32[2,256,1024]{2,1,0:T(8,128)}, s32[]{:T(128)}, /*index=5*/s32[3]{0:T(128)S(1)}, s32[]{:T(128)}) while((s32[]{:T(128)}, f32[2,264,1024]{2,1,0:T(8,128)S(1)}, s32[2,3]{1,0:T(2,128)S(1)}, f32[2,256,1024]{2,1,0:T(8,128)}, s32[]{:T(128)}, ...), condition=%wide.while_cond.4, body=%wide.while_body.4.sunk | while | flops 262163 | bytes 5243051 | solution.py:74
  15.9 2.8 and_reduce_fusion.8
  18.7 3.4 dynamic-slice_select_fusion.8
  22.1 2.1 dynamic-update-slice.32
  24.9 2.8 and_reduce_fusion.8
  27.7 3.4 dynamic-slice_select_fusion.8
  31.1 2.1 dynamic-update-slice.32
  35.0 24.1 %while.13 = (s32[]{:T(128)}, f32[2,264,1024]{2,1,0:T(8,128)}, s32[2,3]{1,0:T(2,128)S(1)}, f32[2,256,1024]{2,1,0:T(8,128)}, s32[]{:T(128)}, /*index=5*/s32[3]{0:T(128)S(1)}, s32[]{:T(128)}) while((s32[]{:T(128)}, f32[2,264,1024]{2,1,0:T(8,128)}, s32[2,3]{1,0:T(2,128)S(1)}, f32[2,256,1024]{2,1,0:T(8,128)}, s32[]{:T(128)}, /*index=5*/s32[3]{0:T(128)S(1)}, ...), condition=%wide.while_cond.5, body=%wide.while_body.5.sunk | while | flops 262163 | bytes 5243051 | solution.py:74
  35.6 2.7 and_reduce_fusion.9
  38.3 3.6 dynamic-slice_select_fusion.9
  42.0 5.1 dynamic-update-slice.33
  47.7 2.7 and_reduce_fusion.9
  50.4 3.6 dynamic-slice_select_fusion.9
  54.0 5.1 dynamic-update-slice.33
  63.3 32.0 %reduce-scatter.5.cloned.1.call-done = f32[16,2,8,1024]{3,2,1,0:T(8,128)} async-done(((f32[32,2,8,1024]{3,2,1,0:T(8,128)}), f32[16,2,8,1024]{3,2,1,0:T(8,128)}) %reduce-scatter.5.cloned.1.call-update) | async-done | bytes 1048592 | tf_op jit(solution)/shard_map/reduce_scatter | solution.py:27
  96.2 17.8 %fusion.50 = f32[2,8,1024]{2,1,0:T(8,128)S(1)} fusion(f32[2,8,1024]{2,1,0:T(8,128)S(1)} %copy-done), kind=kOutput, calls=%fused_computation.67 | convolution fusion | flops 216006656 | bytes 131072 | tf_op jit(solution)/shard_map/dot_general | solution.py:116
  114.1 18.0 %broadcast_multiply_fusion = (f32[2,8,1024]{2,1,0:T(8,128)S(1)}, f32[2,8,1024]{2,1,0:T(8,128)S(1)}, f32[2,8,1024]{2,1,0:T(8,128)S(1)}, f32[2,8,1024]{2,1,0:T(8,128)S(1)}) fusion(f32[1024]{0:T(1024)S(1)} %get-tuple-element.358, f32[2,1024]{1,0:T(2,128)S(1)} %get-tuple-element.348, f32[2,8,1024]{2,1,0:T(8,128)S(1)} %fusion.50, ...), kind=kOutput, calls=%fused_computation.102 | convolution fusion | flops 216154112 | bytes 417792 | tf_op jit(solution)/shard_map/dot_general | solution.py:117
  132.1 18.1 %fusion.24 = f32[32,1024]{1,0:T(8,128)S(1)} fusion(f32[2,8,1024]{2,1,0:T(8,128)S(1)} %get-tuple-element.345, f32[2,8,1024]{2,1,0:T(8,128)S(1)} %get-tuple-element.324), kind=kOutput, calls=%fused_computation.53 | convolution fusion | flops 417366016 | bytes 262144 | tf_op jit(solution)/shard_map/dot_general | solution.py:124
  150.2 18.0 %fusion.47 = f32[32,1024]{1,0:T(8,128)S(1)} fusion(f32[32,1024]{1,0:T(8,128)S(1)} %fusion.24, f32[2,8,1024]{2,1,0:T(8,128)S(1)} %get-tuple-element.323, f32[2,8,1024]{2,1,0:T(8,128)S(1)} %get-tuple-element.346), kind=kOutput, calls=%fused_computation.66 | convolution fusion | flops 417431552 | bytes 393216 | tf_op jit(solution)/shard_map/dot_general | solution.py:125
  169.7 34.7 %all_gather.20 = bf16[16,2,8,1024]{3,2,1,0:T(8,128)(2,1)} all-gather(bf16[1,2,8,1024]{3,2,1,0:T(8,128)(2,1)S(1)} %fusion.69), channel_id=1, replica_groups=mesh['grp'=2,'slab_0'=16,'slab_1'=2,'ang'=4] {'slab_0'}, dimensions={0}, use_global_device_ids=true | all-gather | bytes 557056 | tf_op jit(solution)/shard_map/all_gather | solution.py:51
  204.7 15.5 %all-gather.5.cloned.1.call-done = bf16[32,2,8,1024]{3,2,1,0:T(8,128)(2,1)} async-done(((bf16[16,2,8,1024]{3,2,1,0:T(8,128)(2,1)}), bf16[32,2,8,1024]{3,2,1,0:T(8,128)(2,1)}) %all-gather.5.cloned.1.call-update) | async-done | bytes 1048592 | tf_op jit(solution)/shard_map/all_gather | solution.py:51
  222.5 4.2 fusion.10
  227.3 3.5 add_convert_fusion.1
  230.8 43.7 %all-reduce.6 = f32[2,256,1024]{2,1,0:T(8,128)S(1)} all-reduce(bf16[2,256,1024]{2,1,0:T(8,128)(2,1)S(1)} %bitcast.233), channel_id=1, replica_groups=mesh['grp'=2,'slab_0'=16,'slab_1'=2,'ang'=4] {'ang'}, use_global_device_ids=true, to_apply=%region_6.7 | all-reduce | flops 524288 | bytes 3145728 | tf_op jit(solution)/shard_map/psum | solution.py:99
  277.0 2.6 fusion.14
  279.6 2.6 fusion.6
  282.4 17.7 %while.14 = (s32[]{:T(128)}, f32[2,264,1024]{2,1,0:T(8,128)S(1)}, s32[2,3]{1,0:T(2,128)S(1)}, f32[2,256,1024]{2,1,0:T(8,128)}, s32[]{:T(128)}, /*index=5*/s32[3]{0:T(128)S(1)}, s32[]{:T(128)}) while((s32[]{:T(128)}, f32[2,264,1024]{2,1,0:T(8,128)S(1)}, s32[2,3]{1,0:T(2,128)S(1)}, f32[2,256,1024]{2,1,0:T(8,128)}, s32[]{:T(128)}, ...), condition=%wide.while_cond.6, body=%wide.while_body.6.sunk | while | flops 262163 | bytes 5243051 | solution.py:74
  283.1 2.7 and_reduce_fusion.10
  285.8 3.3 dynamic-slice_select_fusion.10
  292.0 2.7 and_reduce_fusion.10
  294.7 3.3 dynamic-slice_select_fusion.10
  301.7 18.1 %while.15 = (s32[]{:T(128)}, f32[2,264,1024]{2,1,0:T(8,128)S(1)}, s32[2,3]{1,0:T(2,128)S(1)}, f32[2,256,1024]{2,1,0:T(8,128)}, s32[]{:T(128)}, /*index=5*/s32[3]{0:T(128)S(1)}, s32[]{:T(128)}) while((s32[]{:T(128)}, f32[2,264,1024]{2,1,0:T(8,128)S(1)}, s32[2,3]{1,0:T(2,128)S(1)}, f32[2,256,1024]{2,1,0:T(8,128)}, s32[]{:T(128)}, ...), condition=%wide.while_cond.7, body=%wide.while_body.7.sunk | while | flops 262163 | bytes 5243051 | solution.py:74
  302.4 2.8 and_reduce_fusion.11
  305.2 3.4 dynamic-slice_select_fusion.11
  308.6 2.1 dynamic-update-slice.35
  311.4 2.8 and_reduce_fusion.11
  314.2 3.4 dynamic-slice_select_fusion.11
  317.6 2.1 dynamic-update-slice.35
  323.1 18.6 %reduce-scatter.9.cloned.1.call-done = f32[16,2,8,1024]{3,2,1,0:T(8,128)} async-done(((f32[32,2,8,1024]{3,2,1,0:T(8,128)}), f32[16,2,8,1024]{3,2,1,0:T(8,128)}) %reduce-scatter.9.cloned.1.call-update) | async-done | bytes 1048592 | tf_op jit(solution)/shard_map/reduce_scatter | solution.py:27
  341.9 73.1 %reduce-scatter.11.cloned.1.call-done = f32[1,2,8,1024]{3,2,1,0:T(8,128)} async-done(((f32[16,2,8,1024]{3,2,1,0:T(8,128)}), f32[1,2,8,1024]{3,2,1,0:T(8,128)}) %reduce-scatter.11.cloned.1.call-update) | async-done | bytes 65552 | tf_op jit(solution)/shard_map/reduce_scatter | solution.py:27
  415.8 32.9 %all_gather.23 = bf16[16,2,8,1024]{3,2,1,0:T(8,128)(2,1)} all-gather(bf16[1,2,8,1024]{3,2,1,0:T(8,128)(2,1)S(1)} %fusion.70), channel_id=1, replica_groups=mesh['grp'=2,'slab_0'=16,'slab_1'=2,'ang'=4] {'slab_0'}, dimensions={0}, use_global_device_ids=true | all-gather | bytes 557056 | tf_op jit(solution)/shard_map/all_gather | solution.py:51
  450.9 10.6 %all-to-all-start = ((f32[32,1,2]{2,1,0:T(1,128)}), f32[32,1,2]{2,1,0:T(1,128)S(1)}, u32[]{:S(2)}, u32[]{:S(2)}) async-start(f32[32,1,2]{2,1,0:T(1,128)} %broadcast_in_dim.7), calls=%async_computation.4 | async-start | bytes 32768 | tf_op jit(solution)/shard_map/all_to_all | solution.py:64
  461.5 12.1 %all-to-all-done = f32[32,1,2]{2,1,0:T(1,128)S(1)} async-done(((f32[32,1,2]{2,1,0:T(1,128)}), f32[32,1,2]{2,1,0:T(1,128)S(1)}, u32[]{:S(2)}, u32[]{:S(2)}) %all-to-all-start) | async-done | bytes 288 | tf_op jit(solution)/shard_map/all_to_all | solution.py:64
  476.3 4.2 fusion.12
  481.1 4.5 add_convert_fusion
  485.6 42.3 %all-reduce.7 = f32[2,256,1024]{2,1,0:T(8,128)S(1)} all-reduce(bf16[2,256,1024]{2,1,0:T(8,128)(2,1)} %bitcast.234), channel_id=1, replica_groups=mesh['grp'=2,'slab_0'=16,'slab_1'=2,'ang'=4] {'ang'}, use_global_device_ids=true, to_apply=%region_13.14 | all-reduce | flops 524288 | bytes 3145728 | tf_op jit(solution)/shard_map/psum | solution.py:99
  (122 shorter events, 38.3 us)
Async XLA Ops:
  7.2 89.0 %copy-start = (f32[2,8,1024]{2,1,0:T(8,128)S(1)}, f32[2,8,1024]{2,1,0:T(8,128)}, u32[]{:S(2)}) copy-start(f32[2,8,1024]{2,1,0:T(8,128)} %param.8) | copy-start | bytes 196612
  7.2 88.2 %reduce-scatter.5.cloned.1.call-start = ((), (), s32[]{:S(2)}) async-start(), calls=%async_computation.5 | async-start | bytes 3145728 | tf_op jit(solution)/shard_map/reduce_scatter | solution.py:27
  7.3 4.7 copy-start.5
  7.3 4.7 copy-start.10
  12.0 2.6 copy-start.7
  12.0 2.7 copy-start.8
  14.6 0.7 copy-start.6
  63.2 32.8 %copy-start.9 = (f32[2]{0:T(128)S(1)}, f32[2]{0:T(128)}, u32[]{:S(2)}) copy-start(f32[2]{0:T(128)} %param.9) | copy-start | bytes 28
  63.3 105.6 %reduce-scatter.7.cloned.1.call-start = ((), (), s32[]{:S(2)}) async-start(), calls=%async_computation.6 | async-start | bytes 1114112 | tf_op jit(solution)/shard_map/reduce_scatter | solution.py:27
  95.4 124.8 %all-gather.5.cloned.1.call-start = ((), (), s32[]{:S(2)}) async-start(), calls=%async_computation.9 | async-start | bytes 1572864 | tf_op jit(solution)/shard_map/all_gather | solution.py:51
  204.5 137.3 %reduce-scatter.9.cloned.1.call-start = ((), (), s32[]{:S(2)}) async-start(), calls=%async_computation.7 | async-start | bytes 3145728 | tf_op jit(solution)/shard_map/reduce_scatter | solution.py:27
  274.5 2.5 copy-start.11
  277.0 2.6 copy-start.3
  320.0 1.2 copy-start.2
  323.1 91.9 %reduce-scatter.11.cloned.1.call-start = ((), (), s32[]{:S(2)}) async-start(), calls=%async_computation.8 | async-start | bytes 1114112 | tf_op jit(solution)/shard_map/reduce_scatter | solution.py:27
  341.8 132.5 %all-gather.7.cloned.1.call-start = ((), (), s32[]{:S(2)}) async-start(), calls=%async_computation.10 | async-start | bytes 1572864 | tf_op jit(solution)/shard_map/all_gather | solution.py:51
  450.9 22.8 %all-to-all-start = ((f32[32,1,2]{2,1,0:T(1,128)}), f32[32,1,2]{2,1,0:T(1,128)S(1)}, u32[]{:S(2)}, u32[]{:S(2)}) async-start(f32[32,1,2]{2,1,0:T(1,128)} %broadcast_in_dim.7), calls=%async_computation.4 | async-start | bytes 32768 | tf_op jit(solution)/shard_map/all_to_all | solution.py:64
  485.6 42.3 %copy-start.4 = (bf16[2,256,1024]{2,1,0:T(8,128)(2,1)S(1)}, bf16[2,256,1024]{2,1,0:T(8,128)(2,1)}, u32[]{:S(2)}) copy-start(bf16[2,256,1024]{2,1,0:T(8,128)(2,1)} %copy-done.3) | copy-start | bytes 3145732
  485.6 43.6 %copy-start.1 = (f32[2,8,1024]{2,1,0:T(8,128)S(1)}, f32[2,8,1024]{2,1,0:T(8,128)}, u32[]{:S(2)}) copy-start(f32[2,8,1024]{2,1,0:T(8,128)} %param.8) | copy-start | bytes 196612
Sparse Core Ops, SparseCore 0:
  63.4 31.9 reduce-scatter.4
  97.9 70.8 reduce-scatter.6
  204.6 15.5 all-gather.4
  323.2 18.4 reduce-scatter.8
  344.1 70.7 reduce-scatter.10
  448.9 16.3 all-gather.6
where the time goes:
time: 542 us; the launch traced here: 536 us
  blocking collectives  154 us (28%)
  waiting for transfers between devices  152 us (28%)
  matrix products  101 us (19%)
  other arithmetic  59.6 us (11%)
  local copies, waits for them, and re-layouts  43.1 us (8%)
  between operations  14.8 us (3%)
  starting transfers between devices  11.5 us (2%)
    reduce_scatter x4, waiting for transfers between devices, own_block(): tiles = lax.psum_scatter(tiles, axes[k], scatter_dimension=0, tiled=True)  124 us
    psum x2, blocking collectives, apply_update(): gradient = lax.psum(partial_wide, 'ang')  86 us
    all_gather x2, blocking collectives, stacked_from(): tiles = lax.all_gather(tiles, axes[k])  67.7 us
    scatter x16, other arithmetic  49.3 us
    scatter x24, local copies, waits for them, and re-layouts  28.3 us
    dot_general x1, matrix products, per_device(): jnp.dot(first_half, cosine, precision=highest)  18.1 us
    dot_general x1, matrix products, per_device(): jnp.dot(flat_rows, sine, precision=highest)  18 us
    dot_general x1, matrix products, per_device(): jnp.dot(second_half, sine, precision=highest)  18 us
  transfers between devices with their start and end apart: 7, of which 6 were waited for; matrix products, arithmetic and copies ran while one was open for 14% of the time, Pallas kernels for 0%

commit v1 on v0

v1 whole, which is shorter than its diff:
```python
import math

import jax
import jax.numpy as jnp
from jax import lax
from jax.sharding import PartitionSpec as P

OFF = 8
ROUNDS = 2
STEP_SIZE = 0.5


def moments(length):
    waves = [2.0 * math.pi * k / length for k in range(-(length // 2), length // 2)]
    return [sum(w**p for w in waves) / length for p in (2, 4, 6, 8)]


def interpolation_kernels(shifts, taps, length):
    whole = jnp.round(shifts)
    part = shifts - whole
    odd_shift = 1.0 - 2.0 * (whole.astype(jnp.int32) & 1).astype(jnp.float32)
    sine = odd_shift * jnp.sin(math.pi * part)
    cosine = odd_shift * jnp.cos(math.pi * part)
    v = lax.broadcasted_iota(jnp.int32, (1, taps, length), 1)
    u = lax.broadcasted_iota(jnp.int32, (1, taps, length), 2)
    lag = u - v
    lag = jnp.where(lag >= length // 2, lag - length, jnp.where(lag < -(length // 2), lag + length, lag))
    sign = 1.0 - 2.0 * (lag & 1).astype(jnp.float32)
    d = (lag - whole.astype(jnp.int32)[:, None, None]).astype(jnp.float32) - part[:, None, None]
    near = jnp.abs(d) < 0.1
    safe = jnp.where(near, 1.0, d)
    y = safe * (math.pi / length)
    sin_y = jnp.sin(y)
    cos_y = jnp.cos(y)
    inv = 1.0 / sin_y
    cot = cos_y * inv
    sin_d = -sign * sine[:, None, None]
    cos_d = sign * cosine[:, None, None]
    far_h = sin_d * cot * (1.0 / length)
    far_q = (math.pi / length) * (sin_d * inv * inv * (1.0 / length) - cos_d * cot)
    m2, m4, m6, m8 = moments(length)
    s = d * d
    near_h = 1.0 - s * (m2 / 2 - s * (m4 / 24 - s * (m6 / 720 - s * (m8 / 40320))))
    near_q = d * (m2 - s * (m4 / 6 - s * (m6 / 120 - s * (m8 / 5040))))
    return jnp.where(near, near_h, far_h), jnp.where(near, near_q, far_q)


def registered(measured, shifts):
    angles, rows, length = measured.shape
    taps = 128
    blocks = length // taps
    h, q = interpolation_kernels(shifts, taps, length)
    kernels = jnp.concatenate([h, q], axis=2)
    pieces = measured.reshape(angles, rows, blocks, taps).transpose(0, 2, 1, 3)
    pieces = pieces.reshape(angles, blocks * rows, taps)
    spread = jnp.einsum("avr,aru->avu", pieces, kernels, precision=lax.Precision.HIGHEST)
    spread = spread.reshape(angles, blocks, rows, 2, length)
    total = spread[:, 0]
    for k in range(1, blocks):
        total = total + jnp.roll(spread[:, k], taps * k, axis=-1)
    return total[:, :, 0], total[:, :, 1]


def make_per_device(slab):
    def per_device(volume, ray_weights, row_offsets, measured, shifts):
        slices_here, rows_all, cells = volume.shape
        angles_here, band, columns = measured.shape
        slabs = lax.axis_size(slab)
        angs = lax.axis_size("ang")
        chunk = cells // angs
        slices = slices_here * slabs
        angles = angles_here * angs
        f32 = jnp.float32
        bf16 = jnp.bfloat16

        mine = lax.dynamic_slice_in_dim(volume, lax.axis_index("ang") * chunk, chunk, 2)
        mine = mine.reshape(slices_here, slabs, band, chunk).transpose(1, 0, 2, 3)
        own = lax.all_to_all(mine, slab, 0, 0, tiled=True).reshape(slices, band, chunk)
        down_ring = [(i, i + 1) for i in range(slabs - 1)]
        up_ring = [(i + 1, i) for i in range(slabs - 1)]
        above = lax.ppermute(own, slab, down_ring)
        current = jnp.concatenate([above, own], axis=1)

        copies = jnp.broadcast_to(row_offsets, (angs, *row_offsets.shape))
        table = lax.all_to_all(copies, "ang", 0, 0, tiled=True).reshape(angles, slices)

        shifted, slope_field = registered(measured, shifts)

        shape = (angles, band, slices, 2 * band)
        y = lax.broadcasted_iota(jnp.int32, shape, 1)
        r = lax.broadcasted_iota(jnp.int32, shape, 3)
        held = (r >= band) | (lax.axis_index(slab) > 0)
        gather = (r - band == y - table[:, None, :, None]) & held
        gather = gather.astype(bf16).reshape(angles * band, slices * 2 * band)
        shape = (slices, 2 * band, angles, 3 * band)
        r = lax.broadcasted_iota(jnp.int32, shape, 1)
        t = lax.broadcasted_iota(jnp.int32, shape, 3)
        scatter = (t == r + table.T[:, None, :, None]).astype(bf16)

        for round_index in range(ROUNDS):
            last = round_index == ROUNDS - 1
            stacked = jnp.dot(
                gather, current.reshape(slices * 2 * band, chunk), preferred_element_type=f32
            )
            high = lax.reduce_precision(stacked, 8, 7)
            parts = jnp.stack([high.astype(bf16), (stacked - high).astype(bf16)])
            parts = parts.reshape(2, angs, angles_here, band, chunk).transpose(1, 2, 0, 3, 4)
            parts = lax.all_to_all(parts, "ang", 0, 0, tiled=True)
            parts = parts.transpose(1, 2, 3, 0, 4).reshape(angles_here, 2 * band, cells)
            product = jnp.einsum("arx,axu->aru", parts, ray_weights, preferred_element_type=f32)
            projection = product[:, :band] + product[:, band:]
            residual = projection - shifted
            rounded = residual.astype(bf16)
            back = jnp.einsum("aru,axu->arx", rounded, ray_weights, preferred_element_type=f32)
            back = back.astype(bf16).reshape(angles_here, band, angs, chunk).transpose(2, 0, 1, 3)
            back = lax.all_to_all(back, "ang", 0, 0, tiled=True).reshape(angles, band, chunk)
            below = lax.ppermute(back, slab, up_ring)
            if last:
                window = jnp.concatenate([back, below], axis=1)
                pick = scatter[:, band:, :, band:].reshape(slices * band, angles * 2 * band)
                before = current[:, band:]
            else:
                window = jnp.concatenate([lax.ppermute(back, slab, down_ring), back, below], axis=1)
                pick = scatter.reshape(slices * 2 * band, angles * 3 * band)
                before = current
            gradient = jnp.dot(pick, window.reshape(-1, chunk), preferred_element_type=f32)
            current = (before.astype(f32) - STEP_SIZE * gradient.reshape(before.shape)).astype(bf16)

        local_dot = jnp.sum(projection * slope_field, axis=(1, 2))
        dots = jnp.broadcast_to(local_dot, (slabs, angles_here))
        dots = lax.all_to_all(dots, slab, 0, 0, tiled=True)
        shift_slope = jnp.sum(dots, axis=0) / math.sqrt(rows_all * columns)

        home = current.reshape(slabs, slices_here, band, chunk)
        home = lax.all_to_all(home, slab, 0, 0, tiled=True).transpose(1, 0, 2, 3)
        home = home.reshape(slices_here, rows_all, chunk)
        spread = jnp.broadcast_to(home, (angs, *home.shape))
        spread = lax.all_to_all(spread, "ang", 0, 0, tiled=True)
        updated = spread.transpose(1, 2, 0, 3).reshape(slices_here, rows_all, cells)
        return updated, residual, shift_slope

    return per_device


def solution(mesh):
    return jax.shard_map(
        make_per_device("slab"),
        mesh=mesh,
        in_specs=(
            P(("grp", "slab"), None, None),
            P("ang", None, None),
            P("ang", None),
            P(("grp", "ang"), "slab", None),
            P(("grp", "ang")),
        ),
        out_specs=(P(("grp", "slab"), None, None), P(("grp", "ang"), "slab", None), P(("grp", "ang"))),
        check_vma=False,
    )
```

time: 542 us -> 188 us (0.35)
  waiting for transfers between devices: 152 us -> 53.1 us
  blocking collectives: 154 us -> 56.5 us
  matrix products: 101 us -> 11.7 us
  other arithmetic: 59.6 us -> 7.78 us
  starting transfers between devices: 11.5 us -> 46.7 us
  local copies, waits for them, and re-layouts: 43.1 us -> 10.3 us
  between operations: 14.8 us -> 1.12 us
    reduce_scatter x4 -> x0, waiting for transfers between devices: 124 us -> none  [own_block(): tiles = lax.psum_scatter(tiles, axes[k], scatter_dimension=0, tiled=True)]
    dot_general x12 -> x9, matrix products: 101 us -> 11.7 us  [the longest x2 5.99 us: per_device(): jnp.einsum('arx,axu->aru', parts, ray_weights, preferred_element_type=f32)]
    psum x2 -> x0, blocking collectives: 86 us -> none  [apply_update(): gradient = lax.psum(partial_wide, 'ang')]
    all_gather x2 -> x0, blocking collectives: 67.7 us -> none  [stacked_from(): tiles = lax.all_gather(tiles, axes[k])]
    all_to_all x0 -> x4, blocking collectives: none -> 56.5 us  [the longest x1 32.8 us: per_device(): home = lax.all_to_all(home, slab, 0, 0, tiled=True).transpose(1, 0, 2, 3)]
    scatter x17 -> x0, other arithmetic: 49.3 us -> none
    all_to_all x1 -> x5, waiting for transfers between devices: 12.1 us -> 48.2 us  [the longest x1 14.5 us: per_device(): spread = lax.all_to_all(spread, 'ang', 0, 0, tiled=True)]
    all_to_all x1 -> x5, starting transfers between devices: 10.6 us -> 41.2 us  [the longest x1 24.7 us: per_device(): lax.all_to_all(mine, slab, 0, 0, tiled=True).reshape(slices, band, chunk)]
  transfers between devices with their start and end apart: 7 -> 9, of which waited for: 6 -> 7; matrix products, arithmetic and copies ran while one was open for 14% -> 7% of each run, Pallas kernels for 0% -> 0%
where the time goes in v1:
time: 188 us; the launch traced here: 187 us
  blocking collectives  56.5 us (30%)
  waiting for transfers between devices  53.1 us (28%)
  starting transfers between devices  46.7 us (25%)
  matrix products  11.7 us (6%)
  local copies, waits for them, and re-layouts  10.3 us (5%)
  other arithmetic  7.78 us (4%)
    all_to_all x1, blocking collectives, per_device(): home = lax.all_to_all(home, slab, 0, 0, tiled=True).transpose(1, 0, 2, 3)  32.8 us
    all_to_all x1, starting transfers between devices, per_device(): lax.all_to_all(mine, slab, 0, 0, tiled=True).reshape(slices, band, chunk)  24.7 us
    all_to_all x2, blocking collectives, per_device(): lax.all_to_all(back, 'ang', 0, 0, tiled=True).reshape(angles, band, chunk)  15.7 us
    all_to_all x1, waiting for transfers between devices, per_device(): spread = lax.all_to_all(spread, 'ang', 0, 0, tiled=True)  14.5 us
    all_to_all x1, waiting for transfers between devices, per_device(): lax.all_to_all(mine, slab, 0, 0, tiled=True).reshape(slices, band, chunk)  13.7 us
    all_to_all x1, waiting for transfers between devices, per_device(): dots = lax.all_to_all(dots, slab, 0, 0, tiled=True)  11.6 us
    all_to_all x1, blocking collectives, per_device(): parts = lax.all_to_all(parts, 'ang', 0, 0, tiled=True)  8.02 us
    dot_general x2, matrix products, per_device(): jnp.einsum('arx,axu->aru', parts, ray_weights, preferred_element_type=f32)  5.99 us
  transfers between devices with their start and end apart: 9, of which 7 were waited for; matrix products, arithmetic and copies ran while one was open for 7% of the time, Pallas kernels for 0%

profile of v1, /device:TPU:40, one launch (start us, length us, event | category | flops | bytes accessed | tf_op | source)
XLA Modules:
  0.0 187.3 jit_solution(5452041515217577448)
XLA Ops:
  0.7 1.2 copy-done
  1.9 0.7 copy.93
  2.6 24.7 %all-to-all-start = ((bf16[32,2,8,256]{3,2,1,0:T(8,128)(2,1)}), bf16[32,2,8,256]{3,2,1,0:T(8,128)(2,1)S(1)}, u32[]{:S(2)}, u32[]{:S(2)}) async-start(bf16[32,2,8,256]{3,2,1,0:T(8,128)(2,1)} %copy.93), calls=%async_computation | async-start | bytes 524288 | tf_op jit(solution)/shard_map/all_to_all | solution.py:78
  27.4 0.2 multiply_subtract_fusion
  27.7 4.9 %fusion.10 = (f32[2,128,1024]{2,1,0:T(8,128)S(1)}, f32[2,128,1024]{2,1,0:T(8,128)S(1)}) fusion(f32[2]{0:T(128)S(1)} %get-tuple-element.31, f32[128,1024]{1,0:T(8,128)S(1)} %get-tuple-element.35, f32[2]{0:T(128)S(1)} %get-tuple-element.33, s32[2]{0:T(128)S(1)} %get-tuple-element.30, s32[128,1024]{1,0:T(8,128)S(1)} %fusion.26, f32[2]{0:T(128)S(1)} %get-tuple-element.32, ...), kind=kLoop, calls=%fused_computation.20 | loop fusion | flops 9699328 | bytes 3670048 | tf_op jit(solution)/shard_map/jit(_where)/select_n | solution.py:45
  32.6 1.3 convolution_bitcast_fusion
  33.9 0.9 reshape.306
  35.0 0.7 reshape.320
  35.7 13.7 %all-to-all-done = bf16[32,2,8,256]{3,2,1,0:T(8,128)(2,1)S(1)} async-done(((bf16[32,2,8,256]{3,2,1,0:T(8,128)(2,1)}), bf16[32,2,8,256]{3,2,1,0:T(8,128)(2,1)S(1)}, u32[]{:S(2)}, u32[]{:S(2)}) %all-to-all-start) | async-done | bytes 262176 | tf_op jit(solution)/shard_map/all_to_all | solution.py:78
  49.4 4.6 %all-to-all-start.1 = ((s32[4,1,128]{2,1,0:T(1,128)}), s32[4,1,128]{2,1,0:T(1,128)S(1)}, u32[]{:S(2)}, u32[]{:S(2)}) async-start(s32[4,1,128]{2,1,0:T(1,128)} %reshape.320), calls=%async_computation.1 | async-start | bytes 4096 | tf_op jit(solution)/shard_map/all_to_all | solution.py:85
  53.9 1.6 collective-permute-start
  56.0 3.1 %all-to-all-done.1 = s32[4,1,128]{2,1,0:T(1,128)S(1)} async-done(((s32[4,1,128]{2,1,0:T(1,128)}), s32[4,1,128]{2,1,0:T(1,128)S(1)}, u32[]{:S(2)}, u32[]{:S(2)}) %all-to-all-start.1) | async-done | bytes 2080 | tf_op jit(solution)/shard_map/all_to_all | solution.py:85
  59.2 0.5 broadcast.395
  59.7 0.7 reduce.1
  60.4 0.5 fusion.3
  60.9 1.1 and.39
  62.1 0.2 reduce-precision_convert_fusion.1
  62.3 0.6 maximum_bitcast_fusion
  62.9 3.6 %all-to-all-start.2 = ((bf16[4,2,2,8,256]{4,3,1,2,0:T(8,128)(2,1)}), bf16[4,2,2,8,256]{4,3,1,2,0:T(8,128)(2,1)S(1)}, u32[]{:S(2)}, u32[]{:S(2)}) async-start(bf16[4,2,2,8,256]{4,3,1,2,0:T(8,128)(2,1)} %maximum_bitcast_fusion), calls=%async_computation.2 | async-start | bytes 131072 | tf_op jit(solution)/shard_map/all_to_all | solution.py:108
  66.6 5.3 %all-to-all-done.2 = bf16[4,2,2,8,256]{4,3,1,2,0:T(8,128)(2,1)S(1)} async-done(((bf16[4,2,2,8,256]{4,3,1,2,0:T(8,128)(2,1)}), bf16[4,2,2,8,256]{4,3,1,2,0:T(8,128)(2,1)S(1)}, u32[]{:S(2)}, u32[]{:S(2)}) %all-to-all-start.2) | async-done | bytes 65568 | tf_op jit(solution)/shard_map/all_to_all | solution.py:108
  71.9 3.0 %fusion.54 = f32[2,16,1024]{2,1,0:T(8,128)S(1)} fusion(bf16[2,16,1024]{2,1,0:T(8,128)(2,1)S(1)} %bitcast.136, bf16[2,1024,1024]{2,1,0:T(8,128)(2,1)} %param.6), kind=kOutput, calls=%fused_computation.108 | convolution fusion | flops 67108864 | bytes 4390912 | tf_op jit(solution)/shard_map/arx,axu->aru/dot_general | solution.py:110
  74.9 0.5 copy-done.1
  75.3 1.2 convolution_convert_fusion.1
  76.5 7.8 %all_to_all.46 = bf16[4,2,8,256]{3,2,1,0:T(8,128)(2,1)S(1)} all-to-all(bf16[4,2,8,256]{3,2,1,0:T(8,128)(2,1)S(1)} %bitcast.162), channel_id=1, replica_groups=mesh['grp'=2,'slab'=32,'ang'=4] {'ang'}, dimensions={0} | all-to-all | bytes 65536 | tf_op jit(solution)/shard_map/all_to_all | solution.py:116
  84.3 1.3 collective-permute-start.1
  85.7 1.3 collective-permute-start.2
  87.2 3.2 %collective-permute-done.2 = bf16[8,8,256]{2,1,0:T(8,128)(2,1)S(1)} collective-permute-done((bf16[8,8,256]{2,1,0:T(8,128)(2,1)S(1)}, bf16[8,8,256]{2,1,0:T(8,128)(2,1)S(1)}, u32[]{:S(2)}, u32[]{:S(2)}) %collective-permute-start.2) | collective-permute-done | bytes 32800 | tf_op jit(solution)/shard_map/ppermute | solution.py:117
  90.4 0.4 subtract_convert_fusion
  90.7 0.2 reduce-precision_convert_fusion
  91.0 8.0 %all_to_all.47 = bf16[4,2,2,8,256]{4,3,1,2,0:T(8,128)(2,1)S(1)} all-to-all(bf16[4,2,2,8,256]{4,3,1,2,0:T(8,128)(2,1)S(1)} %maximum_bitcast_fusion.1), channel_id=1, replica_groups=mesh['grp'=2,'slab'=32,'ang'=4] {'ang'}, dimensions={0} | all-to-all | bytes 131072 | tf_op jit(solution)/shard_map/all_to_all | solution.py:108
  99.0 3.0 %fusion.55 = f32[2,16,1024]{2,1,0:T(8,128)S(1)} fusion(bf16[2,16,1024]{2,1,0:T(8,128)(2,1)S(1)} %bitcast.137, bf16[2,1024,1024]{2,1,0:T(8,128)(2,1)} %param.6), kind=kOutput, calls=%fused_computation.109 | convolution fusion | flops 67108864 | bytes 4390912 | tf_op jit(solution)/shard_map/arx,axu->aru/dot_general | solution.py:110
  102.0 0.1 fusion.40
  102.1 0.3 copy-done.2
  102.4 1.2 convolution_convert_fusion
  103.6 7.8 %all_to_all.48 = bf16[4,2,8,256]{3,2,1,0:T(8,128)(2,1)S(1)} all-to-all(bf16[4,2,8,256]{3,2,1,0:T(8,128)(2,1)S(1)} %bitcast.163), channel_id=1, replica_groups=mesh['grp'=2,'slab'=32,'ang'=4] {'ang'}, dimensions={0} | all-to-all | bytes 65536 | tf_op jit(solution)/shard_map/all_to_all | solution.py:116
  111.5 1.3 collective-permute-start.3
  112.9 1.7 collective-permute-done.3
  114.6 1.3 fusion.8
  115.9 32.8 %all_to_all.49 = bf16[32,2,8,256]{3,2,1,0:T(8,128)(2,1)S(1)} all-to-all(bf16[32,2,8,256]{3,2,1,0:T(8,128)(2,1)S(1)} %bitcast.153), channel_id=1, replica_groups=mesh['grp'=2,'slab'=32,'ang'=4] {'slab'}, dimensions={0} | all-to-all | bytes 524288 | tf_op jit(solution)/shard_map/all_to_all | solution.py:135
  148.7 0.6 broadcast_in_dim.18
  149.3 4.7 %all-to-all-start.8 = ((f32[32,1,2]{2,1,0:T(1,128)}), f32[32,1,2]{2,1,0:T(1,128)S(1)}, u32[]{:S(2)}, u32[]{:S(2)}) async-start(f32[32,1,2]{2,1,0:T(1,128)} %broadcast_in_dim.18), calls=%async_computation.8 | async-start | bytes 32768 | tf_op jit(solution)/shard_map/all_to_all | solution.py:131
  154.1 11.6 %all-to-all-done.8 = f32[32,1,2]{2,1,0:T(1,128)S(1)} async-done(((f32[32,1,2]{2,1,0:T(1,128)}), f32[32,1,2]{2,1,0:T(1,128)S(1)}, u32[]{:S(2)}, u32[]{:S(2)}) %all-to-all-start.8) | async-done | bytes 288 | tf_op jit(solution)/shard_map/all_to_all | solution.py:131
  165.7 1.0 broadcast_in_dim.9
  166.8 3.6 %all-to-all-start.7 = ((bf16[4,2,256,256]{3,2,1,0:T(8,128)(2,1)}), bf16[4,2,256,256]{3,2,1,0:T(8,128)(2,1)S(1)}, u32[]{:S(2)}, u32[]{:S(2)}) async-start(bf16[4,2,256,256]{3,2,1,0:T(8,128)(2,1)} %broadcast_in_dim.9), calls=%async_computation.7 | async-start | bytes 2097152 | tf_op jit(solution)/shard_map/all_to_all | solution.py:138
  170.5 0.5 broadcast_multiply_fusion
  171.0 14.5 %all-to-all-done.7 = bf16[4,2,256,256]{3,2,1,0:T(8,128)(2,1)S(1)} async-done(((bf16[4,2,256,256]{3,2,1,0:T(8,128)(2,1)}), bf16[4,2,256,256]{3,2,1,0:T(8,128)(2,1)S(1)}, u32[]{:S(2)}, u32[]{:S(2)}) %all-to-all-start.7) | async-done | bytes 1048608 | tf_op jit(solution)/shard_map/all_to_all | solution.py:138
  185.5 0.5 copy.113
  186.0 1.3 copy.115
  (56 shorter events, 1.2 us)
Async XLA Ops:
  0.6 1.2 copy-start
  0.6 27.0 %copy-start.6 = (f32[2]{0:T(128)S(1)}, f32[2]{0:T(128)}, u32[]{:S(2)}) copy-start(f32[2]{0:T(128)} %param.9) | copy-start | bytes 28
  2.6 46.7 %all-to-all-start = ((bf16[32,2,8,256]{3,2,1,0:T(8,128)(2,1)}), bf16[32,2,8,256]{3,2,1,0:T(8,128)(2,1)S(1)}, u32[]{:S(2)}, u32[]{:S(2)}) async-start(bf16[32,2,8,256]{3,2,1,0:T(8,128)(2,1)} %copy.93), calls=%async_computation | async-start | bytes 524288 | tf_op jit(solution)/shard_map/all_to_all | solution.py:78
  27.5 5.1 %copy-start.4 = (f32[2,8,1024]{2,1,0:T(8,128)S(1)}, f32[2,8,1024]{2,1,0:T(8,128)}, u32[]{:S(2)}) copy-start(f32[2,8,1024]{2,1,0:T(8,128)} %param.8) | copy-start | bytes 196612
  33.9 1.1 copy-start.5
  49.4 9.8 %all-to-all-start.1 = ((s32[4,1,128]{2,1,0:T(1,128)}), s32[4,1,128]{2,1,0:T(1,128)S(1)}, u32[]{:S(2)}, u32[]{:S(2)}) async-start(s32[4,1,128]{2,1,0:T(1,128)} %reshape.320), calls=%async_computation.1 | async-start | bytes 4096 | tf_op jit(solution)/shard_map/all_to_all | solution.py:85
  53.9 8.1 %collective-permute-start = (bf16[64,8,256]{2,1,0:T(8,128)(2,1)S(1)}, bf16[64,8,256]{2,1,0:T(8,128)(2,1)S(1)}, u32[]{:S(2)}, u32[]{:S(2)}) collective-permute-start(bf16[64,8,256]{2,1,0:T(8,128)(2,1)S(1)} %bitcast.133), channel_id=1, source_target_pairs={{0,4},{4,8},{8,12},{12,16},{16,20},{20,24},{24,28},{28,32},{32,36}... | collective-permute-start | bytes 786440 | tf_op jit(solution)/shard_map/ppermute | solution.py:81
  62.9 8.9 %all-to-all-start.2 = ((bf16[4,2,2,8,256]{4,3,1,2,0:T(8,128)(2,1)}), bf16[4,2,2,8,256]{4,3,1,2,0:T(8,128)(2,1)S(1)}, u32[]{:S(2)}, u32[]{:S(2)}) async-start(bf16[4,2,2,8,256]{4,3,1,2,0:T(8,128)(2,1)} %maximum_bitcast_fusion), calls=%async_computation.2 | async-start | bytes 131072 | tf_op jit(solution)/shard_map/all_to_all | solution.py:108
  71.9 3.4 %copy-start.1 = (bf16[2,1024,1024]{2,1,0:T(8,128)(2,1)S(1)}, bf16[2,1024,1024]{2,1,0:T(8,128)(2,1)}, u32[]{:S(2)}) copy-start(bf16[2,1024,1024]{2,1,0:T(8,128)(2,1)} %param.6) | copy-start | bytes 12582916
  84.3 2.8 %collective-permute-start.1 = (bf16[8,8,256]{2,1,0:T(8,128)(2,1)S(1)}, bf16[8,8,256]{2,1,0:T(8,128)(2,1)S(1)}, u32[]{:S(2)}, u32[]{:S(2)}) collective-permute-start(bf16[8,8,256]{2,1,0:T(8,128)(2,1)S(1)} %bitcast.164), channel_id=1, source_target_pairs={{0,4},{4,8},{8,12},{12,16},{16,20},{20,24},{24,28},{28,32},{32,36}... | collective-permute-start | bytes 98312 | tf_op jit(solution)/shard_map/ppermute | solution.py:123
  85.7 4.7 %collective-permute-start.2 = (bf16[8,8,256]{2,1,0:T(8,128)(2,1)S(1)}, bf16[8,8,256]{2,1,0:T(8,128)(2,1)S(1)}, u32[]{:S(2)}, u32[]{:S(2)}) collective-permute-start(bf16[8,8,256]{2,1,0:T(8,128)(2,1)S(1)} %bitcast.165), channel_id=1, source_target_pairs={{4,0},{8,4},{12,8},{16,12},{20,16},{24,20},{28,24},{32,28},{36,32}... | collective-permute-start | bytes 98312 | tf_op jit(solution)/shard_map/ppermute | solution.py:117
  99.0 3.4 %copy-start.2 = (bf16[2,1024,1024]{2,1,0:T(8,128)(2,1)S(1)}, bf16[2,1024,1024]{2,1,0:T(8,128)(2,1)}, u32[]{:S(2)}) copy-start(bf16[2,1024,1024]{2,1,0:T(8,128)(2,1)} %param.6) | copy-start | bytes 12582916
  102.1 1.5 copy-start.3
  111.5 3.1 %collective-permute-start.3 = (bf16[8,8,256]{2,1,0:T(8,128)(2,1)S(1)}, bf16[8,8,256]{2,1,0:T(8,128)(2,1)S(1)}, u32[]{:S(2)}, u32[]{:S(2)}) collective-permute-start(bf16[8,8,256]{2,1,0:T(8,128)(2,1)S(1)} %bitcast.171), channel_id=1, source_target_pairs={{4,0},{8,4},{12,8},{16,12},{20,16},{24,20},{28,24},{32,28},{36,32}... | collective-permute-start | bytes 98312 | tf_op jit(solution)/shard_map/ppermute | solution.py:117
  149.3 16.4 %all-to-all-start.8 = ((f32[32,1,2]{2,1,0:T(1,128)}), f32[32,1,2]{2,1,0:T(1,128)S(1)}, u32[]{:S(2)}, u32[]{:S(2)}) async-start(f32[32,1,2]{2,1,0:T(1,128)} %broadcast_in_dim.18), calls=%async_computation.8 | async-start | bytes 32768 | tf_op jit(solution)/shard_map/all_to_all | solution.py:131
  166.8 18.7 %all-to-all-start.7 = ((bf16[4,2,256,256]{3,2,1,0:T(8,128)(2,1)}), bf16[4,2,256,256]{3,2,1,0:T(8,128)(2,1)S(1)}, u32[]{:S(2)}, u32[]{:S(2)}) async-start(bf16[4,2,256,256]{3,2,1,0:T(8,128)(2,1)} %broadcast_in_dim.9), calls=%async_computation.7 | async-start | bytes 2097152 | tf_op jit(solution)/shard_map/all_to_all | solution.py:138

commit v2 on v1

v2 whole, which is shorter than its diff:
```python
import math

import jax
import jax.numpy as jnp
from jax import lax
from jax.experimental import pallas as pl
from jax.experimental.pallas import tpu as pltpu
from jax.sharding import Mesh
from jax.sharding import PartitionSpec as P

OFF = 8
ROUNDS = 2
STEP_SIZE = 0.5


def moments(length):
    waves = [2.0 * math.pi * k / length for k in range(-(length // 2), length // 2)]
    return [sum(w**p for w in waves) / length for p in (2, 4, 6, 8)]


def interpolation_kernels(shifts, taps, length):
    whole = jnp.round(shifts)
    part = shifts - whole
    odd_shift = 1.0 - 2.0 * (whole.astype(jnp.int32) & 1).astype(jnp.float32)
    sine = odd_shift * jnp.sin(math.pi * part)
    cosine = odd_shift * jnp.cos(math.pi * part)
    v = lax.broadcasted_iota(jnp.int32, (1, taps, length), 1)
    u = lax.broadcasted_iota(jnp.int32, (1, taps, length), 2)
    lag = u - v
    lag = jnp.where(lag >= length // 2, lag - length, jnp.where(lag < -(length // 2), lag + length, lag))
    sign = 1.0 - 2.0 * (lag & 1).astype(jnp.float32)
    d = (lag - whole.astype(jnp.int32)[:, None, None]).astype(jnp.float32) - part[:, None, None]
    near = jnp.abs(d) < 0.1
    safe = jnp.where(near, 1.0, d)
    y = safe * (math.pi / length)
    sin_y = jnp.sin(y)
    cos_y = jnp.cos(y)
    inv = 1.0 / sin_y
    cot = cos_y * inv
    sin_d = -sign * sine[:, None, None]
    cos_d = sign * cosine[:, None, None]
    far_h = sin_d * cot * (1.0 / length)
    far_q = (math.pi / length) * (sin_d * inv * inv * (1.0 / length) - cos_d * cot)
    m2, m4, m6, m8 = moments(length)
    s = d * d
    near_h = 1.0 - s * (m2 / 2 - s * (m4 / 24 - s * (m6 / 720 - s * (m8 / 40320))))
    near_q = d * (m2 - s * (m4 / 6 - s * (m6 / 120 - s * (m8 / 5040))))
    return jnp.where(near, near_h, far_h), jnp.where(near, near_q, far_q)


def registered(measured, shifts):
    angles, rows, length = measured.shape
    taps = 128
    blocks = length // taps
    h, q = interpolation_kernels(shifts, taps, length)
    kernels = jnp.concatenate([h, q], axis=2)
    pieces = measured.reshape(angles, rows, blocks, taps).transpose(0, 2, 1, 3)
    pieces = pieces.reshape(angles, blocks * rows, taps)
    spread = jnp.einsum("avr,aru->avu", pieces, kernels, precision=lax.Precision.HIGHEST)
    spread = spread.reshape(angles, blocks, rows, 2, length)
    total = spread[:, 0]
    for k in range(1, blocks):
        total = total + jnp.roll(spread[:, k], taps * k, axis=-1)
    return total[:, :, 0], total[:, :, 1]


SLAB = ("z", "core")


def from_ang(blocks, step):
    size = len(blocks)
    return [
        blocks[k] if k == 0 else lax.ppermute(blocks[k], "ang", [(i, (i + k * step) % size) for i in range(size)])
        for k in range(size)
    ]


def swap_cores(pair):
    first = lax.axis_index("core") == 0
    kept = jnp.where(first, pair[0], pair[1])
    sent = jnp.where(first, pair[1], pair[0])
    got = lax.ppermute(sent, "core", [(0, 1), (1, 0)])
    return jnp.where(first, kept, got), jnp.where(first, got, kept)


def place_chunks(chunks):
    count = len(chunks)
    slices, rows, width = chunks[0].shape

    def kernel(*refs):
        sources, out, sems = refs[:count], refs[count], refs[count + 1]
        here = lax.axis_index("ang")
        copies = []
        for k in range(count):
            start = pl.multiple_of(lax.rem(here + k, count) * width, width)
            copies.append(pltpu.make_async_copy(sources[k], out.at[:, :, pl.ds(start, width)], sems.at[k]))
            copies[-1].start()
        for copy in copies:
            copy.wait()

    return pl.pallas_call(
        kernel,
        out_shape=jax.ShapeDtypeStruct((slices, rows, width * count), chunks[0].dtype),
        in_specs=[pl.BlockSpec(memory_space=pl.ANY)] * count,
        out_specs=pl.BlockSpec(memory_space=pl.ANY),
        scratch_shapes=[pltpu.SemaphoreType.DMA((count,))],
    )(*chunks)


def per_device(volume, ray_weights, row_offsets, measured, shifts):
    slices_here, rows_all, cells = volume.shape
    angles_here, band, columns = measured.shape
    chips = lax.axis_size("z")
    slabs = lax.axis_size(SLAB)
    angs = lax.axis_size("ang")
    here = lax.axis_index("ang")
    chunk = cells // angs
    slices = slices_here * slabs
    angles = angles_here * angs
    f32 = jnp.float32
    bf16 = jnp.bfloat16
    down_ring = [(i, i + 1) for i in range(slabs - 1)]
    up_ring = [(i + 1, i) for i in range(slabs - 1)]

    table = jnp.stack(from_ang([row_offsets] * angs, -1)).reshape(angles, slices)

    mine = lax.dynamic_slice_in_dim(volume, here * chunk, chunk, 2)
    mine = mine.reshape(slices_here, chips, 2, band, chunk).transpose(2, 1, 0, 3, 4)
    mine = jnp.stack(swap_cores(mine), axis=1)
    own = lax.all_to_all(mine, "z", 0, 0, tiled=True).reshape(slices, band, chunk)
    above = lax.ppermute(own, SLAB, down_ring)
    current = jnp.concatenate([above, own], axis=1)

    weights = ray_weights.reshape(angles_here, angs, chunk, columns)
    weights = jnp.concatenate(
        [lax.dynamic_slice_in_dim(weights, (here + angs - k) % angs, 1, 1) for k in range(angs)], axis=1
    ).reshape(angles_here, cells, columns)

    shifted, slope_field = registered(measured, shifts)

    shape = (angles, band, slices, 2 * band)
    y = lax.broadcasted_iota(jnp.int32, shape, 1)
    r = lax.broadcasted_iota(jnp.int32, shape, 3)
    held = (r >= band) | (lax.axis_index(SLAB) > 0)
    gather = (r - band == y - table[:, None, :, None]) & held
    gather = gather.astype(bf16).reshape(angles * band, slices * 2 * band)
    shape = (slices, 2 * band, angles, 3 * band)
    r = lax.broadcasted_iota(jnp.int32, shape, 1)
    t = lax.broadcasted_iota(jnp.int32, shape, 3)
    scatter = (t == r + table.T[:, None, :, None]).astype(bf16)

    for round_index in range(ROUNDS):
        last = round_index == ROUNDS - 1
        stacked = jnp.dot(gather, current.reshape(slices * 2 * band, chunk), preferred_element_type=f32)
        high = lax.reduce_precision(stacked, 8, 7)
        high, low = (
            x.astype(bf16).reshape(angs, angles_here, band, chunk) for x in (high, stacked - high)
        )
        parts = from_ang([jnp.concatenate([high[k], low[k]], axis=1) for k in range(angs)], 1)
        parts = jnp.concatenate(parts, axis=2)
        product = jnp.einsum("arx,axu->aru", parts, weights, preferred_element_type=f32)
        projection = product[:, :band] + product[:, band:]
        residual = projection - shifted
        rounded = residual.astype(bf16)
        back = jnp.einsum("aru,axu->arx", rounded, weights, preferred_element_type=f32).astype(bf16)
        back = from_ang([back[:, :, k * chunk : (k + 1) * chunk] for k in range(angs)], -1)
        back = jnp.concatenate(back, axis=0)
        below = lax.ppermute(back, SLAB, up_ring)
        if last:
            window = jnp.concatenate([back, below], axis=1)
            pick = scatter[:, band:, :, band:].reshape(slices * band, angles * 2 * band)
            before = current[:, band:]
        else:
            window = jnp.concatenate([lax.ppermute(back, SLAB, down_ring), back, below], axis=1)
            pick = scatter.reshape(slices * 2 * band, angles * 3 * band)
            before = current
        gradient = jnp.dot(pick, window.reshape(-1, chunk), preferred_element_type=f32)
        current = (before.astype(f32) - STEP_SIZE * gradient.reshape(before.shape)).astype(bf16)

    home = current.reshape(chips, 2, slices_here, band, chunk)
    dots = jnp.sum(projection * slope_field, axis=(1, 2))
    dots, home = lax.optimization_barrier((dots, home))
    home = lax.all_to_all(home, "z", 0, 0, tiled=True)
    bit = 1
    while bit < slabs:
        dots = dots + lax.ppermute(dots, SLAB, [(i, i ^ bit) for i in range(slabs)])
        bit *= 2
    shift_slope = dots / math.sqrt(rows_all * columns)
    home = jnp.stack(swap_cores(home.transpose(1, 2, 0, 3, 4)), axis=2)
    home = home.reshape(slices_here, rows_all, chunk)
    ahead = [(i, (i + 1) % angs) for i in range(angs)]
    behind = [((i + 1) % angs, i) for i in range(angs)]
    half = slices_here // 2
    lower = lax.ppermute(home, "ang", ahead)
    upper = lax.ppermute(home, "ang", behind)
    far = [lax.ppermute(lower[:half], "ang", ahead), lax.ppermute(upper[half:], "ang", behind)]
    updated = place_chunks([home, upper, jnp.concatenate(far), lower])
    return updated, residual, shift_slope


def solution(mesh):
    slabs = mesh.shape["slab"]
    split = Mesh(
        mesh.devices.reshape(mesh.shape["grp"], slabs // 2, 2, mesh.shape["ang"]),
        ("grp", "z", "core", "ang"),
    )
    part = ("grp", "z", "core")
    return jax.shard_map(
        per_device,
        mesh=split,
        in_specs=(P(part, None, None), P("ang", None, None), P("ang", None), P(("grp", "ang"), SLAB, None), P(("grp", "ang"))),
        out_specs=(P(part, None, None), P(("grp", "ang"), SLAB, None), P(("grp", "ang"))),
        check_vma=False,
    )
```

time: 188 us -> 214 us (1.14)
  Pallas kernels: 0 us -> 32.9 us
  blocking collectives: 56.5 us -> 28.2 us
  starting transfers between devices: 46.7 us -> 74.9 us
  waiting for transfers between devices: 53.1 us -> 47.2 us
  local copies, waits for them, and re-layouts: 10.3 us -> 6.29 us
  other arithmetic: 7.78 us -> 10.9 us
    ppermute x4 -> x30, starting transfers between devices: 5.48 us -> 50.8 us  [the longest x15 19.9 us: from_ang(): lax.ppermute(blocks[k], 'ang', [(i, (i + k * step) % size) for i in range...]
    all_to_all x5 -> x1, waiting for transfers between devices: 48.2 us -> 13 us  [per_device(): lax.all_to_all(mine, 'z', 0, 0, tiled=True).reshape(slices, band, chunk)]
    pallas_call x0 -> x1, Pallas kernels: none -> 32.9 us  [place_chunks(): pl.pallas_call(kernel, out_shape=jax.ShapeDtypeStruct((slices, rows, widt...]
    ppermute x4 -> x30, waiting for transfers between devices: 4.91 us -> 34.2 us  [the longest x15 14.4 us: from_ang(): lax.ppermute(blocks[k], 'ang', [(i, (i + k * step) % size) for i in range...]
    all_to_all x4 -> x1, blocking collectives: 56.5 us -> 28.2 us  [per_device(): home = lax.all_to_all(home, 'z', 0, 0, tiled=True)]
    all_to_all x5 -> x1, starting transfers between devices: 41.2 us -> 24 us  [per_device(): lax.all_to_all(mine, 'z', 0, 0, tiled=True).reshape(slices, band, chunk)]
    unnamed x24 -> x25, local copies, waits for them, and re-layouts: 4.4 us -> 0.36 us
    concatenate x1 -> x11, other arithmetic: 0.01 us -> 3.04 us  [the longest x1 2.28 us: per_device(): jnp.concatenate([lax.dynamic_slice_in_dim(weights, (here + angs - k) % an...]
  transfers between devices with their start and end apart: 9 -> 31, of which waited for: 7 -> 22; matrix products, arithmetic and copies ran while one was open for 7% -> 8% of each run, Pallas kernels for 0% -> 0%
where the time goes in v2:
time: 214 us; the launch traced here: 213 us
  starting transfers between devices  74.9 us (35%)
  waiting for transfers between devices  47.2 us (22%)
  Pallas kernels  32.9 us (15%)
  blocking collectives  28.2 us (13%)
  matrix products  11.4 us (5%)
  other arithmetic  10.9 us (5%)
  local copies, waits for them, and re-layouts  6.29 us (3%)
    pallas_call x1, Pallas kernels, place_chunks(): pl.pallas_call(kernel, out_shape=jax.ShapeDtypeStruct((slices, rows, widt...  32.9 us
    all_to_all x1, blocking collectives, per_device(): home = lax.all_to_all(home, 'z', 0, 0, tiled=True)  28.2 us
    all_to_all x1, starting transfers between devices, per_device(): lax.all_to_all(mine, 'z', 0, 0, tiled=True).reshape(slices, band, chunk)  24 us
    ppermute x15, starting transfers between devices, from_ang(): lax.ppermute(blocks[k], 'ang', [(i, (i + k * step) % size) for i in range...  19.9 us
    ppermute x15, waiting for transfers between devices, from_ang(): lax.ppermute(blocks[k], 'ang', [(i, (i + k * step) % size) for i in range...  14.4 us
    ppermute x5, starting transfers between devices, per_device(): dots = dots + lax.ppermute(dots, SLAB, [(i, i ^ bit) for i in range(slabs)])  13.6 us
    all_to_all x1, waiting for transfers between devices, per_device(): lax.all_to_all(mine, 'z', 0, 0, tiled=True).reshape(slices, band, chunk)  13 us
    ppermute x5, waiting for transfers between devices, per_device(): dots = dots + lax.ppermute(dots, SLAB, [(i, i ^ bit) for i in range(slabs)])  11.8 us
  transfers between devices with their start and end apart: 31, of which 22 were waited for; matrix products, arithmetic and copies ran while one was open for 8% of the time, Pallas kernels for 0%

profile of v2, /device:TPU:40, one launch (start us, length us, event | category | flops | bytes accessed | tf_op | source)
XLA Modules:
  0.0 213.3 jit_solution(8253986433712312884)
XLA Ops:
  0.7 1.7 collective-permute-start.2
  2.4 3.0 %collective-permute-start.1 = (s32[2,64]{1,0:T(2,128)}, s32[2,64]{1,0:T(2,128)S(1)}, u32[]{:S(2)}, u32[]{:S(2)}) collective-permute-start(s32[2,64]{1,0:T(2,128)} %param.7), channel_id=1, source_target_pairs={{0,2},{1,3},{2,0},{3,1},{4,6},{5,7},{6,4},{7,5},{8,10},{9,11},{10,... | collective-permute-start | bytes 1544 | tf_op jit(solution)/shard_map/ppermute | solution.py:73
  5.4 1.3 collective-permute-start
  8.3 4.9 %fusion.10 = (f32[2,128,1024]{2,1,0:T(8,128)S(1)}, f32[2,128,1024]{2,1,0:T(8,128)S(1)}) fusion(f32[2]{0:T(128)S(1)} %get-tuple-element.58, f32[128,1024]{1,0:T(8,128)S(1)} %get-tuple-element.62, f32[2]{0:T(128)S(1)} %get-tuple-element.60, s32[2]{0:T(128)S(1)} %get-tuple-element.57, s32[128,1024]{1,0:T(8,128)S(1)} %fusion.26, f32[2]{0:T(128)S(1)} %get-tuple-element.59, ...), kind=kLoop, calls=%fused_computation.21 | loop fusion | flops 9699328 | bytes 3670048 | tf_op jit(solution)/shard_map/jit(_where)/select_n | solution.py:48
  13.3 1.3 convolution_bitcast_fusion
  16.4 24.0 %all-to-all-start = ((bf16[16,2,2,8,256]{4,3,2,1,0:T(8,128)(2,1)}), bf16[16,2,2,8,256]{4,3,2,1,0:T(8,128)(2,1)S(1)}, u32[]{:S(2)}, u32[]{:S(2)}) async-start(bf16[16,2,2,8,256]{4,3,2,1,0:T(8,128)(2,1)} %copy.34), calls=%async_computation | async-start | bytes 524288 | tf_op jit(solution)/shard_map/all_to_all | solution.py:130
  40.9 2.6 %constant_dynamic-slice_fusion.3 = (bf16[2,1,256,1024]{3,2,1,0:T(8,128)(2,1)S(1)}, bf16[2,1,256,1024]{3,2,1,0:T(8,128)(2,1)S(1)}, bf16[2,1,256,1024]{3,2,1,0:T(8,128)(2,1)S(1)}, bf16[2,1,256,1024]{3,2,1,0:T(8,128)(2,1)S(1)}) fusion(bf16[2,4,256,1024]{3,2,1,0:T(8,128)(2,1)} %bitcast.198, s32[]{:T(128)S(6)} %select_n.150, s32[]{:T(128)S(6)} %select_n.156, ...), kind=kLoop, calls=%fused_computation.160 | loop fusion | bytes 8388624 | tf_op jit(solution)/shard_map/dynamic_slice | solution.py:136
  43.6 2.3 %pad_maximum_fusion = bf16[2,4,256,1024]{3,2,1,0:T(8,128)(2,1)} fusion(bf16[2,1,256,1024]{3,2,1,0:T(8,128)(2,1)S(1)} %get-tuple-element.8, bf16[2,1,256,1024]{3,2,1,0:T(8,128)(2,1)S(1)} %get-tuple-element.9, bf16[2,1,256,1024]{3,2,1,0:T(8,128)(2,1)S(1)} %get-tuple-element.10, bf16[2,1,256,1024]{3,2,1,0:T(8,128)(2,1)S(1)} %get-tuple-element.7), kind=kLoop, calls=%fused_computation | loop fusion | flops 6291456 | bytes 8388608 | tf_op jit(solution)/shard_map/concatenate | solution.py:135
  46.0 13.0 %all-to-all-done = bf16[16,2,2,8,256]{4,3,2,1,0:T(8,128)(2,1)S(1)} async-done(((bf16[16,2,2,8,256]{4,3,2,1,0:T(8,128)(2,1)}), bf16[16,2,2,8,256]{4,3,2,1,0:T(8,128)(2,1)S(1)}, u32[]{:S(2)}, u32[]{:S(2)}) %all-to-all-start) | async-done | bytes 262176 | tf_op jit(solution)/shard_map/all_to_all | solution.py:130
  59.0 1.3 collective-permute-start.4
  60.9 1.1 and.57
  62.5 2.8 %collective-permute-start.6 = (bf16[2,16,256]{2,1,0:T(8,128)(2,1)S(1)}, bf16[2,16,256]{2,1,0:T(8,128)(2,1)S(1)}, u32[]{:S(2)}, u32[]{:S(2)}) collective-permute-start(bf16[2,16,256]{2,1,0:T(8,128)(2,1)S(1)} %pad_maximum_fusion.9), channel_id=1, source_target_pairs={{0,2},{1,3},{2,0},{3,1},{4,6},{5,7},{6,4},{7,5},{8,10},{9,11},{10,... | collective-permute-start | bytes 49160 | tf_op jit(solution)/shard_map/ppermute | solution.py:73
  66.2 1.7 collective-permute-done.6
  67.8 2.3 %collective-permute-done.5 = bf16[2,16,256]{2,1,0:T(8,128)(2,1)S(1)} collective-permute-done((bf16[2,16,256]{2,1,0:T(8,128)(2,1)S(1)}, bf16[2,16,256]{2,1,0:T(8,128)(2,1)S(1)}, u32[]{:S(2)}, u32[]{:S(2)}) %collective-permute-start.5) | collective-permute-done | bytes 16416 | tf_op jit(solution)/shard_map/ppermute | solution.py:73
  70.2 2.8 %fusion.47 = f32[2,16,1024]{2,1,0:T(8,128)S(1)} fusion(bf16[2,1024,1024]{2,1,0:T(8,128)(2,1)} %bitcast.194, bf16[2,16,256]{2,1,0:T(8,128)(2,1)S(1)} %collective-permute-done.7, bf16[2,16,256]{2,1,0:T(8,128)(2,1)S(1)} %collective-permute-done.6, bf16[2,16,256]{2,1,0:T(8,128)(2,1)S(1)} %collective-permute-done.5, ...), kind=kOutput, calls=%fused_computation.99 | convolution fusion | flops 67436544 | bytes 4390912 | tf_op jit(solution)/shard_map/arx,axu->aru/dot_general | solution.py:161
  73.0 1.2 convolution_convert_fusion.1
  74.3 2.1 collective-permute-start.9
  76.4 1.1 collective-permute-start.8
  77.5 1.6 collective-permute-done.10
  80.1 1.3 collective-permute-start.12
  81.4 3.6 %collective-permute-start.11 = (bf16[8,8,256]{2,1,0:T(8,128)(2,1)S(1)}, bf16[8,8,256]{2,1,0:T(8,128)(2,1)S(1)}, u32[]{:S(2)}, u32[]{:S(2)}) collective-permute-start(bf16[8,8,256]{2,1,0:T(8,128)(2,1)S(1)} %pad_maximum_fusion.6), channel_id=1, source_target_pairs={{0,4},{4,8},{8,12},{12,16},{16,20},{20,24},{24,28},{28,32},{32,36}... | collective-permute-start | bytes 98312 | tf_op jit(solution)/shard_map/ppermute | solution.py:174
  86.5 2.7 %collective-permute-start.15 = (bf16[2,16,256]{2,1,0:T(8,128)(2,1)S(1)}, bf16[2,16,256]{2,1,0:T(8,128)(2,1)S(1)}, u32[]{:S(2)}, u32[]{:S(2)}) collective-permute-start(bf16[2,16,256]{2,1,0:T(8,128)(2,1)S(1)} %pad_maximum_fusion.13), channel_id=1, source_target_pairs={{0,3},{1,0},{2,1},{3,2},{4,7},{5,4},{6,5},{7,6},{8,11},{9,8},{10,9... | collective-permute-start | bytes 49160 | tf_op jit(solution)/shard_map/ppermute | solution.py:73
  89.2 1.1 collective-permute-start.14
  90.6 3.8 %collective-permute-done.14 = bf16[2,16,256]{2,1,0:T(8,128)(2,1)S(1)} collective-permute-done((bf16[2,16,256]{2,1,0:T(8,128)(2,1)S(1)}, bf16[2,16,256]{2,1,0:T(8,128)(2,1)S(1)}, u32[]{:S(2)}, u32[]{:S(2)}) %collective-permute-start.14) | collective-permute-done | bytes 16416 | tf_op jit(solution)/shard_map/ppermute | solution.py:73
  95.3 2.8 %fusion.57 = f32[2,16,1024]{2,1,0:T(8,128)S(1)} fusion(bf16[2,1024,1024]{2,1,0:T(8,128)(2,1)} %bitcast.195, bf16[2,16,256]{2,1,0:T(8,128)(2,1)S(1)} %collective-permute-done.15, bf16[2,16,256]{2,1,0:T(8,128)(2,1)S(1)} %collective-permute-done.14, bf16[2,16,256]{2,1,0:T(8,128)(2,1)S(1)} %collective-permute-done.13, ...), kind=kOutput, calls=%fused_computation.109 | convolution fusion | flops 67436544 | bytes 4390912 | tf_op jit(solution)/shard_map/arx,axu->aru/dot_general | solution.py:161
  98.2 1.2 convolution_convert_fusion
  99.5 1.3 collective-permute-start.17
  100.8 2.5 %collective-permute-start.16 = (bf16[2,8,256]{2,1,0:T(8,128)(2,1)S(1)}, bf16[2,8,256]{2,1,0:T(8,128)(2,1)S(1)}, u32[]{:S(2)}, u32[]{:S(2)}) collective-permute-start(bf16[2,8,256]{2,1,0:T(8,128)(2,1)S(1)} %get-tuple-element.36), channel_id=1, source_target_pairs={{0,3},{1,0},{2,1},{3,2},{4,7},{5,4},{6,5},{7,6},{8,11},{9,8},{10,9... | collective-permute-start | bytes 24584 | tf_op jit(solution)/shard_map/ppermute | solution.py:73
  103.3 1.0 collective-permute-done.18
  105.2 1.3 collective-permute-start.19
  106.6 4.2 %collective-permute-done.19 = bf16[8,8,256]{2,1,0:T(8,128)(2,1)S(1)} collective-permute-done((bf16[8,8,256]{2,1,0:T(8,128)(2,1)S(1)}, bf16[8,8,256]{2,1,0:T(8,128)(2,1)S(1)}, u32[]{:S(2)}, u32[]{:S(2)}) %collective-permute-start.19) | collective-permute-done | bytes 32800 | tf_op jit(solution)/shard_map/ppermute | solution.py:168
  110.8 1.3 fusion.8
  112.1 28.2 %all_to_all.10 = bf16[16,2,2,8,256]{4,3,2,1,0:T(8,128)(2,1)S(1)} all-to-all(bf16[16,2,2,8,256]{4,3,2,1,0:T(8,128)(2,1)S(1)} %bitcast.225), channel_id=1, replica_groups=mesh['grp'=2,'z'=16,'core'=2,'ang'=4] {'z'}, dimensions={0} | all-to-all | bytes 524288 | tf_op jit(solution)/shard_map/all_to_all | solution.py:183
  140.3 3.6 %collective-permute-start.20 = (bf16[2,16,8,256]{3,2,0,1:T(8,128)(2,1)S(1)}, bf16[2,16,8,256]{3,2,0,1:T(8,128)(2,1)S(1)}, u32[]{:S(2)}, u32[]{:S(2)}) collective-permute-start(bf16[2,16,8,256]{3,2,0,1:T(8,128)(2,1)S(1)} %fusion.32), channel_id=1, source_target_pairs={{0,4},{4,0},{1,5},{5,1},{2,6},{6,2},{3,7},{7,3},{8,12},{12,8},{9,1... | collective-permute-start | bytes 393224 | tf_op jit(solution)/shard_map/ppermute | solution.py:82
  143.9 1.0 collective-permute-done.20
  145.0 2.8 %collective-permute-start.21 = (bf16[2,256,256]{2,1,0:T(8,128)(2,1)S(1)}, bf16[2,256,256]{2,1,0:T(8,128)(2,1)S(1)}, u32[]{:S(2)}, u32[]{:S(2)}) collective-permute-start(bf16[2,256,256]{2,1,0:T(8,128)(2,1)S(1)} %bitcast.207), channel_id=1, source_target_pairs={{1,0},{2,1},{3,2},{0,3},{5,4},{6,5},{7,6},{4,7},{9,8},{10,9},{11,1... | collective-permute-start | bytes 786440 | tf_op jit(solution)/shard_map/ppermute | solution.py:195
  147.9 1.1 collective-permute-done.25
  149.0 1.9 collective-permute-start.26
  150.9 1.7 collective-permute-done.26
  152.6 2.7 %collective-permute-start.27 = (f32[2]{0:T(128)S(1)}, f32[2]{0:T(128)S(1)}, u32[]{:S(2)}, u32[]{:S(2)}) collective-permute-start(f32[2]{0:T(128)S(1)} %add.179), channel_id=1, source_target_pairs={{0,16},{4,20},{8,24},{12,28},{16,0},{20,4},{24,8},{28,12},{32,48},... | collective-permute-start | bytes 32 | tf_op jit(solution)/shard_map/ppermute | solution.py:186
  155.3 1.7 collective-permute-done.27
  157.0 3.6 %collective-permute-start.28 = (f32[2]{0:T(128)S(1)}, f32[2]{0:T(128)S(1)}, u32[]{:S(2)}, u32[]{:S(2)}) collective-permute-start(f32[2]{0:T(128)S(1)} %add.180), channel_id=1, source_target_pairs={{0,32},{4,36},{8,40},{12,44},{16,48},{20,52},{24,56},{28,60},{32,0... | collective-permute-start | bytes 32 | tf_op jit(solution)/shard_map/ppermute | solution.py:186
  160.6 3.9 %collective-permute-done.28 = f32[2]{0:T(128)S(1)} collective-permute-done((f32[2]{0:T(128)S(1)}, f32[2]{0:T(128)S(1)}, u32[]{:S(2)}, u32[]{:S(2)}) %collective-permute-start.28) | collective-permute-done | bytes 40 | tf_op jit(solution)/shard_map/ppermute | solution.py:186
  164.5 5.3 %collective-permute-start.29 = (f32[2]{0:T(128)S(1)}, f32[2]{0:T(128)S(1)}, u32[]{:S(2)}, u32[]{:S(2)}) collective-permute-start(f32[2]{0:T(128)S(1)} %add.181), channel_id=1, source_target_pairs={{0,64},{4,68},{8,72},{12,76},{16,80},{20,84},{24,88},{28,92},{32,9... | collective-permute-start | bytes 32 | tf_op jit(solution)/shard_map/ppermute | solution.py:186
  169.8 3.3 %collective-permute-start.24 = (bf16[1,256,256]{2,1,0:T(8,128)(2,1)S(1)}, bf16[1,256,256]{2,1,0:T(8,128)(2,1)S(1)}, u32[]{:S(2)}, u32[]{:S(2)}) collective-permute-start(bf16[1,256,256]{2,1,0:T(8,128)(2,1)S(1)} %slice.332), channel_id=1, source_target_pairs={{1,0},{2,1},{3,2},{0,3},{5,4},{6,5},{7,6},{4,7},{9,8},{10,9},{11,1... | collective-permute-start | bytes 393224 | tf_op jit(solution)/shard_map/ppermute | solution.py:196
  173.4 3.4 %collective-permute-done.29 = f32[2]{0:T(128)S(1)} collective-permute-done((f32[2]{0:T(128)S(1)}, f32[2]{0:T(128)S(1)}, u32[]{:S(2)}, u32[]{:S(2)}) %collective-permute-start.29) | collective-permute-done | bytes 40 | tf_op jit(solution)/shard_map/ppermute | solution.py:186
  177.3 2.2 %collective-permute-done.23 = bf16[1,256,256]{2,1,0:T(8,128)(2,1)S(1)} collective-permute-done((bf16[1,256,256]{2,1,0:T(8,128)(2,1)S(1)}, bf16[1,256,256]{2,1,0:T(8,128)(2,1)S(1)}, u32[]{:S(2)}, u32[]{:S(2)}) %collective-permute-start.23) | collective-permute-done | bytes 131104 | tf_op jit(solution)/shard_map/ppermute | solution.py:196
  180.2 32.9 %shard_map.76 = bf16[2,256,1024]{2,1,0:T(8,128)(2,1)} custom-call(bf16[2,256,256]{2,1,0:T(8,128)(2,1)} %bitcast.209, bf16[2,256,256]{2,1,0:T(8,128)(2,1)} %copy-done.4, bf16[2,256,256]{2,1,0:T(8,128)(2,1)} %pad_maximum_fusion.4.refs_2_, bf16[2,256,256]{2,1,0:T(8,128)(2,1)} %copy-done.5), custom_call_target="tpu_custom_call" | custom-call | tf_op jit(solution)/shard_map/pallas_call | solution.py:101
  (115 shorter events, 12.0 us)
Async XLA Ops:
  0.6 6.1 %copy-start = (bf16[2,256,1024]{2,1,0:T(8,128)(2,1)S(1)}, bf16[2,256,1024]{2,1,0:T(8,128)(2,1)}, u32[]{:S(2)}) copy-start(bf16[2,256,1024]{2,1,0:T(8,128)(2,1)} %param.5) | copy-start | bytes 3145732
  0.6 12.6 %copy-start.7 = (f32[2,8,1024]{2,1,0:T(8,128)S(1)}, f32[2,8,1024]{2,1,0:T(8,128)}, u32[]{:S(2)}) copy-start(f32[2,8,1024]{2,1,0:T(8,128)} %param.8) | copy-start | bytes 196612
  0.7 59.7 %collective-permute-start.2 = (s32[2,64]{1,0:T(2,128)}, s32[2,64]{1,0:T(2,128)S(1)}, u32[]{:S(2)}, u32[]{:S(2)}) collective-permute-start(s32[2,64]{1,0:T(2,128)} %param.7), channel_id=1, source_target_pairs={{0,1},{1,2},{2,3},{3,0},{4,5},{5,6},{6,7},{7,4},{8,9},{9,10},{10,1... | collective-permute-start | bytes 1544 | tf_op jit(solution)/shard_map/ppermute | solution.py:73
  2.4 58.0 %collective-permute-start.1 = (s32[2,64]{1,0:T(2,128)}, s32[2,64]{1,0:T(2,128)S(1)}, u32[]{:S(2)}, u32[]{:S(2)}) collective-permute-start(s32[2,64]{1,0:T(2,128)} %param.7), channel_id=1, source_target_pairs={{0,2},{1,3},{2,0},{3,1},{4,6},{5,7},{6,4},{7,5},{8,10},{9,11},{10,... | collective-permute-start | bytes 1544 | tf_op jit(solution)/shard_map/ppermute | solution.py:73
  5.4 55.0 %collective-permute-start = (s32[2,64]{1,0:T(2,128)}, s32[2,64]{1,0:T(2,128)S(1)}, u32[]{:S(2)}, u32[]{:S(2)}) collective-permute-start(s32[2,64]{1,0:T(2,128)} %param.7), channel_id=1, source_target_pairs={{0,3},{1,0},{2,1},{3,2},{4,7},{5,4},{6,5},{7,6},{8,11},{9,8},{10,9... | collective-permute-start | bytes 1544 | tf_op jit(solution)/shard_map/ppermute | solution.py:73
  7.4 8.2 %collective-permute-start.3 = (bf16[16,2,8,256]{3,2,0,1:T(8,128)(2,1)}, bf16[16,2,8,256]{3,2,0,1:T(8,128)(2,1)S(1)}, u32[]{:S(2)}, u32[]{:S(2)}) collective-permute-start(bf16[16,2,8,256]{3,2,0,1:T(8,128)(2,1)} %fusion.31), channel_id=1, source_target_pairs={{0,4},{4,0},{1,5},{5,1},{2,6},{6,2},{3,7},{7,3},{8,12},{12,8},{9,1... | collective-permute-start | bytes 393224 | tf_op jit(solution)/shard_map/ppermute | solution.py:82
  16.4 42.6 %all-to-all-start = ((bf16[16,2,2,8,256]{4,3,2,1,0:T(8,128)(2,1)}), bf16[16,2,2,8,256]{4,3,2,1,0:T(8,128)(2,1)S(1)}, u32[]{:S(2)}, u32[]{:S(2)}) async-start(bf16[16,2,2,8,256]{4,3,2,1,0:T(8,128)(2,1)} %copy.34), calls=%async_computation | async-start | bytes 524288 | tf_op jit(solution)/shard_map/all_to_all | solution.py:130
  43.6 16.8 %copy-start.8 = (s32[2,64]{1,0:T(2,128)S(1)}, s32[2,64]{1,0:T(2,128)}, u32[]{:S(2)}) copy-start(s32[2,64]{1,0:T(2,128)} %param.7) | copy-start | bytes 1540
  59.0 3.0 %collective-permute-start.4 = (bf16[64,8,256]{2,1,0:T(8,128)(2,1)S(1)}, bf16[64,8,256]{2,1,0:T(8,128)(2,1)S(1)}, u32[]{:S(2)}, u32[]{:S(2)}) collective-permute-start(bf16[64,8,256]{2,1,0:T(8,128)(2,1)S(1)} %bitcast.204), channel_id=1, source_target_pairs={{0,4},{4,8},{8,12},{12,16},{16,20},{20,24},{24,28},{28,32},{32,36}... | collective-permute-start | bytes 786440 | tf_op jit(solution)/shard_map/ppermute | solution.py:131
  62.0 11.0 %copy-start.1 = (bf16[2,4,256,1024]{3,2,1,0:T(8,128)(2,1)S(1)}, bf16[2,4,256,1024]{3,2,1,0:T(8,128)(2,1)}, u32[]{:S(2)}) copy-start(bf16[2,4,256,1024]{3,2,1,0:T(8,128)(2,1)} %pad_maximum_fusion) | copy-start | bytes 12582916
  62.3 3.9 %collective-permute-start.7 = (bf16[2,16,256]{2,1,0:T(8,128)(2,1)S(1)}, bf16[2,16,256]{2,1,0:T(8,128)(2,1)S(1)}, u32[]{:S(2)}, u32[]{:S(2)}) collective-permute-start(bf16[2,16,256]{2,1,0:T(8,128)(2,1)S(1)} %pad_maximum_fusion.10), channel_id=1, source_target_pairs={{0,3},{1,0},{2,1},{3,2},{4,7},{5,4},{6,5},{7,6},{8,11},{9,8},{10,9... | collective-permute-start | bytes 49160 | tf_op jit(solution)/shard_map/ppermute | solution.py:73
  62.5 5.4 %collective-permute-start.6 = (bf16[2,16,256]{2,1,0:T(8,128)(2,1)S(1)}, bf16[2,16,256]{2,1,0:T(8,128)(2,1)S(1)}, u32[]{:S(2)}, u32[]{:S(2)}) collective-permute-start(bf16[2,16,256]{2,1,0:T(8,128)(2,1)S(1)} %pad_maximum_fusion.9), channel_id=1, source_target_pairs={{0,2},{1,3},{2,0},{3,1},{4,6},{5,7},{6,4},{7,5},{8,10},{9,11},{10,... | collective-permute-start | bytes 49160 | tf_op jit(solution)/shard_map/ppermute | solution.py:73
  65.2 4.9 %collective-permute-start.5 = (bf16[2,16,256]{2,1,0:T(8,128)(2,1)S(1)}, bf16[2,16,256]{2,1,0:T(8,128)(2,1)S(1)}, u32[]{:S(2)}, u32[]{:S(2)}) collective-permute-start(bf16[2,16,256]{2,1,0:T(8,128)(2,1)S(1)} %pad_maximum_fusion.8), channel_id=1, source_target_pairs={{0,1},{1,2},{2,3},{3,0},{4,5},{5,6},{6,7},{7,4},{8,9},{9,10},{10,1... | collective-permute-start | bytes 49160 | tf_op jit(solution)/shard_map/ppermute | solution.py:73
  74.2 4.9 %collective-permute-start.10 = (bf16[2,8,256]{2,1,0:T(8,128)(2,1)S(1)}, bf16[2,8,256]{2,1,0:T(8,128)(2,1)S(1)}, u32[]{:S(2)}, u32[]{:S(2)}) collective-permute-start(bf16[2,8,256]{2,1,0:T(8,128)(2,1)S(1)} %get-tuple-element.46), channel_id=1, source_target_pairs={{0,1},{1,2},{2,3},{3,0},{4,5},{5,6},{6,7},{7,4},{8,9},{9,10},{10,1... | collective-permute-start | bytes 24584 | tf_op jit(solution)/shard_map/ppermute | solution.py:73
  74.3 5.3 %collective-permute-start.9 = (bf16[2,8,256]{2,1,0:T(8,128)(2,1)S(1)}, bf16[2,8,256]{2,1,0:T(8,128)(2,1)S(1)}, u32[]{:S(2)}, u32[]{:S(2)}) collective-permute-start(bf16[2,8,256]{2,1,0:T(8,128)(2,1)S(1)} %get-tuple-element.47), channel_id=1, source_target_pairs={{0,2},{1,3},{2,0},{3,1},{4,6},{5,7},{6,4},{7,5},{8,10},{9,11},{10,... | collective-permute-start | bytes 24584 | tf_op jit(solution)/shard_map/ppermute | solution.py:73
  76.4 3.7 %collective-permute-start.8 = (bf16[2,8,256]{2,1,0:T(8,128)(2,1)S(1)}, bf16[2,8,256]{2,1,0:T(8,128)(2,1)S(1)}, u32[]{:S(2)}, u32[]{:S(2)}) collective-permute-start(bf16[2,8,256]{2,1,0:T(8,128)(2,1)S(1)} %get-tuple-element.48), channel_id=1, source_target_pairs={{0,3},{1,0},{2,1},{3,2},{4,7},{5,4},{6,5},{7,6},{8,11},{9,8},{10,9... | collective-permute-start | bytes 24584 | tf_op jit(solution)/shard_map/ppermute | solution.py:73
  80.1 5.1 %collective-permute-start.12 = (bf16[8,8,256]{2,1,0:T(8,128)(2,1)S(1)}, bf16[8,8,256]{2,1,0:T(8,128)(2,1)S(1)}, u32[]{:S(2)}, u32[]{:S(2)}) collective-permute-start(bf16[8,8,256]{2,1,0:T(8,128)(2,1)S(1)} %pad_maximum_fusion.6), channel_id=1, source_target_pairs={{4,0},{8,4},{12,8},{16,12},{20,16},{24,20},{28,24},{32,28},{36,32}... | collective-permute-start | bytes 98312 | tf_op jit(solution)/shard_map/ppermute | solution.py:168
  81.4 4.5 %collective-permute-start.11 = (bf16[8,8,256]{2,1,0:T(8,128)(2,1)S(1)}, bf16[8,8,256]{2,1,0:T(8,128)(2,1)S(1)}, u32[]{:S(2)}, u32[]{:S(2)}) collective-permute-start(bf16[8,8,256]{2,1,0:T(8,128)(2,1)S(1)} %pad_maximum_fusion.6), channel_id=1, source_target_pairs={{0,4},{4,8},{8,12},{12,16},{16,20},{20,24},{24,28},{28,32},{32,36}... | collective-permute-start | bytes 98312 | tf_op jit(solution)/shard_map/ppermute | solution.py:174
  85.2 13.0 %copy-start.2 = (bf16[2,4,256,1024]{3,2,1,0:T(8,128)(2,1)S(1)}, bf16[2,4,256,1024]{3,2,1,0:T(8,128)(2,1)}, u32[]{:S(2)}) copy-start(bf16[2,4,256,1024]{3,2,1,0:T(8,128)(2,1)} %pad_maximum_fusion) | copy-start | bytes 12582916
  86.5 4.2 %collective-permute-start.15 = (bf16[2,16,256]{2,1,0:T(8,128)(2,1)S(1)}, bf16[2,16,256]{2,1,0:T(8,128)(2,1)S(1)}, u32[]{:S(2)}, u32[]{:S(2)}) collective-permute-start(bf16[2,16,256]{2,1,0:T(8,128)(2,1)S(1)} %pad_maximum_fusion.13), channel_id=1, source_target_pairs={{0,3},{1,0},{2,1},{3,2},{4,7},{5,4},{6,5},{7,6},{8,11},{9,8},{10,9... | collective-permute-start | bytes 49160 | tf_op jit(solution)/shard_map/ppermute | solution.py:73
  89.2 5.2 %collective-permute-start.14 = (bf16[2,16,256]{2,1,0:T(8,128)(2,1)S(1)}, bf16[2,16,256]{2,1,0:T(8,128)(2,1)S(1)}, u32[]{:S(2)}, u32[]{:S(2)}) collective-permute-start(bf16[2,16,256]{2,1,0:T(8,128)(2,1)S(1)} %pad_maximum_fusion.12), channel_id=1, source_target_pairs={{0,2},{1,3},{2,0},{3,1},{4,6},{5,7},{6,4},{7,5},{8,10},{9,11},{10,... | collective-permute-start | bytes 49160 | tf_op jit(solution)/shard_map/ppermute | solution.py:73
  90.3 5.0 %collective-permute-start.13 = (bf16[2,16,256]{2,1,0:T(8,128)(2,1)S(1)}, bf16[2,16,256]{2,1,0:T(8,128)(2,1)S(1)}, u32[]{:S(2)}, u32[]{:S(2)}) collective-permute-start(bf16[2,16,256]{2,1,0:T(8,128)(2,1)S(1)} %pad_maximum_fusion.11), channel_id=1, source_target_pairs={{0,1},{1,2},{2,3},{3,0},{4,5},{5,6},{6,7},{7,4},{8,9},{9,10},{10,1... | collective-permute-start | bytes 49160 | tf_op jit(solution)/shard_map/ppermute | solution.py:73
  98.2 42.1 %copy-start.6 = (f32[2,8,1024]{2,1,0:T(8,128)}, f32[2,8,1024]{2,1,0:T(8,128)S(1)}, u32[]{:S(2)}) copy-start(f32[2,8,1024]{2,1,0:T(8,128)S(1)} %get-tuple-element.25) | copy-start | bytes 196612
  99.4 4.9 %collective-permute-start.18 = (bf16[2,8,256]{2,1,0:T(8,128)(2,1)S(1)}, bf16[2,8,256]{2,1,0:T(8,128)(2,1)S(1)}, u32[]{:S(2)}, u32[]{:S(2)}) collective-permute-start(bf16[2,8,256]{2,1,0:T(8,128)(2,1)S(1)} %get-tuple-element.34), channel_id=1, source_target_pairs={{0,1},{1,2},{2,3},{3,0},{4,5},{5,6},{6,7},{7,4},{8,9},{9,10},{10,1... | collective-permute-start | bytes 24584 | tf_op jit(solution)/shard_map/ppermute | solution.py:73
  99.5 5.3 %collective-permute-start.17 = (bf16[2,8,256]{2,1,0:T(8,128)(2,1)S(1)}, bf16[2,8,256]{2,1,0:T(8,128)(2,1)S(1)}, u32[]{:S(2)}, u32[]{:S(2)}) collective-permute-start(bf16[2,8,256]{2,1,0:T(8,128)(2,1)S(1)} %get-tuple-element.35), channel_id=1, source_target_pairs={{0,2},{1,3},{2,0},{3,1},{4,6},{5,7},{6,4},{7,5},{8,10},{9,11},{10,... | collective-permute-start | bytes 24584 | tf_op jit(solution)/shard_map/ppermute | solution.py:73
  100.8 4.4 %collective-permute-start.16 = (bf16[2,8,256]{2,1,0:T(8,128)(2,1)S(1)}, bf16[2,8,256]{2,1,0:T(8,128)(2,1)S(1)}, u32[]{:S(2)}, u32[]{:S(2)}) collective-permute-start(bf16[2,8,256]{2,1,0:T(8,128)(2,1)S(1)} %get-tuple-element.36), channel_id=1, source_target_pairs={{0,3},{1,0},{2,1},{3,2},{4,7},{5,4},{6,5},{7,6},{8,11},{9,8},{10,9... | collective-permute-start | bytes 24584 | tf_op jit(solution)/shard_map/ppermute | solution.py:73
  105.2 5.6 %collective-permute-start.19 = (bf16[8,8,256]{2,1,0:T(8,128)(2,1)S(1)}, bf16[8,8,256]{2,1,0:T(8,128)(2,1)S(1)}, u32[]{:S(2)}, u32[]{:S(2)}) collective-permute-start(bf16[8,8,256]{2,1,0:T(8,128)(2,1)S(1)} %pad_maximum_fusion.7), channel_id=1, source_target_pairs={{4,0},{8,4},{12,8},{16,12},{20,16},{24,20},{28,24},{32,28},{36,32}... | collective-permute-start | bytes 98312 | tf_op jit(solution)/shard_map/ppermute | solution.py:168
  140.3 4.6 %collective-permute-start.20 = (bf16[2,16,8,256]{3,2,0,1:T(8,128)(2,1)S(1)}, bf16[2,16,8,256]{3,2,0,1:T(8,128)(2,1)S(1)}, u32[]{:S(2)}, u32[]{:S(2)}) collective-permute-start(bf16[2,16,8,256]{3,2,0,1:T(8,128)(2,1)S(1)} %fusion.32), channel_id=1, source_target_pairs={{0,4},{4,0},{1,5},{5,1},{2,6},{6,2},{3,7},{7,3},{8,12},{12,8},{9,1... | collective-permute-start | bytes 393224 | tf_op jit(solution)/shard_map/ppermute | solution.py:82
  145.0 35.2 %copy-start.3 = (bf16[2,16,2,8,256]{4,3,2,1,0:T(8,128)(2,1)}, bf16[2,16,2,8,256]{4,3,2,1,0:T(8,128)(2,1)S(1)}, u32[]{:S(2)}) copy-start(bf16[2,16,2,8,256]{4,3,2,1,0:T(8,128)(2,1)S(1)} %copy.50) | copy-start | bytes 786436
  145.0 24.8 %collective-permute-start.21 = (bf16[2,256,256]{2,1,0:T(8,128)(2,1)S(1)}, bf16[2,256,256]{2,1,0:T(8,128)(2,1)S(1)}, u32[]{:S(2)}, u32[]{:S(2)}) collective-permute-start(bf16[2,256,256]{2,1,0:T(8,128)(2,1)S(1)} %bitcast.207), channel_id=1, source_target_pairs={{1,0},{2,1},{3,2},{0,3},{5,4},{6,5},{7,6},{4,7},{9,8},{10,9},{11,1... | collective-permute-start | bytes 786440 | tf_op jit(solution)/shard_map/ppermute | solution.py:195
  147.8 25.4 %collective-permute-start.22 = (bf16[2,256,256]{2,1,0:T(8,128)(2,1)S(1)}, bf16[2,256,256]{2,1,0:T(8,128)(2,1)S(1)}, u32[]{:S(2)}, u32[]{:S(2)}) collective-permute-start(bf16[2,256,256]{2,1,0:T(8,128)(2,1)S(1)} %bitcast.208), channel_id=1, source_target_pairs={{0,1},{1,2},{2,3},{3,0},{4,5},{5,6},{6,7},{7,4},{8,9},{9,10},{10,1... | collective-permute-start | bytes 786440 | tf_op jit(solution)/shard_map/ppermute | solution.py:194
  147.8 1.2 collective-permute-start.25
  149.0 3.6 %collective-permute-start.26 = (f32[2]{0:T(128)S(1)}, f32[2]{0:T(128)S(1)}, u32[]{:S(2)}, u32[]{:S(2)}) collective-permute-start(f32[2]{0:T(128)S(1)} %add.178), channel_id=1, source_target_pairs={{0,8},{4,12},{8,0},{12,4},{16,24},{20,28},{24,16},{28,20},{32,40},... | collective-permute-start | bytes 32 | tf_op jit(solution)/shard_map/ppermute | solution.py:186
  152.6 4.5 %collective-permute-start.27 = (f32[2]{0:T(128)S(1)}, f32[2]{0:T(128)S(1)}, u32[]{:S(2)}, u32[]{:S(2)}) collective-permute-start(f32[2]{0:T(128)S(1)} %add.179), channel_id=1, source_target_pairs={{0,16},{4,20},{8,24},{12,28},{16,0},{20,4},{24,8},{28,12},{32,48},... | collective-permute-start | bytes 32 | tf_op jit(solution)/shard_map/ppermute | solution.py:186
  157.0 7.5 %collective-permute-start.28 = (f32[2]{0:T(128)S(1)}, f32[2]{0:T(128)S(1)}, u32[]{:S(2)}, u32[]{:S(2)}) collective-permute-start(f32[2]{0:T(128)S(1)} %add.180), channel_id=1, source_target_pairs={{0,32},{4,36},{8,40},{12,44},{16,48},{20,52},{24,56},{28,60},{32,0... | collective-permute-start | bytes 32 | tf_op jit(solution)/shard_map/ppermute | solution.py:186
  164.5 12.3 %collective-permute-start.29 = (f32[2]{0:T(128)S(1)}, f32[2]{0:T(128)S(1)}, u32[]{:S(2)}, u32[]{:S(2)}) collective-permute-start(f32[2]{0:T(128)S(1)} %add.181), channel_id=1, source_target_pairs={{0,64},{4,68},{8,72},{12,76},{16,80},{20,84},{24,88},{28,92},{32,9... | collective-permute-start | bytes 32 | tf_op jit(solution)/shard_map/ppermute | solution.py:186
  169.8 10.4 %copy-start.4 = (bf16[2,256,256]{2,1,0:T(8,128)(2,1)}, bf16[2,256,256]{2,1,0:T(8,128)(2,1)S(1)}, u32[]{:S(2)}) copy-start(bf16[2,256,256]{2,1,0:T(8,128)(2,1)S(1)} %collective-permute-done.21.refs_1_) | copy-start | bytes 786436
  169.8 7.5 %collective-permute-start.24 = (bf16[1,256,256]{2,1,0:T(8,128)(2,1)S(1)}, bf16[1,256,256]{2,1,0:T(8,128)(2,1)S(1)}, u32[]{:S(2)}, u32[]{:S(2)}) collective-permute-start(bf16[1,256,256]{2,1,0:T(8,128)(2,1)S(1)} %slice.332), channel_id=1, source_target_pairs={{1,0},{2,1},{3,2},{0,3},{5,4},{6,5},{7,6},{4,7},{9,8},{10,9},{11,1... | collective-permute-start | bytes 393224 | tf_op jit(solution)/shard_map/ppermute | solution.py:196
  173.2 7.0 %copy-start.5 = (bf16[2,256,256]{2,1,0:T(8,128)(2,1)}, bf16[2,256,256]{2,1,0:T(8,128)(2,1)S(1)}, u32[]{:S(2)}) copy-start(bf16[2,256,256]{2,1,0:T(8,128)(2,1)S(1)} %collective-permute-done.22.refs_3_) | copy-start | bytes 786436
  173.2 6.3 %collective-permute-start.23 = (bf16[1,256,256]{2,1,0:T(8,128)(2,1)S(1)}, bf16[1,256,256]{2,1,0:T(8,128)(2,1)S(1)}, u32[]{:S(2)}, u32[]{:S(2)}) collective-permute-start(bf16[1,256,256]{2,1,0:T(8,128)(2,1)S(1)} %slice.331), channel_id=1, source_target_pairs={{0,1},{1,2},{2,3},{3,0},{4,5},{5,6},{6,7},{7,4},{8,9},{9,10},{10,1... | collective-permute-start | bytes 393224 | tf_op jit(solution)/shard_map/ppermute | solution.py:196

commit v3 on v2

--- a/solution.py
+++ b/solution.py
@@ -3,9 +3,6 @@
 import jax
 import jax.numpy as jnp
 from jax import lax
-from jax.experimental import pallas as pl
-from jax.experimental.pallas import tpu as pltpu
-from jax.sharding import Mesh
 from jax.sharding import PartitionSpec as P
 
 OFF = 8
@@ -64,7 +61,7 @@
     return total[:, :, 0], total[:, :, 1]
 
 
-SLAB = ("z", "core")
+SLAB = "slab"
 
 
 def from_ang(blocks, step):
@@ -75,42 +72,31 @@
     ]
 
 
-def swap_cores(pair):
-    first = lax.axis_index("core") == 0
-    kept = jnp.where(first, pair[0], pair[1])
-    sent = jnp.where(first, pair[1], pair[0])
-    got = lax.ppermute(sent, "core", [(0, 1), (1, 0)])
-    return jnp.where(first, kept, got), jnp.where(first, got, kept)
-
-
-def place_chunks(chunks):
+def split_parts(value, count):
+    parts = []
+    for _ in range(count):
+        high = lax.reduce_precision(value, 8, 7)
+        parts.append(high.astype(jnp.bfloat16))
+        value = value - high
+    return parts
+
+
+def in_order(chunks):
     count = len(chunks)
-    slices, rows, width = chunks[0].shape
-
-    def kernel(*refs):
-        sources, out, sems = refs[:count], refs[count], refs[count + 1]
-        here = lax.axis_index("ang")
-        copies = []
-        for k in range(count):
-            start = pl.multiple_of(lax.rem(here + k, count) * width, width)
-            copies.append(pltpu.make_async_copy(sources[k], out.at[:, :, pl.ds(start, width)], sems.at[k]))
-            copies[-1].start()
-        for copy in copies:
-            copy.wait()
-
-    return pl.pallas_call(
-        kernel,
-        out_shape=jax.ShapeDtypeStruct((slices, rows, width * count), chunks[0].dtype),
-        in_specs=[pl.BlockSpec(memory_space=pl.ANY)] * count,
-        out_specs=pl.BlockSpec(memory_space=pl.ANY),
-        scratch_shapes=[pltpu.SemaphoreType.DMA((count,))],
-    )(*chunks)
+    here = lax.axis_index("ang")
+
+    def pick(column):
+        found = chunks[column]
+        for k in range(1, count):
+            found = jnp.where(here == k, chunks[(column - k) % count], found)
+        return found
+
+    return jnp.concatenate([pick(column) for column in range(count)], axis=2)
 
 
 def per_device(volume, ray_weights, row_offsets, measured, shifts):
     slices_here, rows_all, cells = volume.shape
     angles_here, band, columns = measured.shape
-    chips = lax.axis_size("z")
     slabs = lax.axis_size(SLAB)
     angs = lax.axis_size("ang")
     here = lax.axis_index("ang")
@@ -125,9 +111,8 @@
     table = jnp.stack(from_ang([row_offsets] * angs, -1)).reshape(angles, slices)
 
     mine = lax.dynamic_slice_in_dim(volume, here * chunk, chunk, 2)
-    mine = mine.reshape(slices_here, chips, 2, band, chunk).transpose(2, 1, 0, 3, 4)
-    mine = jnp.stack(swap_cores(mine), axis=1)
-    own = lax.all_to_all(mine, "z", 0, 0, tiled=True).reshape(slices, band, chunk)
+    mine = mine.reshape(slices_here, slabs, band, chunk).transpose(1, 0, 2, 3)
+    own = lax.all_to_all(mine, SLAB, 0, 0, tiled=True).reshape(slices, band, chunk)
     above = lax.ppermute(own, SLAB, down_ring)
     current = jnp.concatenate([above, own], axis=1)
 
@@ -138,12 +123,17 @@
 
     shifted, slope_field = registered(measured, shifts)
 
-    shape = (angles, band, slices, 2 * band)
+    places = slices * 2 * band
+    spread = lax.broadcasted_iota(jnp.int32, (slices, places), 0) == lax.broadcasted_iota(
+        jnp.int32, (slices, places), 1
+    ) // (2 * band)
+    offsets = jnp.dot(table.astype(bf16), spread.astype(bf16), preferred_element_type=f32)
+    shape = (angles, band, places)
     y = lax.broadcasted_iota(jnp.int32, shape, 1)
-    r = lax.broadcasted_iota(jnp.int32, shape, 3)
+    r = lax.broadcasted_iota(jnp.int32, shape, 2) % (2 * band)
     held = (r >= band) | (lax.axis_index(SLAB) > 0)
-    gather = (r - band == y - table[:, None, :, None]) & held
-    gather = gather.astype(bf16).reshape(angles * band, slices * 2 * band)
+    gather = (y - (r - band) == offsets.astype(jnp.int32)[:, None, :]) & held
+    gather = gather.astype(bf16).reshape(angles * band, places)
     shape = (slices, 2 * band, angles, 3 * band)
     r = lax.broadcasted_iota(jnp.int32, shape, 1)
     t = lax.broadcasted_iota(jnp.int32, shape, 3)
@@ -152,9 +142,8 @@
     for round_index in range(ROUNDS):
         last = round_index == ROUNDS - 1
         stacked = jnp.dot(gather, current.reshape(slices * 2 * band, chunk), preferred_element_type=f32)
-        high = lax.reduce_precision(stacked, 8, 7)
         high, low = (
-            x.astype(bf16).reshape(angs, angles_here, band, chunk) for x in (high, stacked - high)
+            x.reshape(angs, angles_here, band, chunk) for x in split_parts(stacked, 2)
         )
         parts = from_ang([jnp.concatenate([high[k], low[k]], axis=1) for k in range(angs)], 1)
         parts = jnp.concatenate(parts, axis=2)
@@ -177,38 +166,38 @@
         gradient = jnp.dot(pick, window.reshape(-1, chunk), preferred_element_type=f32)
         current = (before.astype(f32) - STEP_SIZE * gradient.reshape(before.shape)).astype(bf16)
 
-    home = current.reshape(chips, 2, slices_here, band, chunk)
-    dots = jnp.sum(projection * slope_field, axis=(1, 2))
-    dots, home = lax.optimization_barrier((dots, home))
-    home = lax.all_to_all(home, "z", 0, 0, tiled=True)
-    bit = 1
-    while bit < slabs:
-        dots = dots + lax.ppermute(dots, SLAB, [(i, i ^ bit) for i in range(slabs)])
-        bit *= 2
-    shift_slope = dots / math.sqrt(rows_all * columns)
-    home = jnp.stack(swap_cores(home.transpose(1, 2, 0, 3, 4)), axis=2)
-    home = home.reshape(slices_here, rows_all, chunk)
+    lanes = 128
+    dots = jnp.stack(split_parts(jnp.sum(projection * slope_field, axis=(1, 2)), 3))
+    dots = jnp.pad(dots.reshape(1, -1), ((0, band - 1), (0, lanes - dots.size)))
+    dots = jnp.broadcast_to(dots, (slabs, 1, band, lanes))
+    home = current.reshape(slabs, slices_here, band, chunk // lanes, lanes).transpose(0, 1, 3, 2, 4)
+    home = home.reshape(slabs, -1, band, lanes)
+    home = lax.all_to_all(jnp.concatenate([home, dots], axis=1), SLAB, 0, 0, tiled=True)
+    dots = home[:, -1, 0, : 3 * angles_here].astype(f32).reshape(slabs, 3, angles_here)
+    shift_slope = jnp.sum(dots, axis=(0, 1)) / math.sqrt(rows_all * columns)
+    home = home[:, :-1].reshape(slabs, slices_here, chunk // lanes, band, lanes)
+    home = home.transpose(1, 0, 3, 2, 4).reshape(slices_here, rows_all, chunk)
     ahead = [(i, (i + 1) % angs) for i in range(angs)]
     behind = [((i + 1) % angs, i) for i in range(angs)]
     half = slices_here // 2
     lower = lax.ppermute(home, "ang", ahead)
     upper = lax.ppermute(home, "ang", behind)
     far = [lax.ppermute(lower[:half], "ang", ahead), lax.ppermute(upper[half:], "ang", behind)]
-    updated = place_chunks([home, upper, jnp.concatenate(far), lower])
+    updated = in_order([home, upper, jnp.concatenate(far), lower])
     return updated, residual, shift_slope
 
 
 def solution(mesh):
-    slabs = mesh.shape["slab"]
-    split = Mesh(
-        mesh.devices.reshape(mesh.shape["grp"], slabs // 2, 2, mesh.shape["ang"]),
-        ("grp", "z", "core", "ang"),
-    )
-    part = ("grp", "z", "core")
     return jax.shard_map(
         per_device,
-        mesh=split,
-        in_specs=(P(part, None, None), P("ang", None, None), P("ang", None), P(("grp", "ang"), SLAB, None), P(("grp", "ang"))),
-        out_specs=(P(part, None, None), P(("grp", "ang"), SLAB, None), P(("grp", "ang"))),
+        mesh=mesh,
+        in_specs=(
+            P(("grp", SLAB), None, None),
+            P("ang", None, None),
+            P("ang", None),
+            P(("grp", "ang"), SLAB, None),
+            P(("grp", "ang")),
+        ),
+        out_specs=(P(("grp", SLAB), None, None), P(("grp", "ang"), SLAB, None), P(("grp", "ang"))),
         check_vma=False,
     )

time: 214 us -> 162 us (0.76)
  Pallas kernels: 32.9 us -> 0 us
  starting transfers between devices: 74.9 us -> 59.7 us
  waiting for transfers between devices: 47.2 us -> 35 us
  blocking collectives: 28.2 us -> 38.3 us
    pallas_call x1 -> x0, Pallas kernels: 32.9 us -> none  [place_chunks(): pl.pallas_call(kernel, out_shape=jax.ShapeDtypeStruct((slices, rows, widt...]
    ppermute x7 -> x0, starting transfers between devices: 17.2 us -> none  [the longest x5 13.6 us: per_device(): dots = dots + lax.ppermute(dots, SLAB, [(i, i ^ bit) for i in range(slabs)])]
    ppermute x7 -> x0, waiting for transfers between devices: 12.8 us -> none  [the longest x5 11.8 us: per_device(): dots = dots + lax.ppermute(dots, SLAB, [(i, i ^ bit) for i in range(slabs)])]
    all_to_all x1, blocking collectives: 28.2 us -> 38.3 us  [per_device(): lax.all_to_all(jnp.concatenate([home, dots], axis=1), SLAB, 0, 0, tiled=T...]
    ppermute x1, waiting for transfers between devices: 0.01 us -> 5.84 us  [per_device(): lower = lax.ppermute(home, 'ang', ahead)]
    all_to_all x1, waiting for transfers between devices: 13 us -> 8.05 us  [per_device(): lax.all_to_all(mine, SLAB, 0, 0, tiled=True).reshape(slices, band, chunk)]
    ppermute x1, starting transfers between devices: 0.01 us -> 2.31 us  [per_device(): lower = lax.ppermute(home, 'ang', ahead)]
  transfers between devices with their start and end apart: 31 -> 24, of which waited for: 22 -> 17; matrix products, arithmetic and copies ran while one was open for 8% -> 10% of each run, Pallas kernels for 0% -> 0%
where the time goes in v3:
time: 162 us
  starting transfers between devices  59.7 us (37%)
  blocking collectives  38.3 us (24%)
  waiting for transfers between devices  35 us (22%)
  matrix products  11.6 us (7%)
  other arithmetic  10.3 us (6%)
  local copies, waits for them, and re-layouts  5.36 us (3%)
    all_to_all x1, blocking collectives, per_device(): lax.all_to_all(jnp.concatenate([home, dots], axis=1), SLAB, 0, 0, tiled=T...  38.3 us
    all_to_all x1, starting transfers between devices, per_device(): lax.all_to_all(mine, SLAB, 0, 0, tiled=True).reshape(slices, band, chunk)  24.9 us
    ppermute x15, starting transfers between devices, from_ang(): lax.ppermute(blocks[k], 'ang', [(i, (i + k * step) % size) for i in range...  19.9 us
    ppermute x15, waiting for transfers between devices, from_ang(): lax.ppermute(blocks[k], 'ang', [(i, (i + k * step) % size) for i in range...  14.5 us
    all_to_all x1, waiting for transfers between devices, per_device(): lax.all_to_all(mine, SLAB, 0, 0, tiled=True).reshape(slices, band, chunk)  8.05 us
    ppermute x1, waiting for transfers between devices, per_device(): lower = lax.ppermute(home, 'ang', ahead)  5.84 us
    dot_general x2, matrix products, per_device(): jnp.einsum('arx,axu->aru', parts, weights, preferred_element_type=f32)  5.68 us
    select_n x1, other arithmetic, interpolation_kernels(): return (jnp.where(near, near_h, far_h), jnp.where(near, near_q, far_q))  4.93 us
  transfers between devices with their start and end apart: 24, of which 17 were waited for; matrix products, arithmetic and copies ran while one was open for 10% of the time, Pallas kernels for 0%

profile of v3, /device:TPU:40, one launch (start us, length us, event | category | flops | bytes accessed | tf_op | source)
XLA Modules:
  0.0 161.5 jit_solution(12300252443602447802)
XLA Ops:
  0.7 1.7 %collective-permute-start.3 = (s32[2,64]{1,0:T(2,128)}, s32[2,64]{1,0:T(2,128)S(1)}, u32[]{:S(2)}, u32[]{:S(2)}) collective-permute-start(s32[2,64]{1,0:T(2,128)} %param.7), channel_id=1, source_target_pairs={{0,1},{1,2},{2,3},{3,0},{4,5},{5,6},{6,7},{7,4},{8,9},{9,10},{10,1... | collective-permute-start | bytes 1544 | tf_op jit(solution)/shard_map/ppermute | solution.py:70
  2.4 3.0 %collective-permute-start.2 = (s32[2,64]{1,0:T(2,128)}, s32[2,64]{1,0:T(2,128)S(1)}, u32[]{:S(2)}, u32[]{:S(2)}) collective-permute-start(s32[2,64]{1,0:T(2,128)} %param.7), channel_id=1, source_target_pairs={{0,2},{1,3},{2,0},{3,1},{4,6},{5,7},{6,4},{7,5},{8,10},{9,11},{10,... | collective-permute-start | bytes 1544 | tf_op jit(solution)/shard_map/ppermute | solution.py:70
  5.4 1.3 collective-permute-start.1
  6.7 0.7 copy.34
  7.5 24.9 %all-to-all-start = ((bf16[32,2,8,256]{3,2,1,0:T(8,128)(2,1)}), bf16[32,2,8,256]{3,2,1,0:T(8,128)(2,1)S(1)}, u32[]{:S(2)}, u32[]{:S(2)}) async-start(bf16[32,2,8,256]{3,2,1,0:T(8,128)(2,1)} %copy.34), calls=%async_computation | async-start | bytes 524288 | tf_op jit(solution)/shard_map/all_to_all | solution.py:115
  32.6 0.7 round-nearest-even_convert_fusion
  33.3 4.9 %fusion.9 = (f32[2,128,1024]{2,1,0:T(8,128)S(1)}, f32[2,128,1024]{2,1,0:T(8,128)S(1)}) fusion(f32[2]{0:T(128)S(1)} %get-tuple-element.57, f32[128,1024]{1,0:T(8,128)S(1)} %get-tuple-element.61, f32[2]{0:T(128)S(1)} %get-tuple-element.59, s32[2]{0:T(128)S(1)} %get-tuple-element.56, s32[128,1024]{1,0:T(8,128)S(1)} %fusion.25, f32[2]{0:T(128)S(1)} %get-tuple-element.58, ...), kind=kLoop, calls=%fused_computation.20 | loop fusion | flops 9699328 | bytes 3670048 | tf_op jit(solution)/shard_map/jit(_where)/select_n | solution.py:45
  38.3 1.3 convolution_bitcast_fusion
  39.6 0.9 reshape.378
  41.2 2.6 %constant_dynamic-slice_fusion.3 = (bf16[2,1,256,1024]{3,2,1,0:T(8,128)(2,1)S(1)}, bf16[2,1,256,1024]{3,2,1,0:T(8,128)(2,1)S(1)}, bf16[2,1,256,1024]{3,2,1,0:T(8,128)(2,1)S(1)}, bf16[2,1,256,1024]{3,2,1,0:T(8,128)(2,1)S(1)}) fusion(bf16[2,4,256,1024]{3,2,1,0:T(8,128)(2,1)} %bitcast.162, s32[]{:T(128)S(6)} %select_n.168, s32[]{:T(128)S(6)} %select_n.174, ...), kind=kLoop, calls=%fused_computation.179 | loop fusion | bytes 8388624 | tf_op jit(solution)/shard_map/dynamic_slice | solution.py:121
  43.9 2.3 %pad_maximum_fusion = bf16[2,4,256,1024]{3,2,1,0:T(8,128)(2,1)} fusion(bf16[2,1,256,1024]{3,2,1,0:T(8,128)(2,1)S(1)} %get-tuple-element.4, bf16[2,1,256,1024]{3,2,1,0:T(8,128)(2,1)S(1)} %get-tuple-element.5, bf16[2,1,256,1024]{3,2,1,0:T(8,128)(2,1)S(1)} %get-tuple-element.6, bf16[2,1,256,1024]{3,2,1,0:T(8,128)(2,1)S(1)} %get-tuple-element.3), kind=kLoop, calls=%fused_computation | loop fusion | flops 6291456 | bytes 8388608 | tf_op jit(solution)/shard_map/concatenate | solution.py:120
  46.2 8.1 %all-to-all-done = bf16[32,2,8,256]{3,2,1,0:T(8,128)(2,1)S(1)} async-done(((bf16[32,2,8,256]{3,2,1,0:T(8,128)(2,1)}), bf16[32,2,8,256]{3,2,1,0:T(8,128)(2,1)S(1)}, u32[]{:S(2)}, u32[]{:S(2)}) %all-to-all-start) | async-done | bytes 262176 | tf_op jit(solution)/shard_map/all_to_all | solution.py:115
  54.2 2.1 %collective-permute-start = (bf16[64,8,256]{2,1,0:T(8,128)(2,1)S(1)}, bf16[64,8,256]{2,1,0:T(8,128)(2,1)S(1)}, u32[]{:S(2)}, u32[]{:S(2)}) collective-permute-start(bf16[64,8,256]{2,1,0:T(8,128)(2,1)S(1)} %bitcast.165), channel_id=1, source_target_pairs={{0,4},{4,8},{8,12},{12,16},{16,20},{20,24},{24,28},{28,32},{32,36}... | collective-permute-start | bytes 786440 | tf_op jit(solution)/shard_map/ppermute | solution.py:116
  56.6 0.9 collective-permute-done
  57.9 2.8 %collective-permute-start.5 = (bf16[2,16,256]{2,1,0:T(8,128)(2,1)S(1)}, bf16[2,16,256]{2,1,0:T(8,128)(2,1)S(1)}, u32[]{:S(2)}, u32[]{:S(2)}) collective-permute-start(bf16[2,16,256]{2,1,0:T(8,128)(2,1)S(1)} %pad_maximum_fusion.8), channel_id=1, source_target_pairs={{0,2},{1,3},{2,0},{3,1},{4,6},{5,7},{6,4},{7,5},{8,10},{9,11},{10,... | collective-permute-start | bytes 49160 | tf_op jit(solution)/shard_map/ppermute | solution.py:70
  60.8 0.8 collective-permute-done.6
  61.6 1.7 %collective-permute-done.5 = bf16[2,16,256]{2,1,0:T(8,128)(2,1)S(1)} collective-permute-done((bf16[2,16,256]{2,1,0:T(8,128)(2,1)S(1)}, bf16[2,16,256]{2,1,0:T(8,128)(2,1)S(1)}, u32[]{:S(2)}, u32[]{:S(2)}) %collective-permute-start.5) | collective-permute-done | bytes 16416 | tf_op jit(solution)/shard_map/ppermute | solution.py:70
  63.3 2.3 %collective-permute-done.4 = bf16[2,16,256]{2,1,0:T(8,128)(2,1)S(1)} collective-permute-done((bf16[2,16,256]{2,1,0:T(8,128)(2,1)S(1)}, bf16[2,16,256]{2,1,0:T(8,128)(2,1)S(1)}, u32[]{:S(2)}, u32[]{:S(2)}) %collective-permute-start.4) | collective-permute-done | bytes 16416 | tf_op jit(solution)/shard_map/ppermute | solution.py:70
  65.6 2.8 %fusion.52 = f32[2,16,1024]{2,1,0:T(8,128)S(1)} fusion(bf16[2,1024,1024]{2,1,0:T(8,128)(2,1)} %bitcast.158, bf16[2,16,256]{2,1,0:T(8,128)(2,1)S(1)} %collective-permute-done.6, bf16[2,16,256]{2,1,0:T(8,128)(2,1)S(1)} %collective-permute-done.5, bf16[2,16,256]{2,1,0:T(8,128)(2,1)S(1)} %collective-permute-done.4, ...), kind=kOutput, calls=%fused_computation.104 | convolution fusion | flops 67436544 | bytes 4390912 | tf_op jit(solution)/shard_map/arx,axu->aru/dot_general | solution.py:150
  68.5 1.2 convolution_convert_fusion.1
  69.7 2.1 %collective-permute-start.8 = (bf16[2,8,256]{2,1,0:T(8,128)(2,1)S(1)}, bf16[2,8,256]{2,1,0:T(8,128)(2,1)S(1)}, u32[]{:S(2)}, u32[]{:S(2)}) collective-permute-start(bf16[2,8,256]{2,1,0:T(8,128)(2,1)S(1)} %get-tuple-element.43), channel_id=1, source_target_pairs={{0,2},{1,3},{2,0},{3,1},{4,6},{5,7},{6,4},{7,5},{8,10},{9,11},{10,... | collective-permute-start | bytes 24584 | tf_op jit(solution)/shard_map/ppermute | solution.py:70
  71.9 1.1 collective-permute-start.7
  72.9 1.6 %collective-permute-done.9 = bf16[2,8,256]{2,1,0:T(8,128)(2,1)S(1)} collective-permute-done((bf16[2,8,256]{2,1,0:T(8,128)(2,1)S(1)}, bf16[2,8,256]{2,1,0:T(8,128)(2,1)S(1)}, u32[]{:S(2)}, u32[]{:S(2)}) %collective-permute-start.9) | collective-permute-done | bytes 8224 | tf_op jit(solution)/shard_map/ppermute | solution.py:70
  75.0 0.5 collective-permute-done.7
  75.5 1.3 collective-permute-start.11
  76.8 3.1 %collective-permute-start.10 = (bf16[8,8,256]{2,1,0:T(8,128)(2,1)S(1)}, bf16[8,8,256]{2,1,0:T(8,128)(2,1)S(1)}, u32[]{:S(2)}, u32[]{:S(2)}) collective-permute-start(bf16[8,8,256]{2,1,0:T(8,128)(2,1)S(1)} %pad_maximum_fusion.5), channel_id=1, source_target_pairs={{0,4},{4,8},{8,12},{12,16},{16,20},{20,24},{24,28},{28,32},{32,36}... | collective-permute-start | bytes 98312 | tf_op jit(solution)/shard_map/ppermute | solution.py:163
  80.1 0.6 collective-permute-done.10
  81.4 2.7 %collective-permute-start.14 = (bf16[2,16,256]{2,1,0:T(8,128)(2,1)S(1)}, bf16[2,16,256]{2,1,0:T(8,128)(2,1)S(1)}, u32[]{:S(2)}, u32[]{:S(2)}) collective-permute-start(bf16[2,16,256]{2,1,0:T(8,128)(2,1)S(1)} %pad_maximum_fusion.12), channel_id=1, source_target_pairs={{0,3},{1,0},{2,1},{3,2},{4,7},{5,4},{6,5},{7,6},{8,11},{9,8},{10,9... | collective-permute-start | bytes 49160 | tf_op jit(solution)/shard_map/ppermute | solution.py:70
  84.1 1.4 collective-permute-start.13
  85.6 3.7 %collective-permute-done.13 = bf16[2,16,256]{2,1,0:T(8,128)(2,1)S(1)} collective-permute-done((bf16[2,16,256]{2,1,0:T(8,128)(2,1)S(1)}, bf16[2,16,256]{2,1,0:T(8,128)(2,1)S(1)}, u32[]{:S(2)}, u32[]{:S(2)}) %collective-permute-start.13) | collective-permute-done | bytes 16416 | tf_op jit(solution)/shard_map/ppermute | solution.py:70
  89.3 1.1 collective-permute-done.12
  90.5 2.8 %fusion.62 = f32[2,16,1024]{2,1,0:T(8,128)S(1)} fusion(bf16[2,1024,1024]{2,1,0:T(8,128)(2,1)} %bitcast.159, bf16[2,16,256]{2,1,0:T(8,128)(2,1)S(1)} %collective-permute-done.14, bf16[2,16,256]{2,1,0:T(8,128)(2,1)S(1)} %collective-permute-done.13, bf16[2,16,256]{2,1,0:T(8,128)(2,1)S(1)} %collective-permute-done.12, ...), kind=kOutput, calls=%fused_computation.114 | convolution fusion | flops 67436544 | bytes 4390912 | tf_op jit(solution)/shard_map/arx,axu->aru/dot_general | solution.py:150
  93.4 1.2 convolution_convert_fusion
  94.7 1.2 collective-permute-start.16
  95.8 2.3 %collective-permute-start.15 = (bf16[2,8,256]{2,1,0:T(8,128)(2,1)S(1)}, bf16[2,8,256]{2,1,0:T(8,128)(2,1)S(1)}, u32[]{:S(2)}, u32[]{:S(2)}) collective-permute-start(bf16[2,8,256]{2,1,0:T(8,128)(2,1)S(1)} %get-tuple-element.32), channel_id=1, source_target_pairs={{0,3},{1,0},{2,1},{3,2},{4,7},{5,4},{6,5},{7,6},{8,11},{9,8},{10,9... | collective-permute-start | bytes 24584 | tf_op jit(solution)/shard_map/ppermute | solution.py:70
  98.2 1.3 collective-permute-done.17
  100.4 1.3 collective-permute-start.18
  101.9 2.7 %collective-permute-done.18 = bf16[8,8,256]{2,1,0:T(8,128)(2,1)S(1)} collective-permute-done((bf16[8,8,256]{2,1,0:T(8,128)(2,1)S(1)}, bf16[8,8,256]{2,1,0:T(8,128)(2,1)S(1)}, u32[]{:S(2)}, u32[]{:S(2)}) %collective-permute-start.18) | collective-permute-done | bytes 32800 | tf_op jit(solution)/shard_map/ppermute | solution.py:157
  104.6 1.3 fusion.7
  106.0 38.3 %all_to_all.10 = bf16[32,5,8,128]{3,2,1,0:T(8,128)(2,1)S(1)} all-to-all(bf16[32,5,8,128]{3,2,1,0:T(8,128)(2,1)S(1)} %pad_maximum_fusion.3), channel_id=1, replica_groups=mesh['grp'=2,'slab'=32,'ang'=4] {'slab'}, dimensions={0} | all-to-all | bytes 655360 | tf_op jit(solution)/shard_map/all_to_all | solution.py:175
  144.3 2.3 %collective-permute-start.20 = (bf16[2,256,256]{2,1,0:T(8,128)(2,1)S(1)}, bf16[2,256,256]{2,1,0:T(8,128)(2,1)S(1)}, u32[]{:S(2)}, u32[]{:S(2)}) collective-permute-start(bf16[2,256,256]{2,1,0:T(8,128)(2,1)S(1)} %bitcast.183), channel_id=1, source_target_pairs={{0,1},{1,2},{2,3},{3,0},{4,5},{5,6},{6,7},{7,4},{8,9},{9,10},{10,1... | collective-permute-start | bytes 786440 | tf_op jit(solution)/shard_map/ppermute | solution.py:183
  146.6 1.3 collective-permute-start.19
  148.1 5.8 %collective-permute-done.20 = bf16[2,256,256]{2,1,0:T(8,128)(2,1)S(1)} collective-permute-done((bf16[2,256,256]{2,1,0:T(8,128)(2,1)S(1)}, bf16[2,256,256]{2,1,0:T(8,128)(2,1)S(1)}, u32[]{:S(2)}, u32[]{:S(2)}) %collective-permute-start.20) | collective-permute-done | bytes 262176 | tf_op jit(solution)/shard_map/ppermute | solution.py:183
  154.0 0.8 collective-permute-start.21
  154.8 2.6 %collective-permute-start.22 = (bf16[1,256,256]{2,1,0:T(8,128)(2,1)S(1)}, bf16[1,256,256]{2,1,0:T(8,128)(2,1)S(1)}, u32[]{:S(2)}, u32[]{:S(2)}) collective-permute-start(bf16[1,256,256]{2,1,0:T(8,128)(2,1)S(1)} %slice.317), channel_id=1, source_target_pairs={{1,0},{2,1},{3,2},{0,3},{5,4},{6,5},{7,6},{4,7},{9,8},{10,9},{11,1... | collective-permute-start | bytes 393224 | tf_op jit(solution)/shard_map/ppermute | solution.py:185
  157.4 0.5 broadcast_multiply_fusion
  158.0 2.3 %collective-permute-done.21 = bf16[1,256,256]{2,1,0:T(8,128)(2,1)S(1)} collective-permute-done((bf16[1,256,256]{2,1,0:T(8,128)(2,1)S(1)}, bf16[1,256,256]{2,1,0:T(8,128)(2,1)S(1)}, u32[]{:S(2)}, u32[]{:S(2)}) %collective-permute-start.21) | collective-permute-done | bytes 131104 | tf_op jit(solution)/shard_map/ppermute | solution.py:185
  160.4 1.1 pad_maximum_fusion.1
  (99 shorter events, 4.4 us)
Async XLA Ops:
  0.6 6.1 %copy-start = (bf16[2,256,1024]{2,1,0:T(8,128)(2,1)S(1)}, bf16[2,256,1024]{2,1,0:T(8,128)(2,1)}, u32[]{:S(2)}) copy-start(bf16[2,256,1024]{2,1,0:T(8,128)(2,1)} %param.5) | copy-start | bytes 3145732
  0.6 37.6 %copy-start.4 = (f32[2,8,1024]{2,1,0:T(8,128)S(1)}, f32[2,8,1024]{2,1,0:T(8,128)}, u32[]{:S(2)}) copy-start(f32[2,8,1024]{2,1,0:T(8,128)} %param.8) | copy-start | bytes 196612
  0.7 55.7 %collective-permute-start.3 = (s32[2,64]{1,0:T(2,128)}, s32[2,64]{1,0:T(2,128)S(1)}, u32[]{:S(2)}, u32[]{:S(2)}) collective-permute-start(s32[2,64]{1,0:T(2,128)} %param.7), channel_id=1, source_target_pairs={{0,1},{1,2},{2,3},{3,0},{4,5},{5,6},{6,7},{7,4},{8,9},{9,10},{10,1... | collective-permute-start | bytes 1544 | tf_op jit(solution)/shard_map/ppermute | solution.py:70
  2.4 54.0 %collective-permute-start.2 = (s32[2,64]{1,0:T(2,128)}, s32[2,64]{1,0:T(2,128)S(1)}, u32[]{:S(2)}, u32[]{:S(2)}) collective-permute-start(s32[2,64]{1,0:T(2,128)} %param.7), channel_id=1, source_target_pairs={{0,2},{1,3},{2,0},{3,1},{4,6},{5,7},{6,4},{7,5},{8,10},{9,11},{10,... | collective-permute-start | bytes 1544 | tf_op jit(solution)/shard_map/ppermute | solution.py:70
  5.4 51.0 %collective-permute-start.1 = (s32[2,64]{1,0:T(2,128)}, s32[2,64]{1,0:T(2,128)S(1)}, u32[]{:S(2)}, u32[]{:S(2)}) collective-permute-start(s32[2,64]{1,0:T(2,128)} %param.7), channel_id=1, source_target_pairs={{0,3},{1,0},{2,1},{3,2},{4,7},{5,4},{6,5},{7,6},{8,11},{9,8},{10,9... | collective-permute-start | bytes 1544 | tf_op jit(solution)/shard_map/ppermute | solution.py:70
  7.5 46.7 %all-to-all-start = ((bf16[32,2,8,256]{3,2,1,0:T(8,128)(2,1)}), bf16[32,2,8,256]{3,2,1,0:T(8,128)(2,1)S(1)}, u32[]{:S(2)}, u32[]{:S(2)}) async-start(bf16[32,2,8,256]{3,2,1,0:T(8,128)(2,1)} %copy.34), calls=%async_computation | async-start | bytes 524288 | tf_op jit(solution)/shard_map/all_to_all | solution.py:115
  43.9 12.5 %copy-start.5 = (s32[2,64]{1,0:T(2,128)S(1)}, s32[2,64]{1,0:T(2,128)}, u32[]{:S(2)}) copy-start(s32[2,64]{1,0:T(2,128)} %param.7) | copy-start | bytes 1540
  54.2 14.3 %copy-start.1 = (bf16[2,4,256,1024]{3,2,1,0:T(8,128)(2,1)S(1)}, bf16[2,4,256,1024]{3,2,1,0:T(8,128)(2,1)}, u32[]{:S(2)}) copy-start(bf16[2,4,256,1024]{3,2,1,0:T(8,128)(2,1)} %pad_maximum_fusion) | copy-start | bytes 12582916
  54.2 3.3 %collective-permute-start = (bf16[64,8,256]{2,1,0:T(8,128)(2,1)S(1)}, bf16[64,8,256]{2,1,0:T(8,128)(2,1)S(1)}, u32[]{:S(2)}, u32[]{:S(2)}) collective-permute-start(bf16[64,8,256]{2,1,0:T(8,128)(2,1)S(1)} %bitcast.165), channel_id=1, source_target_pairs={{0,4},{4,8},{8,12},{12,16},{16,20},{20,24},{24,28},{28,32},{32,36}... | collective-permute-start | bytes 786440 | tf_op jit(solution)/shard_map/ppermute | solution.py:116
  57.8 3.9 %collective-permute-start.6 = (bf16[2,16,256]{2,1,0:T(8,128)(2,1)S(1)}, bf16[2,16,256]{2,1,0:T(8,128)(2,1)S(1)}, u32[]{:S(2)}, u32[]{:S(2)}) collective-permute-start(bf16[2,16,256]{2,1,0:T(8,128)(2,1)S(1)} %pad_maximum_fusion.9), channel_id=1, source_target_pairs={{0,3},{1,0},{2,1},{3,2},{4,7},{5,4},{6,5},{7,6},{8,11},{9,8},{10,9... | collective-permute-start | bytes 49160 | tf_op jit(solution)/shard_map/ppermute | solution.py:70
  57.9 5.4 %collective-permute-start.5 = (bf16[2,16,256]{2,1,0:T(8,128)(2,1)S(1)}, bf16[2,16,256]{2,1,0:T(8,128)(2,1)S(1)}, u32[]{:S(2)}, u32[]{:S(2)}) collective-permute-start(bf16[2,16,256]{2,1,0:T(8,128)(2,1)S(1)} %pad_maximum_fusion.8), channel_id=1, source_target_pairs={{0,2},{1,3},{2,0},{3,1},{4,6},{5,7},{6,4},{7,5},{8,10},{9,11},{10,... | collective-permute-start | bytes 49160 | tf_op jit(solution)/shard_map/ppermute | solution.py:70
  60.7 5.0 %collective-permute-start.4 = (bf16[2,16,256]{2,1,0:T(8,128)(2,1)S(1)}, bf16[2,16,256]{2,1,0:T(8,128)(2,1)S(1)}, u32[]{:S(2)}, u32[]{:S(2)}) collective-permute-start(bf16[2,16,256]{2,1,0:T(8,128)(2,1)S(1)} %pad_maximum_fusion.7), channel_id=1, source_target_pairs={{0,1},{1,2},{2,3},{3,0},{4,5},{5,6},{6,7},{7,4},{8,9},{9,10},{10,1... | collective-permute-start | bytes 49160 | tf_op jit(solution)/shard_map/ppermute | solution.py:70
  69.7 4.9 %collective-permute-start.9 = (bf16[2,8,256]{2,1,0:T(8,128)(2,1)S(1)}, bf16[2,8,256]{2,1,0:T(8,128)(2,1)S(1)}, u32[]{:S(2)}, u32[]{:S(2)}) collective-permute-start(bf16[2,8,256]{2,1,0:T(8,128)(2,1)S(1)} %get-tuple-element.42), channel_id=1, source_target_pairs={{0,1},{1,2},{2,3},{3,0},{4,5},{5,6},{6,7},{7,4},{8,9},{9,10},{10,1... | collective-permute-start | bytes 24584 | tf_op jit(solution)/shard_map/ppermute | solution.py:70
  69.7 5.3 %collective-permute-start.8 = (bf16[2,8,256]{2,1,0:T(8,128)(2,1)S(1)}, bf16[2,8,256]{2,1,0:T(8,128)(2,1)S(1)}, u32[]{:S(2)}, u32[]{:S(2)}) collective-permute-start(bf16[2,8,256]{2,1,0:T(8,128)(2,1)S(1)} %get-tuple-element.43), channel_id=1, source_target_pairs={{0,2},{1,3},{2,0},{3,1},{4,6},{5,7},{6,4},{7,5},{8,10},{9,11},{10,... | collective-permute-start | bytes 24584 | tf_op jit(solution)/shard_map/ppermute | solution.py:70
  71.9 3.7 %collective-permute-start.7 = (bf16[2,8,256]{2,1,0:T(8,128)(2,1)S(1)}, bf16[2,8,256]{2,1,0:T(8,128)(2,1)S(1)}, u32[]{:S(2)}, u32[]{:S(2)}) collective-permute-start(bf16[2,8,256]{2,1,0:T(8,128)(2,1)S(1)} %get-tuple-element.44), channel_id=1, source_target_pairs={{0,3},{1,0},{2,1},{3,2},{4,7},{5,4},{6,5},{7,6},{8,11},{9,8},{10,9... | collective-permute-start | bytes 24584 | tf_op jit(solution)/shard_map/ppermute | solution.py:70
  75.5 4.6 %collective-permute-start.11 = (bf16[8,8,256]{2,1,0:T(8,128)(2,1)S(1)}, bf16[8,8,256]{2,1,0:T(8,128)(2,1)S(1)}, u32[]{:S(2)}, u32[]{:S(2)}) collective-permute-start(bf16[8,8,256]{2,1,0:T(8,128)(2,1)S(1)} %pad_maximum_fusion.5), channel_id=1, source_target_pairs={{4,0},{8,4},{12,8},{16,12},{20,16},{24,20},{28,24},{32,28},{36,32}... | collective-permute-start | bytes 98312 | tf_op jit(solution)/shard_map/ppermute | solution.py:157
  76.8 3.9 %collective-permute-start.10 = (bf16[8,8,256]{2,1,0:T(8,128)(2,1)S(1)}, bf16[8,8,256]{2,1,0:T(8,128)(2,1)S(1)}, u32[]{:S(2)}, u32[]{:S(2)}) collective-permute-start(bf16[8,8,256]{2,1,0:T(8,128)(2,1)S(1)} %pad_maximum_fusion.5), channel_id=1, source_target_pairs={{0,4},{4,8},{8,12},{12,16},{16,20},{20,24},{24,28},{28,32},{32,36}... | collective-permute-start | bytes 98312 | tf_op jit(solution)/shard_map/ppermute | solution.py:163
  81.4 4.2 %collective-permute-start.14 = (bf16[2,16,256]{2,1,0:T(8,128)(2,1)S(1)}, bf16[2,16,256]{2,1,0:T(8,128)(2,1)S(1)}, u32[]{:S(2)}, u32[]{:S(2)}) collective-permute-start(bf16[2,16,256]{2,1,0:T(8,128)(2,1)S(1)} %pad_maximum_fusion.12), channel_id=1, source_target_pairs={{0,3},{1,0},{2,1},{3,2},{4,7},{5,4},{6,5},{7,6},{8,11},{9,8},{10,9... | collective-permute-start | bytes 49160 | tf_op jit(solution)/shard_map/ppermute | solution.py:70
  84.1 5.2 %collective-permute-start.13 = (bf16[2,16,256]{2,1,0:T(8,128)(2,1)S(1)}, bf16[2,16,256]{2,1,0:T(8,128)(2,1)S(1)}, u32[]{:S(2)}, u32[]{:S(2)}) collective-permute-start(bf16[2,16,256]{2,1,0:T(8,128)(2,1)S(1)} %pad_maximum_fusion.11), channel_id=1, source_target_pairs={{0,2},{1,3},{2,0},{3,1},{4,6},{5,7},{6,4},{7,5},{8,10},{9,11},{10,... | collective-permute-start | bytes 49160 | tf_op jit(solution)/shard_map/ppermute | solution.py:70
  85.5 4.9 %collective-permute-start.12 = (bf16[2,16,256]{2,1,0:T(8,128)(2,1)S(1)}, bf16[2,16,256]{2,1,0:T(8,128)(2,1)S(1)}, u32[]{:S(2)}, u32[]{:S(2)}) collective-permute-start(bf16[2,16,256]{2,1,0:T(8,128)(2,1)S(1)} %pad_maximum_fusion.10), channel_id=1, source_target_pairs={{0,1},{1,2},{2,3},{3,0},{4,5},{5,6},{6,7},{7,4},{8,9},{9,10},{10,1... | collective-permute-start | bytes 49160 | tf_op jit(solution)/shard_map/ppermute | solution.py:70
  85.6 7.8 %copy-start.2 = (bf16[2,4,256,1024]{3,2,1,0:T(8,128)(2,1)S(1)}, bf16[2,4,256,1024]{3,2,1,0:T(8,128)(2,1)}, u32[]{:S(2)}) copy-start(bf16[2,4,256,1024]{3,2,1,0:T(8,128)(2,1)} %pad_maximum_fusion) | copy-start | bytes 12582916
  93.4 12.6 %copy-start.3 = (f32[2,8,1024]{2,1,0:T(8,128)}, f32[2,8,1024]{2,1,0:T(8,128)S(1)}, u32[]{:S(2)}) copy-start(f32[2,8,1024]{2,1,0:T(8,128)S(1)} %get-tuple-element.21) | copy-start | bytes 196612
  94.6 4.9 %collective-permute-start.17 = (bf16[2,8,256]{2,1,0:T(8,128)(2,1)S(1)}, bf16[2,8,256]{2,1,0:T(8,128)(2,1)S(1)}, u32[]{:S(2)}, u32[]{:S(2)}) collective-permute-start(bf16[2,8,256]{2,1,0:T(8,128)(2,1)S(1)} %get-tuple-element.30), channel_id=1, source_target_pairs={{0,1},{1,2},{2,3},{3,0},{4,5},{5,6},{6,7},{7,4},{8,9},{9,10},{10,1... | collective-permute-start | bytes 24584 | tf_op jit(solution)/shard_map/ppermute | solution.py:70
  94.7 5.3 %collective-permute-start.16 = (bf16[2,8,256]{2,1,0:T(8,128)(2,1)S(1)}, bf16[2,8,256]{2,1,0:T(8,128)(2,1)S(1)}, u32[]{:S(2)}, u32[]{:S(2)}) collective-permute-start(bf16[2,8,256]{2,1,0:T(8,128)(2,1)S(1)} %get-tuple-element.31), channel_id=1, source_target_pairs={{0,2},{1,3},{2,0},{3,1},{4,6},{5,7},{6,4},{7,5},{8,10},{9,11},{10,... | collective-permute-start | bytes 24584 | tf_op jit(solution)/shard_map/ppermute | solution.py:70
  95.8 4.6 %collective-permute-start.15 = (bf16[2,8,256]{2,1,0:T(8,128)(2,1)S(1)}, bf16[2,8,256]{2,1,0:T(8,128)(2,1)S(1)}, u32[]{:S(2)}, u32[]{:S(2)}) collective-permute-start(bf16[2,8,256]{2,1,0:T(8,128)(2,1)S(1)} %get-tuple-element.32), channel_id=1, source_target_pairs={{0,3},{1,0},{2,1},{3,2},{4,7},{5,4},{6,5},{7,6},{8,11},{9,8},{10,9... | collective-permute-start | bytes 24584 | tf_op jit(solution)/shard_map/ppermute | solution.py:70
  100.4 4.1 %collective-permute-start.18 = (bf16[8,8,256]{2,1,0:T(8,128)(2,1)S(1)}, bf16[8,8,256]{2,1,0:T(8,128)(2,1)S(1)}, u32[]{:S(2)}, u32[]{:S(2)}) collective-permute-start(bf16[8,8,256]{2,1,0:T(8,128)(2,1)S(1)} %pad_maximum_fusion.6), channel_id=1, source_target_pairs={{4,0},{8,4},{12,8},{16,12},{20,16},{24,20},{28,24},{32,28},{36,32}... | collective-permute-start | bytes 98312 | tf_op jit(solution)/shard_map/ppermute | solution.py:157
  144.3 9.6 %collective-permute-start.20 = (bf16[2,256,256]{2,1,0:T(8,128)(2,1)S(1)}, bf16[2,256,256]{2,1,0:T(8,128)(2,1)S(1)}, u32[]{:S(2)}, u32[]{:S(2)}) collective-permute-start(bf16[2,256,256]{2,1,0:T(8,128)(2,1)S(1)} %bitcast.183), channel_id=1, source_target_pairs={{0,1},{1,2},{2,3},{3,0},{4,5},{5,6},{6,7},{7,4},{8,9},{9,10},{10,1... | collective-permute-start | bytes 786440 | tf_op jit(solution)/shard_map/ppermute | solution.py:183
  146.6 8.2 %collective-permute-start.19 = (bf16[2,256,256]{2,1,0:T(8,128)(2,1)S(1)}, bf16[2,256,256]{2,1,0:T(8,128)(2,1)S(1)}, u32[]{:S(2)}, u32[]{:S(2)}) collective-permute-start(bf16[2,256,256]{2,1,0:T(8,128)(2,1)S(1)} %bitcast.184), channel_id=1, source_target_pairs={{1,0},{2,1},{3,2},{0,3},{5,4},{6,5},{7,6},{4,7},{9,8},{10,9},{11,1... | collective-permute-start | bytes 786440 | tf_op jit(solution)/shard_map/ppermute | solution.py:184
  154.0 6.3 %collective-permute-start.21 = (bf16[1,256,256]{2,1,0:T(8,128)(2,1)S(1)}, bf16[1,256,256]{2,1,0:T(8,128)(2,1)S(1)}, u32[]{:S(2)}, u32[]{:S(2)}) collective-permute-start(bf16[1,256,256]{2,1,0:T(8,128)(2,1)S(1)} %slice.316), channel_id=1, source_target_pairs={{0,1},{1,2},{2,3},{3,0},{4,5},{5,6},{6,7},{7,4},{8,9},{9,10},{10,1... | collective-permute-start | bytes 393224 | tf_op jit(solution)/shard_map/ppermute | solution.py:185
  154.8 5.4 %collective-permute-start.22 = (bf16[1,256,256]{2,1,0:T(8,128)(2,1)S(1)}, bf16[1,256,256]{2,1,0:T(8,128)(2,1)S(1)}, u32[]{:S(2)}, u32[]{:S(2)}) collective-permute-start(bf16[1,256,256]{2,1,0:T(8,128)(2,1)S(1)} %slice.317), channel_id=1, source_target_pairs={{1,0},{2,1},{3,2},{0,3},{5,4},{6,5},{7,6},{4,7},{9,8},{10,9},{11,1... | collective-permute-start | bytes 393224 | tf_op jit(solution)/shard_map/ppermute | solution.py:185

commit v4 on v3

--- a/solution.py
+++ b/solution.py
@@ -5,7 +5,7 @@
 from jax import lax
 from jax.sharding import PartitionSpec as P
 
-OFF = 8
+
 ROUNDS = 2
 STEP_SIZE = 0.5
 
@@ -108,18 +108,19 @@
     down_ring = [(i, i + 1) for i in range(slabs - 1)]
     up_ring = [(i + 1, i) for i in range(slabs - 1)]
 
-    table = jnp.stack(from_ang([row_offsets] * angs, -1)).reshape(angles, slices)
+    table = from_ang([row_offsets] * angs, -1)
+    table = jnp.stack(table).reshape(angles, slices)
 
     mine = lax.dynamic_slice_in_dim(volume, here * chunk, chunk, 2)
     mine = mine.reshape(slices_here, slabs, band, chunk).transpose(1, 0, 2, 3)
-    own = lax.all_to_all(mine, SLAB, 0, 0, tiled=True).reshape(slices, band, chunk)
+    own = lax.all_to_all(mine, SLAB, 0, 0, tiled=True)
+    own = own.reshape(slices, band, chunk)
     above = lax.ppermute(own, SLAB, down_ring)
     current = jnp.concatenate([above, own], axis=1)
 
-    weights = ray_weights.reshape(angles_here, angs, chunk, columns)
-    weights = jnp.concatenate(
-        [lax.dynamic_slice_in_dim(weights, (here + angs - k) % angs, 1, 1) for k in range(angs)], axis=1
-    ).reshape(angles_here, cells, columns)
+    weights = [
+        lax.dynamic_slice_in_dim(ray_weights, (here + angs - k) % angs * chunk, chunk, 1) for k in range(angs)
+    ]
 
     shifted, slope_field = registered(measured, shifts)
 
@@ -146,13 +147,16 @@
             x.reshape(angs, angles_here, band, chunk) for x in split_parts(stacked, 2)
         )
         parts = from_ang([jnp.concatenate([high[k], low[k]], axis=1) for k in range(angs)], 1)
-        parts = jnp.concatenate(parts, axis=2)
-        product = jnp.einsum("arx,axu->aru", parts, weights, preferred_element_type=f32)
+        product = sum(
+            jnp.einsum("arx,axu->aru", x, w, preferred_element_type=f32) for x, w in zip(parts, weights)
+        )
         projection = product[:, :band] + product[:, band:]
         residual = projection - shifted
         rounded = residual.astype(bf16)
-        back = jnp.einsum("aru,axu->arx", rounded, weights, preferred_element_type=f32).astype(bf16)
-        back = from_ang([back[:, :, k * chunk : (k + 1) * chunk] for k in range(angs)], -1)
+        back = [
+            jnp.einsum("aru,axu->arx", rounded, w, preferred_element_type=f32).astype(bf16) for w in weights
+        ]
+        back = from_ang(back, -1)
         back = jnp.concatenate(back, axis=0)
         below = lax.ppermute(back, SLAB, up_ring)
         if last:
@@ -166,17 +170,15 @@
         gradient = jnp.dot(pick, window.reshape(-1, chunk), preferred_element_type=f32)
         current = (before.astype(f32) - STEP_SIZE * gradient.reshape(before.shape)).astype(bf16)
 
-    lanes = 128
-    dots = jnp.stack(split_parts(jnp.sum(projection * slope_field, axis=(1, 2)), 3))
-    dots = jnp.pad(dots.reshape(1, -1), ((0, band - 1), (0, lanes - dots.size)))
-    dots = jnp.broadcast_to(dots, (slabs, 1, band, lanes))
-    home = current.reshape(slabs, slices_here, band, chunk // lanes, lanes).transpose(0, 1, 3, 2, 4)
-    home = home.reshape(slabs, -1, band, lanes)
-    home = lax.all_to_all(jnp.concatenate([home, dots], axis=1), SLAB, 0, 0, tiled=True)
-    dots = home[:, -1, 0, : 3 * angles_here].astype(f32).reshape(slabs, 3, angles_here)
-    shift_slope = jnp.sum(dots, axis=(0, 1)) / math.sqrt(rows_all * columns)
-    home = home[:, :-1].reshape(slabs, slices_here, chunk // lanes, band, lanes)
-    home = home.transpose(1, 0, 3, 2, 4).reshape(slices_here, rows_all, chunk)
+    home = current.reshape(slabs, slices_here, band, chunk)
+    home = lax.all_to_all(home, SLAB, 0, 0, tiled=True)
+    home = home.transpose(1, 0, 2, 3).reshape(slices_here, rows_all, chunk)
+    dots = jnp.sum(projection * slope_field, axis=(1, 2))
+    bit = 1
+    while bit < slabs:
+        dots = dots + lax.ppermute(dots, SLAB, [(i, i ^ bit) for i in range(slabs)])
+        bit *= 2
+    shift_slope = dots * (1.0 / math.sqrt(rows_all * columns))
     ahead = [(i, (i + 1) % angs) for i in range(angs)]
     behind = [((i + 1) % angs, i) for i in range(angs)]
     half = slices_here // 2

time: 162 us -> 173 us (1.068)
  waiting for transfers between devices: 35 us -> 56.6 us
  blocking collectives: 38.3 us -> 32.2 us
  local copies, waits for them, and re-layouts: 5.36 us -> 2.51 us
    ppermute x0 -> x5, waiting for transfers between devices: none -> 24.8 us  [per_device(): dots = dots + lax.ppermute(dots, SLAB, [(i, i ^ bit) for i in range(slabs)])]
    all_to_all x1, blocking collectives: 38.3 us -> 32.2 us  [per_device(): home = lax.all_to_all(home, SLAB, 0, 0, tiled=True)]
    ppermute x1, waiting for transfers between devices: 5.84 us -> 0.01 us  [per_device(): lower = lax.ppermute(home, 'ang', ahead)]
    ppermute x2, waiting for transfers between devices: 2.72 us -> 8.48 us  [per_device(): below = lax.ppermute(back, SLAB, up_ring)]
    ppermute x15, waiting for transfers between devices: 14.5 us -> 9.47 us  [from_ang(): lax.ppermute(blocks[k], 'ang', [(i, (i + k * step) % size) for i in range...]
    all_to_all x1, waiting for transfers between devices: 8.05 us -> 13 us  [per_device(): own = lax.all_to_all(mine, SLAB, 0, 0, tiled=True)]
    dynamic_slice x1 -> x0, local copies, waits for them, and re-layouts: 2.63 us -> none  [per_device(): lax.dynamic_slice_in_dim(weights, (here + angs - k) % angs, 1, 1)]
    ppermute x1, waiting for transfers between devices: 2.3 us -> 0.01 us  [per_device(): lax.ppermute(lower[:half], 'ang', ahead)]
  transfers between devices with their start and end apart: 24 -> 29, of which waited for: 17 -> 15; matrix products, arithmetic and copies ran while one was open for 10% -> 9% of each run, Pallas kernels for 0% -> 0%
where the time goes in v4:
time: 173 us; the launch traced here: 172 us
  starting transfers between devices  58.7 us (34%)
  waiting for transfers between devices  56.6 us (33%)
  blocking collectives  32.2 us (19%)
  matrix products  12.3 us (7%)
  other arithmetic  8.65 us (5%)
  local copies, waits for them, and re-layouts  2.51 us (1%)
    all_to_all x1, blocking collectives, per_device(): home = lax.all_to_all(home, SLAB, 0, 0, tiled=True)  32.2 us
    ppermute x5, waiting for transfers between devices, per_device(): dots = dots + lax.ppermute(dots, SLAB, [(i, i ^ bit) for i in range(slabs)])  24.8 us
    all_to_all x1, starting transfers between devices, per_device(): own = lax.all_to_all(mine, SLAB, 0, 0, tiled=True)  24.7 us
    ppermute x15, starting transfers between devices, from_ang(): lax.ppermute(blocks[k], 'ang', [(i, (i + k * step) % size) for i in range...  20.3 us
    all_to_all x1, waiting for transfers between devices, per_device(): own = lax.all_to_all(mine, SLAB, 0, 0, tiled=True)  13 us
    ppermute x15, waiting for transfers between devices, from_ang(): lax.ppermute(blocks[k], 'ang', [(i, (i + k * step) % size) for i in range...  9.47 us
    ppermute x2, waiting for transfers between devices, per_device(): below = lax.ppermute(back, SLAB, up_ring)  8.48 us
    dot_general x8, matrix products, per_device(): jnp.einsum('arx,axu->aru', x, w, preferred_element_type=f32)  5.7 us
  transfers between devices with their start and end apart: 29, of which 15 were waited for; matrix products, arithmetic and copies ran while one was open for 9% of the time, Pallas kernels for 0%

profile of v4, /device:TPU:40, one launch (start us, length us, event | category | flops | bytes accessed | tf_op | source)
XLA Modules:
  0.0 172.2 jit_solution(2005482115066912757)
XLA Ops:
  0.7 3.3 %collective-permute-start.1 = (s32[2,64]{1,0:T(2,128)}, s32[2,64]{1,0:T(2,128)S(1)}, u32[]{:S(2)}, u32[]{:S(2)}) collective-permute-start(s32[2,64]{1,0:T(2,128)} %param.7), channel_id=1, source_target_pairs={{0,3},{1,0},{2,1},{3,2},{4,7},{5,4},{6,5},{7,6},{8,11},{9,8},{10,9... | collective-permute-start | bytes 1544 | tf_op jit(solution)/shard_map/ppermute | solution.py:70
  3.9 0.5 collective-permute-start.2
  4.5 1.0 collective-permute-start.3
  5.5 0.7 copy.23
  6.2 24.7 %all-to-all-start = ((bf16[32,2,8,256]{3,2,1,0:T(8,128)(2,1)}), bf16[32,2,8,256]{3,2,1,0:T(8,128)(2,1)S(1)}, u32[]{:S(2)}, u32[]{:S(2)}) async-start(bf16[32,2,8,256]{3,2,1,0:T(8,128)(2,1)} %copy.23), calls=%async_computation | async-start | bytes 524288 | tf_op jit(solution)/shard_map/all_to_all | solution.py:116
  31.2 0.7 round-nearest-even_convert_fusion
  31.9 4.9 %fusion.11 = (f32[2,128,1024]{2,1,0:T(8,128)S(1)}, f32[2,128,1024]{2,1,0:T(8,128)S(1)}) fusion(f32[2]{0:T(128)S(1)} %get-tuple-element.43, f32[128,1024]{1,0:T(8,128)S(1)} %get-tuple-element.51, f32[2]{0:T(128)S(1)} %get-tuple-element.45, s32[2]{0:T(128)S(1)} %get-tuple-element.42, s32[128,1024]{1,0:T(8,128)S(1)} %fusion.47, f32[2]{0:T(128)S(1)} %get-tuple-element.44, ...), kind=kLoop, calls=%fused_computation.31 | loop fusion | flops 9699328 | bytes 3670048 | tf_op jit(solution)/shard_map/jit(_where)/select_n | solution.py:45
  36.9 1.3 convolution_bitcast_fusion
  38.2 0.9 reshape.322
  40.0 13.0 %all-to-all-done = bf16[32,2,8,256]{3,2,1,0:T(8,128)(2,1)S(1)} async-done(((bf16[32,2,8,256]{3,2,1,0:T(8,128)(2,1)}), bf16[32,2,8,256]{3,2,1,0:T(8,128)(2,1)S(1)}, u32[]{:S(2)}, u32[]{:S(2)}) %all-to-all-start) | async-done | bytes 262176 | tf_op jit(solution)/shard_map/all_to_all | solution.py:116
  53.0 2.3 %collective-permute-start = (bf16[64,8,256]{2,1,0:T(8,128)(2,1)S(1)}, bf16[64,8,256]{2,1,0:T(8,128)(2,1)S(1)}, u32[]{:S(2)}, u32[]{:S(2)}) collective-permute-start(bf16[64,8,256]{2,1,0:T(8,128)(2,1)S(1)} %bitcast.156), channel_id=1, source_target_pairs={{0,4},{4,8},{8,12},{12,16},{16,20},{20,24},{24,28},{28,32},{32,36}... | collective-permute-start | bytes 786440 | tf_op jit(solution)/shard_map/ppermute | solution.py:118
  55.5 0.7 collective-permute-done
  56.6 2.1 %collective-permute-start.4 = (bf16[2,16,256]{2,1,0:T(8,128)(2,1)S(1)}, bf16[2,16,256]{2,1,0:T(8,128)(2,1)S(1)}, u32[]{:S(2)}, u32[]{:S(2)}) collective-permute-start(bf16[2,16,256]{2,1,0:T(8,128)(2,1)S(1)} %pad_maximum_fusion.5), channel_id=1, source_target_pairs={{0,1},{1,2},{2,3},{3,0},{4,5},{5,6},{6,7},{7,4},{8,9},{9,10},{10,1... | collective-permute-start | bytes 49160 | tf_op jit(solution)/shard_map/ppermute | solution.py:70
  58.6 1.3 collective-permute-start.6
  59.9 0.9 collective-permute-start.5
  60.8 1.5 fusion.45
  62.3 1.5 convolution_add_fusion.3
  64.1 1.1 collective-permute-done.5
  65.8 0.4 convolution_convert_fusion.6
  66.6 1.4 collective-permute-start.7
  68.0 1.4 collective-permute-start.8
  70.3 2.9 %collective-permute-done.8 = bf16[2,8,256]{2,1,0:T(8,128)(2,1)S(1)} collective-permute-done((bf16[2,8,256]{2,1,0:T(8,128)(2,1)S(1)}, bf16[2,8,256]{2,1,0:T(8,128)(2,1)S(1)}, u32[]{:S(2)}, u32[]{:S(2)}) %collective-permute-start.8) | collective-permute-done | bytes 8224 | tf_op jit(solution)/shard_map/ppermute | solution.py:70
  73.2 1.1 collective-permute-done.9
  74.3 1.3 collective-permute-start.10
  75.6 1.3 collective-permute-start.11
  77.1 6.8 %collective-permute-done.11 = bf16[8,8,256]{2,1,0:T(8,128)(2,1)S(1)} collective-permute-done((bf16[8,8,256]{2,1,0:T(8,128)(2,1)S(1)}, bf16[8,8,256]{2,1,0:T(8,128)(2,1)S(1)}, u32[]{:S(2)}, u32[]{:S(2)}) %collective-permute-start.11) | collective-permute-done | bytes 32800 | tf_op jit(solution)/shard_map/ppermute | solution.py:161
  84.5 1.0 collective-permute-start.13
  85.5 0.6 collective-permute-start.12
  86.2 2.6 %collective-permute-start.14 = (bf16[2,16,256]{2,1,0:T(8,128)(2,1)S(1)}, bf16[2,16,256]{2,1,0:T(8,128)(2,1)S(1)}, u32[]{:S(2)}, u32[]{:S(2)}) collective-permute-start(bf16[2,16,256]{2,1,0:T(8,128)(2,1)S(1)} %pad_maximum_fusion.10), channel_id=1, source_target_pairs={{0,3},{1,0},{2,1},{3,2},{4,7},{5,4},{6,5},{7,6},{8,11},{9,8},{10,9... | collective-permute-start | bytes 49160 | tf_op jit(solution)/shard_map/ppermute | solution.py:70
  88.8 1.5 fusion.42
  91.3 0.7 fusion.122
  93.1 3.0 %collective-permute-start.15 = (bf16[2,8,256]{2,1,0:T(8,128)(2,1)S(1)}, bf16[2,8,256]{2,1,0:T(8,128)(2,1)S(1)}, u32[]{:S(2)}, u32[]{:S(2)}) collective-permute-start(bf16[2,8,256]{2,1,0:T(8,128)(2,1)S(1)} %convolution_convert_fusion.3), channel_id=1, source_target_pairs={{0,3},{1,0},{2,1},{3,2},{4,7},{5,4},{6,5},{7,6},{8,11},{9,8},{10,9... | collective-permute-start | bytes 24584 | tf_op jit(solution)/shard_map/ppermute | solution.py:70
  96.3 0.8 collective-permute-start.17
  97.4 3.8 %collective-permute-done.16 = bf16[2,8,256]{2,1,0:T(8,128)(2,1)S(1)} collective-permute-done((bf16[2,8,256]{2,1,0:T(8,128)(2,1)S(1)}, bf16[2,8,256]{2,1,0:T(8,128)(2,1)S(1)}, u32[]{:S(2)}, u32[]{:S(2)}) %collective-permute-start.16) | collective-permute-done | bytes 8224 | tf_op jit(solution)/shard_map/ppermute | solution.py:70
  101.2 1.3 collective-permute-start.18
  102.6 1.7 %collective-permute-done.18 = bf16[8,8,256]{2,1,0:T(8,128)(2,1)S(1)} collective-permute-done((bf16[8,8,256]{2,1,0:T(8,128)(2,1)S(1)}, bf16[8,8,256]{2,1,0:T(8,128)(2,1)S(1)}, u32[]{:S(2)}, u32[]{:S(2)}) %collective-permute-start.18) | collective-permute-done | bytes 32800 | tf_op jit(solution)/shard_map/ppermute | solution.py:161
  104.4 1.3 fusion.7
  105.7 32.2 %all_to_all.10 = bf16[32,2,8,256]{3,2,1,0:T(8,128)(2,1)S(1)} all-to-all(bf16[32,2,8,256]{3,2,1,0:T(8,128)(2,1)S(1)} %bitcast.174), channel_id=1, replica_groups=mesh['grp'=2,'slab'=32,'ang'=4] {'slab'}, dimensions={0} | all-to-all | bytes 524288 | tf_op jit(solution)/shard_map/all_to_all | solution.py:174
  138.0 3.2 %collective-permute-start.19 = (bf16[2,256,256]{2,1,0:T(8,128)(2,1)S(1)}, bf16[2,256,256]{2,1,0:T(8,128)(2,1)S(1)}, u32[]{:S(2)}, u32[]{:S(2)}) collective-permute-start(bf16[2,256,256]{2,1,0:T(8,128)(2,1)S(1)} %copy_bitcast_fusion), channel_id=1, source_target_pairs={{1,0},{2,1},{3,2},{0,3},{5,4},{6,5},{7,6},{4,7},{9,8},{10,9},{11,1... | collective-permute-start | bytes 786440 | tf_op jit(solution)/shard_map/ppermute | solution.py:186
  141.2 1.2 collective-permute-done.23
  142.6 3.4 %collective-permute-done.24 = f32[2]{0:T(128)S(1)} collective-permute-done((f32[2]{0:T(128)S(1)}, f32[2]{0:T(128)S(1)}, u32[]{:S(2)}, u32[]{:S(2)}) %collective-permute-start.24) | collective-permute-done | bytes 40 | tf_op jit(solution)/shard_map/ppermute | solution.py:179
  146.0 4.5 %collective-permute-done.25 = f32[2]{0:T(128)S(1)} collective-permute-done((f32[2]{0:T(128)S(1)}, f32[2]{0:T(128)S(1)}, u32[]{:S(2)}, u32[]{:S(2)}) %collective-permute-start.25) | collective-permute-done | bytes 40 | tf_op jit(solution)/shard_map/ppermute | solution.py:179
  150.4 7.5 %collective-permute-done.26 = f32[2]{0:T(128)S(1)} collective-permute-done((f32[2]{0:T(128)S(1)}, f32[2]{0:T(128)S(1)}, u32[]{:S(2)}, u32[]{:S(2)}) %collective-permute-start.26) | collective-permute-done | bytes 40 | tf_op jit(solution)/shard_map/ppermute | solution.py:179
  157.9 0.4 collective-permute-start.27
  158.5 3.3 %collective-permute-start.22 = (bf16[1,256,256]{2,1,0:T(8,128)(2,1)S(1)}, bf16[1,256,256]{2,1,0:T(8,128)(2,1)S(1)}, u32[]{:S(2)}, u32[]{:S(2)}) collective-permute-start(bf16[1,256,256]{2,1,0:T(8,128)(2,1)S(1)} %slice.267), channel_id=1, source_target_pairs={{1,0},{2,1},{3,2},{0,3},{5,4},{6,5},{7,6},{4,7},{9,8},{10,9},{11,1... | collective-permute-start | bytes 393224 | tf_op jit(solution)/shard_map/ppermute | solution.py:187
  161.8 8.4 %collective-permute-done.27 = f32[2]{0:T(128)S(1)} collective-permute-done((f32[2]{0:T(128)S(1)}, f32[2]{0:T(128)S(1)}, u32[]{:S(2)}, u32[]{:S(2)}) %collective-permute-start.27) | collective-permute-done | bytes 40 | tf_op jit(solution)/shard_map/ppermute | solution.py:179
  170.2 0.5 add_multiply_fusion
  171.1 1.1 pad_maximum_fusion
  (110 shorter events, 7.9 us)
Async XLA Ops:
  0.6 4.9 %copy-start = (bf16[2,256,1024]{2,1,0:T(8,128)(2,1)S(1)}, bf16[2,256,1024]{2,1,0:T(8,128)(2,1)}, u32[]{:S(2)}) copy-start(bf16[2,256,1024]{2,1,0:T(8,128)(2,1)} %param.5) | copy-start | bytes 3145732
  0.6 36.2 %copy-start.3 = (f32[2,8,1024]{2,1,0:T(8,128)S(1)}, f32[2,8,1024]{2,1,0:T(8,128)}, u32[]{:S(2)}) copy-start(f32[2,8,1024]{2,1,0:T(8,128)} %param.8) | copy-start | bytes 196612
  0.7 54.7 %collective-permute-start.1 = (s32[2,64]{1,0:T(2,128)}, s32[2,64]{1,0:T(2,128)S(1)}, u32[]{:S(2)}, u32[]{:S(2)}) collective-permute-start(s32[2,64]{1,0:T(2,128)} %param.7), channel_id=1, source_target_pairs={{0,3},{1,0},{2,1},{3,2},{4,7},{5,4},{6,5},{7,6},{8,11},{9,8},{10,9... | collective-permute-start | bytes 1544 | tf_op jit(solution)/shard_map/ppermute | solution.py:70
  3.9 51.4 %collective-permute-start.2 = (s32[2,64]{1,0:T(2,128)}, s32[2,64]{1,0:T(2,128)S(1)}, u32[]{:S(2)}, u32[]{:S(2)}) collective-permute-start(s32[2,64]{1,0:T(2,128)} %param.7), channel_id=1, source_target_pairs={{0,2},{1,3},{2,0},{3,1},{4,6},{5,7},{6,4},{7,5},{8,10},{9,11},{10,... | collective-permute-start | bytes 1544 | tf_op jit(solution)/shard_map/ppermute | solution.py:70
  4.5 50.9 %collective-permute-start.3 = (s32[2,64]{1,0:T(2,128)}, s32[2,64]{1,0:T(2,128)S(1)}, u32[]{:S(2)}, u32[]{:S(2)}) collective-permute-start(s32[2,64]{1,0:T(2,128)} %param.7), channel_id=1, source_target_pairs={{0,1},{1,2},{2,3},{3,0},{4,5},{5,6},{6,7},{7,4},{8,9},{9,10},{10,1... | collective-permute-start | bytes 1544 | tf_op jit(solution)/shard_map/ppermute | solution.py:70
  6.2 46.7 %all-to-all-start = ((bf16[32,2,8,256]{3,2,1,0:T(8,128)(2,1)}), bf16[32,2,8,256]{3,2,1,0:T(8,128)(2,1)S(1)}, u32[]{:S(2)}, u32[]{:S(2)}) async-start(bf16[32,2,8,256]{3,2,1,0:T(8,128)(2,1)} %copy.23), calls=%async_computation | async-start | bytes 524288 | tf_op jit(solution)/shard_map/all_to_all | solution.py:116
  38.2 17.2 %copy-start.4 = (s32[2,64]{1,0:T(2,128)S(1)}, s32[2,64]{1,0:T(2,128)}, u32[]{:S(2)}) copy-start(s32[2,64]{1,0:T(2,128)} %param.7) | copy-start | bytes 1540
  53.0 10.8 %copy-start.1 = (bf16[2,1024,1024]{2,1,0:T(8,128)(2,1)S(1)}, bf16[2,1024,1024]{2,1,0:T(8,128)(2,1)}, u32[]{:S(2)}) copy-start(bf16[2,1024,1024]{2,1,0:T(8,128)(2,1)} %param.6) | copy-start | bytes 12582916
  53.0 3.3 %collective-permute-start = (bf16[64,8,256]{2,1,0:T(8,128)(2,1)S(1)}, bf16[64,8,256]{2,1,0:T(8,128)(2,1)S(1)}, u32[]{:S(2)}, u32[]{:S(2)}) collective-permute-start(bf16[64,8,256]{2,1,0:T(8,128)(2,1)S(1)} %bitcast.156), channel_id=1, source_target_pairs={{0,4},{4,8},{8,12},{12,16},{16,20},{20,24},{24,28},{28,32},{32,36}... | collective-permute-start | bytes 786440 | tf_op jit(solution)/shard_map/ppermute | solution.py:118
  56.6 5.7 %collective-permute-start.4 = (bf16[2,16,256]{2,1,0:T(8,128)(2,1)S(1)}, bf16[2,16,256]{2,1,0:T(8,128)(2,1)S(1)}, u32[]{:S(2)}, u32[]{:S(2)}) collective-permute-start(bf16[2,16,256]{2,1,0:T(8,128)(2,1)S(1)} %pad_maximum_fusion.5), channel_id=1, source_target_pairs={{0,1},{1,2},{2,3},{3,0},{4,5},{5,6},{6,7},{7,4},{8,9},{9,10},{10,1... | collective-permute-start | bytes 49160 | tf_op jit(solution)/shard_map/ppermute | solution.py:70
  58.6 5.2 %collective-permute-start.6 = (bf16[2,16,256]{2,1,0:T(8,128)(2,1)S(1)}, bf16[2,16,256]{2,1,0:T(8,128)(2,1)S(1)}, u32[]{:S(2)}, u32[]{:S(2)}) collective-permute-start(bf16[2,16,256]{2,1,0:T(8,128)(2,1)S(1)} %pad_maximum_fusion.7), channel_id=1, source_target_pairs={{0,3},{1,0},{2,1},{3,2},{4,7},{5,4},{6,5},{7,6},{8,11},{9,8},{10,9... | collective-permute-start | bytes 49160 | tf_op jit(solution)/shard_map/ppermute | solution.py:70
  59.9 5.2 %collective-permute-start.5 = (bf16[2,16,256]{2,1,0:T(8,128)(2,1)S(1)}, bf16[2,16,256]{2,1,0:T(8,128)(2,1)S(1)}, u32[]{:S(2)}, u32[]{:S(2)}) collective-permute-start(bf16[2,16,256]{2,1,0:T(8,128)(2,1)S(1)} %pad_maximum_fusion.6), channel_id=1, source_target_pairs={{0,2},{1,3},{2,0},{3,1},{4,6},{5,7},{6,4},{7,5},{8,10},{9,11},{10,... | collective-permute-start | bytes 49160 | tf_op jit(solution)/shard_map/ppermute | solution.py:70
  66.6 3.7 %collective-permute-start.7 = (bf16[2,8,256]{2,1,0:T(8,128)(2,1)S(1)}, bf16[2,8,256]{2,1,0:T(8,128)(2,1)S(1)}, u32[]{:S(2)}, u32[]{:S(2)}) collective-permute-start(bf16[2,8,256]{2,1,0:T(8,128)(2,1)S(1)} %convolution_convert_fusion.7), channel_id=1, source_target_pairs={{0,3},{1,0},{2,1},{3,2},{4,7},{5,4},{6,5},{7,6},{8,11},{9,8},{10,9... | collective-permute-start | bytes 24584 | tf_op jit(solution)/shard_map/ppermute | solution.py:70
  68.0 5.2 %collective-permute-start.8 = (bf16[2,8,256]{2,1,0:T(8,128)(2,1)S(1)}, bf16[2,8,256]{2,1,0:T(8,128)(2,1)S(1)}, u32[]{:S(2)}, u32[]{:S(2)}) collective-permute-start(bf16[2,8,256]{2,1,0:T(8,128)(2,1)S(1)} %convolution_convert_fusion.6), channel_id=1, source_target_pairs={{0,2},{1,3},{2,0},{3,1},{4,6},{5,7},{6,4},{7,5},{8,10},{9,11},{10,... | collective-permute-start | bytes 24584 | tf_op jit(solution)/shard_map/ppermute | solution.py:70
  69.4 4.9 %collective-permute-start.9 = (bf16[2,8,256]{2,1,0:T(8,128)(2,1)S(1)}, bf16[2,8,256]{2,1,0:T(8,128)(2,1)S(1)}, u32[]{:S(2)}, u32[]{:S(2)}) collective-permute-start(bf16[2,8,256]{2,1,0:T(8,128)(2,1)S(1)} %convolution_convert_fusion.5), channel_id=1, source_target_pairs={{0,1},{1,2},{2,3},{3,0},{4,5},{5,6},{6,7},{7,4},{8,9},{9,10},{10,1... | collective-permute-start | bytes 24584 | tf_op jit(solution)/shard_map/ppermute | solution.py:70
  74.3 2.8 %collective-permute-start.10 = (bf16[8,8,256]{2,1,0:T(8,128)(2,1)S(1)}, bf16[8,8,256]{2,1,0:T(8,128)(2,1)S(1)}, u32[]{:S(2)}, u32[]{:S(2)}) collective-permute-start(bf16[8,8,256]{2,1,0:T(8,128)(2,1)S(1)} %pad_maximum_fusion.3), channel_id=1, source_target_pairs={{0,4},{4,8},{8,12},{12,16},{16,20},{20,24},{24,28},{28,32},{32,36}... | collective-permute-start | bytes 98312 | tf_op jit(solution)/shard_map/ppermute | solution.py:167
  75.6 8.3 %collective-permute-start.11 = (bf16[8,8,256]{2,1,0:T(8,128)(2,1)S(1)}, bf16[8,8,256]{2,1,0:T(8,128)(2,1)S(1)}, u32[]{:S(2)}, u32[]{:S(2)}) collective-permute-start(bf16[8,8,256]{2,1,0:T(8,128)(2,1)S(1)} %pad_maximum_fusion.3), channel_id=1, source_target_pairs={{4,0},{8,4},{12,8},{16,12},{20,16},{24,20},{28,24},{32,28},{36,32}... | collective-permute-start | bytes 98312 | tf_op jit(solution)/shard_map/ppermute | solution.py:161
  77.1 13.4 %copy-start.2 = (bf16[2,1024,1024]{2,1,0:T(8,128)(2,1)S(1)}, bf16[2,1024,1024]{2,1,0:T(8,128)(2,1)}, u32[]{:S(2)}) copy-start(bf16[2,1024,1024]{2,1,0:T(8,128)(2,1)} %param.6) | copy-start | bytes 12582916
  84.5 6.5 %collective-permute-start.13 = (bf16[2,16,256]{2,1,0:T(8,128)(2,1)S(1)}, bf16[2,16,256]{2,1,0:T(8,128)(2,1)S(1)}, u32[]{:S(2)}, u32[]{:S(2)}) collective-permute-start(bf16[2,16,256]{2,1,0:T(8,128)(2,1)S(1)} %pad_maximum_fusion.9), channel_id=1, source_target_pairs={{0,2},{1,3},{2,0},{3,1},{4,6},{5,7},{6,4},{7,5},{8,10},{9,11},{10,... | collective-permute-start | bytes 49160 | tf_op jit(solution)/shard_map/ppermute | solution.py:70
  85.5 4.9 %collective-permute-start.12 = (bf16[2,16,256]{2,1,0:T(8,128)(2,1)S(1)}, bf16[2,16,256]{2,1,0:T(8,128)(2,1)S(1)}, u32[]{:S(2)}, u32[]{:S(2)}) collective-permute-start(bf16[2,16,256]{2,1,0:T(8,128)(2,1)S(1)} %pad_maximum_fusion.8), channel_id=1, source_target_pairs={{0,1},{1,2},{2,3},{3,0},{4,5},{5,6},{6,7},{7,4},{8,9},{9,10},{10,1... | collective-permute-start | bytes 49160 | tf_op jit(solution)/shard_map/ppermute | solution.py:70
  86.2 4.6 %collective-permute-start.14 = (bf16[2,16,256]{2,1,0:T(8,128)(2,1)S(1)}, bf16[2,16,256]{2,1,0:T(8,128)(2,1)S(1)}, u32[]{:S(2)}, u32[]{:S(2)}) collective-permute-start(bf16[2,16,256]{2,1,0:T(8,128)(2,1)S(1)} %pad_maximum_fusion.10), channel_id=1, source_target_pairs={{0,3},{1,0},{2,1},{3,2},{4,7},{5,4},{6,5},{7,6},{8,11},{9,8},{10,9... | collective-permute-start | bytes 49160 | tf_op jit(solution)/shard_map/ppermute | solution.py:70
  93.1 4.4 %collective-permute-start.15 = (bf16[2,8,256]{2,1,0:T(8,128)(2,1)S(1)}, bf16[2,8,256]{2,1,0:T(8,128)(2,1)S(1)}, u32[]{:S(2)}, u32[]{:S(2)}) collective-permute-start(bf16[2,8,256]{2,1,0:T(8,128)(2,1)S(1)} %convolution_convert_fusion.3), channel_id=1, source_target_pairs={{0,3},{1,0},{2,1},{3,2},{4,7},{5,4},{6,5},{7,6},{8,11},{9,8},{10,9... | collective-permute-start | bytes 24584 | tf_op jit(solution)/shard_map/ppermute | solution.py:70
  96.1 5.2 %collective-permute-start.16 = (bf16[2,8,256]{2,1,0:T(8,128)(2,1)S(1)}, bf16[2,8,256]{2,1,0:T(8,128)(2,1)S(1)}, u32[]{:S(2)}, u32[]{:S(2)}) collective-permute-start(bf16[2,8,256]{2,1,0:T(8,128)(2,1)S(1)} %convolution_convert_fusion.2), channel_id=1, source_target_pairs={{0,2},{1,3},{2,0},{3,1},{4,6},{5,7},{6,4},{7,5},{8,10},{9,11},{10,... | collective-permute-start | bytes 24584 | tf_op jit(solution)/shard_map/ppermute | solution.py:70
  96.3 5.0 %collective-permute-start.17 = (bf16[2,8,256]{2,1,0:T(8,128)(2,1)S(1)}, bf16[2,8,256]{2,1,0:T(8,128)(2,1)S(1)}, u32[]{:S(2)}, u32[]{:S(2)}) collective-permute-start(bf16[2,8,256]{2,1,0:T(8,128)(2,1)S(1)} %convolution_convert_fusion.1), channel_id=1, source_target_pairs={{0,1},{1,2},{2,3},{3,0},{4,5},{5,6},{6,7},{7,4},{8,9},{9,10},{10,1... | collective-permute-start | bytes 24584 | tf_op jit(solution)/shard_map/ppermute | solution.py:70
  101.2 3.1 %collective-permute-start.18 = (bf16[8,8,256]{2,1,0:T(8,128)(2,1)S(1)}, bf16[8,8,256]{2,1,0:T(8,128)(2,1)S(1)}, u32[]{:S(2)}, u32[]{:S(2)}) collective-permute-start(bf16[8,8,256]{2,1,0:T(8,128)(2,1)S(1)} %pad_maximum_fusion.4), channel_id=1, source_target_pairs={{4,0},{8,4},{12,8},{16,12},{20,16},{24,20},{28,24},{32,28},{36,32}... | collective-permute-start | bytes 98312 | tf_op jit(solution)/shard_map/ppermute | solution.py:161
  137.9 20.5 %collective-permute-start.20 = (bf16[2,256,256]{2,1,0:T(8,128)(2,1)S(1)}, bf16[2,256,256]{2,1,0:T(8,128)(2,1)S(1)}, u32[]{:S(2)}, u32[]{:S(2)}) collective-permute-start(bf16[2,256,256]{2,1,0:T(8,128)(2,1)S(1)} %copy_bitcast_fusion), channel_id=1, source_target_pairs={{0,1},{1,2},{2,3},{3,0},{4,5},{5,6},{6,7},{7,4},{8,9},{9,10},{10,1... | collective-permute-start | bytes 786440 | tf_op jit(solution)/shard_map/ppermute | solution.py:185
  138.0 20.5 %collective-permute-start.19 = (bf16[2,256,256]{2,1,0:T(8,128)(2,1)S(1)}, bf16[2,256,256]{2,1,0:T(8,128)(2,1)S(1)}, u32[]{:S(2)}, u32[]{:S(2)}) collective-permute-start(bf16[2,256,256]{2,1,0:T(8,128)(2,1)S(1)} %copy_bitcast_fusion), channel_id=1, source_target_pairs={{1,0},{2,1},{3,2},{0,3},{5,4},{6,5},{7,6},{4,7},{9,8},{10,9},{11,1... | collective-permute-start | bytes 786440 | tf_op jit(solution)/shard_map/ppermute | solution.py:186
  141.2 1.2 collective-permute-start.23
  142.4 3.6 %collective-permute-start.24 = (f32[2]{0:T(128)S(1)}, f32[2]{0:T(128)S(1)}, u32[]{:S(2)}, u32[]{:S(2)}) collective-permute-start(f32[2]{0:T(128)S(1)} %add.221), channel_id=1, source_target_pairs={{0,8},{4,12},{8,0},{12,4},{16,24},{20,28},{24,16},{28,20},{32,40},... | collective-permute-start | bytes 32 | tf_op jit(solution)/shard_map/ppermute | solution.py:179
  146.0 4.5 %collective-permute-start.25 = (f32[2]{0:T(128)S(1)}, f32[2]{0:T(128)S(1)}, u32[]{:S(2)}, u32[]{:S(2)}) collective-permute-start(f32[2]{0:T(128)S(1)} %add.222), channel_id=1, source_target_pairs={{0,16},{4,20},{8,24},{12,28},{16,0},{20,4},{24,8},{28,12},{32,48},... | collective-permute-start | bytes 32 | tf_op jit(solution)/shard_map/ppermute | solution.py:179
  150.4 7.5 %collective-permute-start.26 = (f32[2]{0:T(128)S(1)}, f32[2]{0:T(128)S(1)}, u32[]{:S(2)}, u32[]{:S(2)}) collective-permute-start(f32[2]{0:T(128)S(1)} %add.223), channel_id=1, source_target_pairs={{0,32},{4,36},{8,40},{12,44},{16,48},{20,52},{24,56},{28,60},{32,0... | collective-permute-start | bytes 32 | tf_op jit(solution)/shard_map/ppermute | solution.py:179
  157.9 12.3 %collective-permute-start.27 = (f32[2]{0:T(128)S(1)}, f32[2]{0:T(128)S(1)}, u32[]{:S(2)}, u32[]{:S(2)}) collective-permute-start(f32[2]{0:T(128)S(1)} %add.224), channel_id=1, source_target_pairs={{0,64},{4,68},{8,72},{12,76},{16,80},{20,84},{24,88},{28,92},{32,9... | collective-permute-start | bytes 32 | tf_op jit(solution)/shard_map/ppermute | solution.py:179
  158.3 12.4 %collective-permute-start.21 = (bf16[1,256,256]{2,1,0:T(8,128)(2,1)S(1)}, bf16[1,256,256]{2,1,0:T(8,128)(2,1)S(1)}, u32[]{:S(2)}, u32[]{:S(2)}) collective-permute-start(bf16[1,256,256]{2,1,0:T(8,128)(2,1)S(1)} %slice.266), channel_id=1, source_target_pairs={{0,1},{1,2},{2,3},{3,0},{4,5},{5,6},{6,7},{7,4},{8,9},{9,10},{10,1... | collective-permute-start | bytes 393224 | tf_op jit(solution)/shard_map/ppermute | solution.py:187
  158.5 12.2 %collective-permute-start.22 = (bf16[1,256,256]{2,1,0:T(8,128)(2,1)S(1)}, bf16[1,256,256]{2,1,0:T(8,128)(2,1)S(1)}, u32[]{:S(2)}, u32[]{:S(2)}) collective-permute-start(bf16[1,256,256]{2,1,0:T(8,128)(2,1)S(1)} %slice.267), channel_id=1, source_target_pairs={{1,0},{2,1},{3,2},{0,3},{5,4},{6,5},{7,6},{4,7},{9,8},{10,9},{11,1... | collective-permute-start | bytes 393224 | tf_op jit(solution)/shard_map/ppermute | solution.py:187

commit v5 on v4

--- a/solution.py
+++ b/solution.py
@@ -12,36 +12,43 @@
 
 def moments(length):
     waves = [2.0 * math.pi * k / length for k in range(-(length // 2), length // 2)]
-    return [sum(w**p for w in waves) / length for p in (2, 4, 6, 8)]
+    return [sum(w**p for w in waves) / length for p in range(2, 16, 2)]
+
+
+def series(square, terms):
+    total = terms[-1]
+    for term in terms[-2::-1]:
+        total = term - square * total
+    return total
 
 
 def interpolation_kernels(shifts, taps, length):
     whole = jnp.round(shifts)
-    part = shifts - whole
-    odd_shift = 1.0 - 2.0 * (whole.astype(jnp.int32) & 1).astype(jnp.float32)
+    part = (shifts - whole)[:, None, None]
+    whole = whole.astype(jnp.int32)[:, None, None]
+    odd_shift = 1.0 - 2.0 * (whole & 1).astype(jnp.float32)
     sine = odd_shift * jnp.sin(math.pi * part)
     cosine = odd_shift * jnp.cos(math.pi * part)
-    v = lax.broadcasted_iota(jnp.int32, (1, taps, length), 1)
-    u = lax.broadcasted_iota(jnp.int32, (1, taps, length), 2)
-    lag = u - v
-    lag = jnp.where(lag >= length // 2, lag - length, jnp.where(lag < -(length // 2), lag + length, lag))
-    sign = 1.0 - 2.0 * (lag & 1).astype(jnp.float32)
-    d = (lag - whole.astype(jnp.int32)[:, None, None]).astype(jnp.float32) - part[:, None, None]
-    near = jnp.abs(d) < 0.1
-    safe = jnp.where(near, 1.0, d)
-    y = safe * (math.pi / length)
-    sin_y = jnp.sin(y)
-    cos_y = jnp.cos(y)
-    inv = 1.0 / sin_y
+    step = math.pi / length
+    v = lax.broadcasted_iota(jnp.int32, (1, taps, 1), 1) - taps // 2
+    u = lax.broadcasted_iota(jnp.int32, (1, 1, length), 2) - taps // 2
+    u = jnp.where(u >= length // 2, u - length, u)
+    sign = (1.0 - 2.0 * (v & 1).astype(jnp.float32)) * (1.0 - 2.0 * (u & 1).astype(jnp.float32))
+    ahead = ((u - whole).astype(jnp.float32) - part) * step
+    behind = v.astype(jnp.float32) * step
+    sin_u, cos_u, sin_v, cos_v = jnp.sin(ahead), jnp.cos(ahead), jnp.sin(behind), jnp.cos(behind)
+    sin_y = sin_u * cos_v - cos_u * sin_v
+    cos_y = cos_u * cos_v + sin_u * sin_v
+    d = (u - v - whole).astype(jnp.float32) - part
+    near = jnp.abs(d) <= 0.5
+    inv = 1.0 / jnp.where(near, 1.0, sin_y)
     cot = cos_y * inv
-    sin_d = -sign * sine[:, None, None]
-    cos_d = sign * cosine[:, None, None]
+    sin_d = -sign * sine
     far_h = sin_d * cot * (1.0 / length)
-    far_q = (math.pi / length) * (sin_d * inv * inv * (1.0 / length) - cos_d * cot)
-    m2, m4, m6, m8 = moments(length)
-    s = d * d
-    near_h = 1.0 - s * (m2 / 2 - s * (m4 / 24 - s * (m6 / 720 - s * (m8 / 40320))))
-    near_q = d * (m2 - s * (m4 / 6 - s * (m6 / 120 - s * (m8 / 5040))))
+    far_q = step * (sin_d * (inv * inv) * (1.0 / length) - sign * cosine * cot)
+    rates = moments(length)
+    near_h = series(d * d, [1.0] + [m / math.factorial(2 * k + 2) for k, m in enumerate(rates)])
+    near_q = d * series(d * d, [m / math.factorial(2 * k + 1) for k, m in enumerate(rates)])
     return jnp.where(near, near_h, far_h), jnp.where(near, near_q, far_q)
 
 
@@ -173,11 +180,9 @@
     home = current.reshape(slabs, slices_here, band, chunk)
     home = lax.all_to_all(home, SLAB, 0, 0, tiled=True)
     home = home.transpose(1, 0, 2, 3).reshape(slices_here, rows_all, chunk)
-    dots = jnp.sum(projection * slope_field, axis=(1, 2))
-    bit = 1
-    while bit < slabs:
-        dots = dots + lax.ppermute(dots, SLAB, [(i, i ^ bit) for i in range(slabs)])
-        bit *= 2
+    dots = jnp.broadcast_to(jnp.sum(projection * slope_field, axis=(1, 2)), (slabs, angles_here))
+    dots = lax.all_to_all(dots, SLAB, 0, 0, tiled=True)
+    dots = jnp.sum(dots, axis=0)
     shift_slope = dots * (1.0 / math.sqrt(rows_all * columns))
     ahead = [(i, (i + 1) % angs) for i in range(angs)]
     behind = [((i + 1) % angs, i) for i in range(angs)]

time: 173 us -> 167 us (0.965)
  waiting for transfers between devices: 56.6 us -> 48.6 us
  starting transfers between devices: 58.7 us -> 62.6 us
  other arithmetic: 8.65 us -> 5.97 us
    ppermute x5 -> x0, waiting for transfers between devices: 24.8 us -> none  [per_device(): dots = dots + lax.ppermute(dots, SLAB, [(i, i ^ bit) for i in range(slabs)])]
    all_to_all x0 -> x1, waiting for transfers between devices: none -> 11.7 us  [per_device(): dots = lax.all_to_all(dots, SLAB, 0, 0, tiled=True)]
    all_to_all x0 -> x1, starting transfers between devices: none -> 4.74 us  [per_device(): dots = lax.all_to_all(dots, SLAB, 0, 0, tiled=True)]
    select_n x1, other arithmetic: 4.93 us -> 1.91 us  [interpolation_kernels(): return (jnp.where(near, near_h, far_h), jnp.where(near, near_q, far_q))]
    all_to_all x1, waiting for transfers between devices: 13 us -> 15.7 us  [per_device(): own = lax.all_to_all(mine, SLAB, 0, 0, tiled=True)]
    ppermute x1, waiting for transfers between devices: 0.01 us -> 2.38 us  [per_device(): lax.ppermute(lower[:half], 'ang', ahead)]
  transfers between devices with their start and end apart: 29 -> 25, of which waited for: 15 -> 12; matrix products, arithmetic and copies ran while one was open for 9% -> 9% of each run, Pallas kernels for 0% -> 0%
where the time goes in v5:
time: 167 us; the launch traced here: 166 us
  starting transfers between devices  62.6 us (37%)
  waiting for transfers between devices  48.6 us (29%)
  blocking collectives  32.2 us (19%)
  matrix products  12.3 us (7%)
  other arithmetic  5.97 us (4%)
  local copies, waits for them, and re-layouts  3.13 us (2%)
    all_to_all x1, blocking collectives, per_device(): home = lax.all_to_all(home, SLAB, 0, 0, tiled=True)  32.2 us
    all_to_all x1, starting transfers between devices, per_device(): own = lax.all_to_all(mine, SLAB, 0, 0, tiled=True)  24.7 us
    ppermute x15, starting transfers between devices, from_ang(): lax.ppermute(blocks[k], 'ang', [(i, (i + k * step) % size) for i in range...  20.3 us
    all_to_all x1, waiting for transfers between devices, per_device(): own = lax.all_to_all(mine, SLAB, 0, 0, tiled=True)  15.7 us
    all_to_all x1, waiting for transfers between devices, per_device(): dots = lax.all_to_all(dots, SLAB, 0, 0, tiled=True)  11.7 us
    ppermute x15, waiting for transfers between devices, from_ang(): lax.ppermute(blocks[k], 'ang', [(i, (i + k * step) % size) for i in range...  9.47 us
    ppermute x2, waiting for transfers between devices, per_device(): below = lax.ppermute(back, SLAB, up_ring)  8.48 us
    dot_general x8, matrix products, per_device(): jnp.einsum('arx,axu->aru', x, w, preferred_element_type=f32)  5.7 us
  transfers between devices with their start and end apart: 25, of which 12 were waited for; matrix products, arithmetic and copies ran while one was open for 9% of the time, Pallas kernels for 0%

profile of v5, /device:TPU:40, one launch (start us, length us, event | category | flops | bytes accessed | tf_op | source)
XLA Modules:
  0.0 166.2 jit_solution(15120485976999308681)
XLA Ops:
  0.7 3.3 %collective-permute-start.1 = (s32[2,64]{1,0:T(2,128)}, s32[2,64]{1,0:T(2,128)S(1)}, u32[]{:S(2)}, u32[]{:S(2)}) collective-permute-start(s32[2,64]{1,0:T(2,128)} %param.7), channel_id=1, source_target_pairs={{0,3},{1,0},{2,1},{3,2},{4,7},{5,4},{6,5},{7,6},{8,11},{9,8},{10,9... | collective-permute-start | bytes 1544 | tf_op jit(solution)/shard_map/ppermute | solution.py:77
  3.9 0.5 collective-permute-start.2
  4.5 1.0 collective-permute-start.3
  5.5 0.7 copy.49
  6.2 24.7 %all-to-all-start = ((bf16[32,2,8,256]{3,2,1,0:T(8,128)(2,1)}), bf16[32,2,8,256]{3,2,1,0:T(8,128)(2,1)S(1)}, u32[]{:S(2)}, u32[]{:S(2)}) async-start(bf16[32,2,8,256]{3,2,1,0:T(8,128)(2,1)} %copy.49), calls=%async_computation | async-start | bytes 524288 | tf_op jit(solution)/shard_map/all_to_all | solution.py:123
  31.1 0.7 sine_multiply_fusion
  32.3 1.9 %fusion.11 = (f32[2,128,1024]{2,1,0:T(8,128)S(1)}, f32[2,128,1024]{2,1,0:T(8,128)S(1)}) fusion(f32[128]{0:T(128)S(1)} %get-tuple-element.54, f32[2,1024]{1,0:T(2,128)S(1)} %get-tuple-element.43, f32[128]{0:T(128)S(1)} %get-tuple-element.55, f32[2,1024]{1,0:T(2,128)S(1)} %get-tuple-element.42, f32[2]{0:T(128)S(1)} %get-tuple-element.46, ...), kind=kLoop, calls=%fused_computation.30 | loop fusion | flops 14155776 | bytes 3687456 | tf_op jit(solution)/shard_map/jit(_where)/select_n | solution.py:52
  34.2 1.3 convolution_bitcast_fusion
  35.5 0.9 reshape.514
  37.3 15.7 %all-to-all-done = bf16[32,2,8,256]{3,2,1,0:T(8,128)(2,1)S(1)} async-done(((bf16[32,2,8,256]{3,2,1,0:T(8,128)(2,1)}), bf16[32,2,8,256]{3,2,1,0:T(8,128)(2,1)S(1)}, u32[]{:S(2)}, u32[]{:S(2)}) %all-to-all-start) | async-done | bytes 262176 | tf_op jit(solution)/shard_map/all_to_all | solution.py:123
  53.0 2.1 %collective-permute-start = (bf16[64,8,256]{2,1,0:T(8,128)(2,1)S(1)}, bf16[64,8,256]{2,1,0:T(8,128)(2,1)S(1)}, u32[]{:S(2)}, u32[]{:S(2)}) collective-permute-start(bf16[64,8,256]{2,1,0:T(8,128)(2,1)S(1)} %bitcast.156), channel_id=1, source_target_pairs={{0,4},{4,8},{8,12},{12,16},{16,20},{20,24},{24,28},{28,32},{32,36}... | collective-permute-start | bytes 786440 | tf_op jit(solution)/shard_map/ppermute | solution.py:125
  55.4 0.9 collective-permute-done
  56.6 2.1 %collective-permute-start.4 = (bf16[2,16,256]{2,1,0:T(8,128)(2,1)S(1)}, bf16[2,16,256]{2,1,0:T(8,128)(2,1)S(1)}, u32[]{:S(2)}, u32[]{:S(2)}) collective-permute-start(bf16[2,16,256]{2,1,0:T(8,128)(2,1)S(1)} %pad_maximum_fusion.5), channel_id=1, source_target_pairs={{0,1},{1,2},{2,3},{3,0},{4,5},{5,6},{6,7},{7,4},{8,9},{9,10},{10,1... | collective-permute-start | bytes 49160 | tf_op jit(solution)/shard_map/ppermute | solution.py:77
  58.6 1.3 collective-permute-start.6
  59.9 0.9 collective-permute-start.5
  60.8 1.5 fusion.48
  62.3 1.5 convolution_add_fusion.3
  64.1 1.1 collective-permute-done.5
  65.8 0.4 convolution_convert_fusion.6
  66.2 0.4 convolution_convert_fusion.5
  66.6 1.4 collective-permute-start.7
  68.0 1.4 collective-permute-start.8
  70.3 2.9 %collective-permute-done.8 = bf16[2,8,256]{2,1,0:T(8,128)(2,1)S(1)} collective-permute-done((bf16[2,8,256]{2,1,0:T(8,128)(2,1)S(1)}, bf16[2,8,256]{2,1,0:T(8,128)(2,1)S(1)}, u32[]{:S(2)}, u32[]{:S(2)}) %collective-permute-start.8) | collective-permute-done | bytes 8224 | tf_op jit(solution)/shard_map/ppermute | solution.py:77
  73.2 1.1 collective-permute-done.9
  74.3 1.3 collective-permute-start.10
  75.6 1.3 collective-permute-start.11
  77.1 6.8 %collective-permute-done.11 = bf16[8,8,256]{2,1,0:T(8,128)(2,1)S(1)} collective-permute-done((bf16[8,8,256]{2,1,0:T(8,128)(2,1)S(1)}, bf16[8,8,256]{2,1,0:T(8,128)(2,1)S(1)}, u32[]{:S(2)}, u32[]{:S(2)}) %collective-permute-start.11) | collective-permute-done | bytes 32800 | tf_op jit(solution)/shard_map/ppermute | solution.py:168
  84.5 1.0 collective-permute-start.13
  85.5 0.6 collective-permute-start.12
  86.2 2.6 %collective-permute-start.14 = (bf16[2,16,256]{2,1,0:T(8,128)(2,1)S(1)}, bf16[2,16,256]{2,1,0:T(8,128)(2,1)S(1)}, u32[]{:S(2)}, u32[]{:S(2)}) collective-permute-start(bf16[2,16,256]{2,1,0:T(8,128)(2,1)S(1)} %pad_maximum_fusion.10), channel_id=1, source_target_pairs={{0,3},{1,0},{2,1},{3,2},{4,7},{5,4},{6,5},{7,6},{8,11},{9,8},{10,9... | collective-permute-start | bytes 49160 | tf_op jit(solution)/shard_map/ppermute | solution.py:77
  88.8 1.5 fusion.45
  91.3 0.7 fusion.127
  92.3 0.4 convolution_convert_fusion.2
  93.1 3.0 %collective-permute-start.15 = (bf16[2,8,256]{2,1,0:T(8,128)(2,1)S(1)}, bf16[2,8,256]{2,1,0:T(8,128)(2,1)S(1)}, u32[]{:S(2)}, u32[]{:S(2)}) collective-permute-start(bf16[2,8,256]{2,1,0:T(8,128)(2,1)S(1)} %convolution_convert_fusion.3), channel_id=1, source_target_pairs={{0,3},{1,0},{2,1},{3,2},{4,7},{5,4},{6,5},{7,6},{8,11},{9,8},{10,9... | collective-permute-start | bytes 24584 | tf_op jit(solution)/shard_map/ppermute | solution.py:77
  96.3 0.8 collective-permute-start.17
  97.4 3.8 %collective-permute-done.16 = bf16[2,8,256]{2,1,0:T(8,128)(2,1)S(1)} collective-permute-done((bf16[2,8,256]{2,1,0:T(8,128)(2,1)S(1)}, bf16[2,8,256]{2,1,0:T(8,128)(2,1)S(1)}, u32[]{:S(2)}, u32[]{:S(2)}) %collective-permute-start.16) | collective-permute-done | bytes 8224 | tf_op jit(solution)/shard_map/ppermute | solution.py:77
  101.2 1.3 collective-permute-start.18
  102.6 1.7 %collective-permute-done.18 = bf16[8,8,256]{2,1,0:T(8,128)(2,1)S(1)} collective-permute-done((bf16[8,8,256]{2,1,0:T(8,128)(2,1)S(1)}, bf16[8,8,256]{2,1,0:T(8,128)(2,1)S(1)}, u32[]{:S(2)}, u32[]{:S(2)}) %collective-permute-start.18) | collective-permute-done | bytes 32800 | tf_op jit(solution)/shard_map/ppermute | solution.py:168
  104.4 1.3 fusion.7
  105.7 32.2 %all_to_all.16 = bf16[32,2,8,256]{3,2,1,0:T(8,128)(2,1)S(1)} all-to-all(bf16[32,2,8,256]{3,2,1,0:T(8,128)(2,1)S(1)} %bitcast.174), channel_id=1, replica_groups=mesh['grp'=2,'slab'=32,'ang'=4] {'slab'}, dimensions={0} | all-to-all | bytes 524288 | tf_op jit(solution)/shard_map/all_to_all | solution.py:181
  138.0 3.2 %collective-permute-start.19 = (bf16[2,256,256]{2,1,0:T(8,128)(2,1)S(1)}, bf16[2,256,256]{2,1,0:T(8,128)(2,1)S(1)}, u32[]{:S(2)}, u32[]{:S(2)}) collective-permute-start(bf16[2,256,256]{2,1,0:T(8,128)(2,1)S(1)} %copy_bitcast_fusion), channel_id=1, source_target_pairs={{1,0},{2,1},{3,2},{0,3},{5,4},{6,5},{7,6},{4,7},{9,8},{10,9},{11,1... | collective-permute-start | bytes 786440 | tf_op jit(solution)/shard_map/ppermute | solution.py:191
  141.2 0.6 broadcast_in_dim.4
  141.8 4.7 %all-to-all-start.2 = ((f32[32,1,2]{2,1,0:T(1,128)}), f32[32,1,2]{2,1,0:T(1,128)S(1)}, u32[]{:S(2)}, u32[]{:S(2)}) async-start(f32[32,1,2]{2,1,0:T(1,128)} %broadcast_in_dim.4), calls=%async_computation.2 | async-start | bytes 32768 | tf_op jit(solution)/shard_map/all_to_all | solution.py:184
  146.6 11.7 %all-to-all-done.2 = f32[32,1,2]{2,1,0:T(1,128)S(1)} async-done(((f32[32,1,2]{2,1,0:T(1,128)}), f32[32,1,2]{2,1,0:T(1,128)S(1)}, u32[]{:S(2)}, u32[]{:S(2)}) %all-to-all-start.2) | async-done | bytes 288 | tf_op jit(solution)/shard_map/all_to_all | solution.py:184
  158.5 3.3 %collective-permute-start.22 = (bf16[1,256,256]{2,1,0:T(8,128)(2,1)S(1)}, bf16[1,256,256]{2,1,0:T(8,128)(2,1)S(1)}, u32[]{:S(2)}, u32[]{:S(2)}) collective-permute-start(bf16[1,256,256]{2,1,0:T(8,128)(2,1)S(1)} %slice.267), channel_id=1, source_target_pairs={{1,0},{2,1},{3,2},{0,3},{5,4},{6,5},{7,6},{4,7},{9,8},{10,9},{11,1... | collective-permute-start | bytes 393224 | tf_op jit(solution)/shard_map/ppermute | solution.py:192
  161.8 0.5 broadcast_multiply_fusion.1
  162.3 2.4 %collective-permute-done.21 = bf16[1,256,256]{2,1,0:T(8,128)(2,1)S(1)} collective-permute-done((bf16[1,256,256]{2,1,0:T(8,128)(2,1)S(1)}, bf16[1,256,256]{2,1,0:T(8,128)(2,1)S(1)}, u32[]{:S(2)}, u32[]{:S(2)}) %collective-permute-start.21) | collective-permute-done | bytes 131104 | tf_op jit(solution)/shard_map/ppermute | solution.py:192
  165.1 1.1 pad_maximum_fusion
  (106 shorter events, 7.3 us)
Async XLA Ops:
  0.6 4.9 %copy-start = (bf16[2,256,1024]{2,1,0:T(8,128)(2,1)S(1)}, bf16[2,256,1024]{2,1,0:T(8,128)(2,1)}, u32[]{:S(2)}) copy-start(bf16[2,256,1024]{2,1,0:T(8,128)(2,1)} %param.5) | copy-start | bytes 3145732
  0.6 33.5 %copy-start.3 = (f32[2,8,1024]{2,1,0:T(8,128)S(1)}, f32[2,8,1024]{2,1,0:T(8,128)}, u32[]{:S(2)}) copy-start(f32[2,8,1024]{2,1,0:T(8,128)} %param.8) | copy-start | bytes 196612
  0.7 54.5 %collective-permute-start.1 = (s32[2,64]{1,0:T(2,128)}, s32[2,64]{1,0:T(2,128)S(1)}, u32[]{:S(2)}, u32[]{:S(2)}) collective-permute-start(s32[2,64]{1,0:T(2,128)} %param.7), channel_id=1, source_target_pairs={{0,3},{1,0},{2,1},{3,2},{4,7},{5,4},{6,5},{7,6},{8,11},{9,8},{10,9... | collective-permute-start | bytes 1544 | tf_op jit(solution)/shard_map/ppermute | solution.py:77
  3.9 51.2 %collective-permute-start.2 = (s32[2,64]{1,0:T(2,128)}, s32[2,64]{1,0:T(2,128)S(1)}, u32[]{:S(2)}, u32[]{:S(2)}) collective-permute-start(s32[2,64]{1,0:T(2,128)} %param.7), channel_id=1, source_target_pairs={{0,2},{1,3},{2,0},{3,1},{4,6},{5,7},{6,4},{7,5},{8,10},{9,11},{10,... | collective-permute-start | bytes 1544 | tf_op jit(solution)/shard_map/ppermute | solution.py:77
  4.5 50.7 %collective-permute-start.3 = (s32[2,64]{1,0:T(2,128)}, s32[2,64]{1,0:T(2,128)S(1)}, u32[]{:S(2)}, u32[]{:S(2)}) collective-permute-start(s32[2,64]{1,0:T(2,128)} %param.7), channel_id=1, source_target_pairs={{0,1},{1,2},{2,3},{3,0},{4,5},{5,6},{6,7},{7,4},{8,9},{9,10},{10,1... | collective-permute-start | bytes 1544 | tf_op jit(solution)/shard_map/ppermute | solution.py:77
  6.2 46.7 %all-to-all-start = ((bf16[32,2,8,256]{3,2,1,0:T(8,128)(2,1)}), bf16[32,2,8,256]{3,2,1,0:T(8,128)(2,1)S(1)}, u32[]{:S(2)}, u32[]{:S(2)}) async-start(bf16[32,2,8,256]{3,2,1,0:T(8,128)(2,1)} %copy.49), calls=%async_computation | async-start | bytes 524288 | tf_op jit(solution)/shard_map/all_to_all | solution.py:123
  35.5 19.7 %copy-start.4 = (s32[2,64]{1,0:T(2,128)S(1)}, s32[2,64]{1,0:T(2,128)}, u32[]{:S(2)}) copy-start(s32[2,64]{1,0:T(2,128)} %param.7) | copy-start | bytes 1540
  53.0 10.8 %copy-start.1 = (bf16[2,1024,1024]{2,1,0:T(8,128)(2,1)S(1)}, bf16[2,1024,1024]{2,1,0:T(8,128)(2,1)}, u32[]{:S(2)}) copy-start(bf16[2,1024,1024]{2,1,0:T(8,128)(2,1)} %param.6) | copy-start | bytes 12582916
  53.0 3.3 %collective-permute-start = (bf16[64,8,256]{2,1,0:T(8,128)(2,1)S(1)}, bf16[64,8,256]{2,1,0:T(8,128)(2,1)S(1)}, u32[]{:S(2)}, u32[]{:S(2)}) collective-permute-start(bf16[64,8,256]{2,1,0:T(8,128)(2,1)S(1)} %bitcast.156), channel_id=1, source_target_pairs={{0,4},{4,8},{8,12},{12,16},{16,20},{20,24},{24,28},{28,32},{32,36}... | collective-permute-start | bytes 786440 | tf_op jit(solution)/shard_map/ppermute | solution.py:125
  56.6 5.7 %collective-permute-start.4 = (bf16[2,16,256]{2,1,0:T(8,128)(2,1)S(1)}, bf16[2,16,256]{2,1,0:T(8,128)(2,1)S(1)}, u32[]{:S(2)}, u32[]{:S(2)}) collective-permute-start(bf16[2,16,256]{2,1,0:T(8,128)(2,1)S(1)} %pad_maximum_fusion.5), channel_id=1, source_target_pairs={{0,1},{1,2},{2,3},{3,0},{4,5},{5,6},{6,7},{7,4},{8,9},{9,10},{10,1... | collective-permute-start | bytes 49160 | tf_op jit(solution)/shard_map/ppermute | solution.py:77
  58.6 5.2 %collective-permute-start.6 = (bf16[2,16,256]{2,1,0:T(8,128)(2,1)S(1)}, bf16[2,16,256]{2,1,0:T(8,128)(2,1)S(1)}, u32[]{:S(2)}, u32[]{:S(2)}) collective-permute-start(bf16[2,16,256]{2,1,0:T(8,128)(2,1)S(1)} %pad_maximum_fusion.7), channel_id=1, source_target_pairs={{0,3},{1,0},{2,1},{3,2},{4,7},{5,4},{6,5},{7,6},{8,11},{9,8},{10,9... | collective-permute-start | bytes 49160 | tf_op jit(solution)/shard_map/ppermute | solution.py:77
  59.9 5.2 %collective-permute-start.5 = (bf16[2,16,256]{2,1,0:T(8,128)(2,1)S(1)}, bf16[2,16,256]{2,1,0:T(8,128)(2,1)S(1)}, u32[]{:S(2)}, u32[]{:S(2)}) collective-permute-start(bf16[2,16,256]{2,1,0:T(8,128)(2,1)S(1)} %pad_maximum_fusion.6), channel_id=1, source_target_pairs={{0,2},{1,3},{2,0},{3,1},{4,6},{5,7},{6,4},{7,5},{8,10},{9,11},{10,... | collective-permute-start | bytes 49160 | tf_op jit(solution)/shard_map/ppermute | solution.py:77
  66.6 3.7 %collective-permute-start.7 = (bf16[2,8,256]{2,1,0:T(8,128)(2,1)S(1)}, bf16[2,8,256]{2,1,0:T(8,128)(2,1)S(1)}, u32[]{:S(2)}, u32[]{:S(2)}) collective-permute-start(bf16[2,8,256]{2,1,0:T(8,128)(2,1)S(1)} %convolution_convert_fusion.7), channel_id=1, source_target_pairs={{0,3},{1,0},{2,1},{3,2},{4,7},{5,4},{6,5},{7,6},{8,11},{9,8},{10,9... | collective-permute-start | bytes 24584 | tf_op jit(solution)/shard_map/ppermute | solution.py:77
  68.0 5.2 %collective-permute-start.8 = (bf16[2,8,256]{2,1,0:T(8,128)(2,1)S(1)}, bf16[2,8,256]{2,1,0:T(8,128)(2,1)S(1)}, u32[]{:S(2)}, u32[]{:S(2)}) collective-permute-start(bf16[2,8,256]{2,1,0:T(8,128)(2,1)S(1)} %convolution_convert_fusion.6), channel_id=1, source_target_pairs={{0,2},{1,3},{2,0},{3,1},{4,6},{5,7},{6,4},{7,5},{8,10},{9,11},{10,... | collective-permute-start | bytes 24584 | tf_op jit(solution)/shard_map/ppermute | solution.py:77
  69.4 4.9 %collective-permute-start.9 = (bf16[2,8,256]{2,1,0:T(8,128)(2,1)S(1)}, bf16[2,8,256]{2,1,0:T(8,128)(2,1)S(1)}, u32[]{:S(2)}, u32[]{:S(2)}) collective-permute-start(bf16[2,8,256]{2,1,0:T(8,128)(2,1)S(1)} %convolution_convert_fusion.5), channel_id=1, source_target_pairs={{0,1},{1,2},{2,3},{3,0},{4,5},{5,6},{6,7},{7,4},{8,9},{9,10},{10,1... | collective-permute-start | bytes 24584 | tf_op jit(solution)/shard_map/ppermute | solution.py:77
  74.3 2.8 %collective-permute-start.10 = (bf16[8,8,256]{2,1,0:T(8,128)(2,1)S(1)}, bf16[8,8,256]{2,1,0:T(8,128)(2,1)S(1)}, u32[]{:S(2)}, u32[]{:S(2)}) collective-permute-start(bf16[8,8,256]{2,1,0:T(8,128)(2,1)S(1)} %pad_maximum_fusion.3), channel_id=1, source_target_pairs={{0,4},{4,8},{8,12},{12,16},{16,20},{20,24},{24,28},{28,32},{32,36}... | collective-permute-start | bytes 98312 | tf_op jit(solution)/shard_map/ppermute | solution.py:174
  75.6 8.3 %collective-permute-start.11 = (bf16[8,8,256]{2,1,0:T(8,128)(2,1)S(1)}, bf16[8,8,256]{2,1,0:T(8,128)(2,1)S(1)}, u32[]{:S(2)}, u32[]{:S(2)}) collective-permute-start(bf16[8,8,256]{2,1,0:T(8,128)(2,1)S(1)} %pad_maximum_fusion.3), channel_id=1, source_target_pairs={{4,0},{8,4},{12,8},{16,12},{20,16},{24,20},{28,24},{32,28},{36,32}... | collective-permute-start | bytes 98312 | tf_op jit(solution)/shard_map/ppermute | solution.py:168
  77.1 13.4 %copy-start.2 = (bf16[2,1024,1024]{2,1,0:T(8,128)(2,1)S(1)}, bf16[2,1024,1024]{2,1,0:T(8,128)(2,1)}, u32[]{:S(2)}) copy-start(bf16[2,1024,1024]{2,1,0:T(8,128)(2,1)} %param.6) | copy-start | bytes 12582916
  84.5 6.5 %collective-permute-start.13 = (bf16[2,16,256]{2,1,0:T(8,128)(2,1)S(1)}, bf16[2,16,256]{2,1,0:T(8,128)(2,1)S(1)}, u32[]{:S(2)}, u32[]{:S(2)}) collective-permute-start(bf16[2,16,256]{2,1,0:T(8,128)(2,1)S(1)} %pad_maximum_fusion.9), channel_id=1, source_target_pairs={{0,2},{1,3},{2,0},{3,1},{4,6},{5,7},{6,4},{7,5},{8,10},{9,11},{10,... | collective-permute-start | bytes 49160 | tf_op jit(solution)/shard_map/ppermute | solution.py:77
  85.5 4.9 %collective-permute-start.12 = (bf16[2,16,256]{2,1,0:T(8,128)(2,1)S(1)}, bf16[2,16,256]{2,1,0:T(8,128)(2,1)S(1)}, u32[]{:S(2)}, u32[]{:S(2)}) collective-permute-start(bf16[2,16,256]{2,1,0:T(8,128)(2,1)S(1)} %pad_maximum_fusion.8), channel_id=1, source_target_pairs={{0,1},{1,2},{2,3},{3,0},{4,5},{5,6},{6,7},{7,4},{8,9},{9,10},{10,1... | collective-permute-start | bytes 49160 | tf_op jit(solution)/shard_map/ppermute | solution.py:77
  86.2 4.6 %collective-permute-start.14 = (bf16[2,16,256]{2,1,0:T(8,128)(2,1)S(1)}, bf16[2,16,256]{2,1,0:T(8,128)(2,1)S(1)}, u32[]{:S(2)}, u32[]{:S(2)}) collective-permute-start(bf16[2,16,256]{2,1,0:T(8,128)(2,1)S(1)} %pad_maximum_fusion.10), channel_id=1, source_target_pairs={{0,3},{1,0},{2,1},{3,2},{4,7},{5,4},{6,5},{7,6},{8,11},{9,8},{10,9... | collective-permute-start | bytes 49160 | tf_op jit(solution)/shard_map/ppermute | solution.py:77
  93.1 4.4 %collective-permute-start.15 = (bf16[2,8,256]{2,1,0:T(8,128)(2,1)S(1)}, bf16[2,8,256]{2,1,0:T(8,128)(2,1)S(1)}, u32[]{:S(2)}, u32[]{:S(2)}) collective-permute-start(bf16[2,8,256]{2,1,0:T(8,128)(2,1)S(1)} %convolution_convert_fusion.3), channel_id=1, source_target_pairs={{0,3},{1,0},{2,1},{3,2},{4,7},{5,4},{6,5},{7,6},{8,11},{9,8},{10,9... | collective-permute-start | bytes 24584 | tf_op jit(solution)/shard_map/ppermute | solution.py:77
  96.1 5.2 %collective-permute-start.16 = (bf16[2,8,256]{2,1,0:T(8,128)(2,1)S(1)}, bf16[2,8,256]{2,1,0:T(8,128)(2,1)S(1)}, u32[]{:S(2)}, u32[]{:S(2)}) collective-permute-start(bf16[2,8,256]{2,1,0:T(8,128)(2,1)S(1)} %convolution_convert_fusion.2), channel_id=1, source_target_pairs={{0,2},{1,3},{2,0},{3,1},{4,6},{5,7},{6,4},{7,5},{8,10},{9,11},{10,... | collective-permute-start | bytes 24584 | tf_op jit(solution)/shard_map/ppermute | solution.py:77
  96.3 5.0 %collective-permute-start.17 = (bf16[2,8,256]{2,1,0:T(8,128)(2,1)S(1)}, bf16[2,8,256]{2,1,0:T(8,128)(2,1)S(1)}, u32[]{:S(2)}, u32[]{:S(2)}) collective-permute-start(bf16[2,8,256]{2,1,0:T(8,128)(2,1)S(1)} %convolution_convert_fusion.1), channel_id=1, source_target_pairs={{0,1},{1,2},{2,3},{3,0},{4,5},{5,6},{6,7},{7,4},{8,9},{9,10},{10,1... | collective-permute-start | bytes 24584 | tf_op jit(solution)/shard_map/ppermute | solution.py:77
  101.2 3.1 %collective-permute-start.18 = (bf16[8,8,256]{2,1,0:T(8,128)(2,1)S(1)}, bf16[8,8,256]{2,1,0:T(8,128)(2,1)S(1)}, u32[]{:S(2)}, u32[]{:S(2)}) collective-permute-start(bf16[8,8,256]{2,1,0:T(8,128)(2,1)S(1)} %pad_maximum_fusion.4), channel_id=1, source_target_pairs={{4,0},{8,4},{12,8},{16,12},{20,16},{24,20},{28,24},{32,28},{36,32}... | collective-permute-start | bytes 98312 | tf_op jit(solution)/shard_map/ppermute | solution.py:168
  137.9 20.4 %collective-permute-start.20 = (bf16[2,256,256]{2,1,0:T(8,128)(2,1)S(1)}, bf16[2,256,256]{2,1,0:T(8,128)(2,1)S(1)}, u32[]{:S(2)}, u32[]{:S(2)}) collective-permute-start(bf16[2,256,256]{2,1,0:T(8,128)(2,1)S(1)} %copy_bitcast_fusion), channel_id=1, source_target_pairs={{0,1},{1,2},{2,3},{3,0},{4,5},{5,6},{6,7},{7,4},{8,9},{9,10},{10,1... | collective-permute-start | bytes 786440 | tf_op jit(solution)/shard_map/ppermute | solution.py:190
  138.0 20.5 %collective-permute-start.19 = (bf16[2,256,256]{2,1,0:T(8,128)(2,1)S(1)}, bf16[2,256,256]{2,1,0:T(8,128)(2,1)S(1)}, u32[]{:S(2)}, u32[]{:S(2)}) collective-permute-start(bf16[2,256,256]{2,1,0:T(8,128)(2,1)S(1)} %copy_bitcast_fusion), channel_id=1, source_target_pairs={{1,0},{2,1},{3,2},{0,3},{5,4},{6,5},{7,6},{4,7},{9,8},{10,9},{11,1... | collective-permute-start | bytes 786440 | tf_op jit(solution)/shard_map/ppermute | solution.py:191
  141.8 16.4 %all-to-all-start.2 = ((f32[32,1,2]{2,1,0:T(1,128)}), f32[32,1,2]{2,1,0:T(1,128)S(1)}, u32[]{:S(2)}, u32[]{:S(2)}) async-start(f32[32,1,2]{2,1,0:T(1,128)} %broadcast_in_dim.4), calls=%async_computation.2 | async-start | bytes 32768 | tf_op jit(solution)/shard_map/all_to_all | solution.py:184
  158.3 6.4 %collective-permute-start.21 = (bf16[1,256,256]{2,1,0:T(8,128)(2,1)S(1)}, bf16[1,256,256]{2,1,0:T(8,128)(2,1)S(1)}, u32[]{:S(2)}, u32[]{:S(2)}) collective-permute-start(bf16[1,256,256]{2,1,0:T(8,128)(2,1)S(1)} %slice.266), channel_id=1, source_target_pairs={{0,1},{1,2},{2,3},{3,0},{4,5},{5,6},{6,7},{7,4},{8,9},{9,10},{10,1... | collective-permute-start | bytes 393224 | tf_op jit(solution)/shard_map/ppermute | solution.py:192
  158.5 6.2 %collective-permute-start.22 = (bf16[1,256,256]{2,1,0:T(8,128)(2,1)S(1)}, bf16[1,256,256]{2,1,0:T(8,128)(2,1)S(1)}, u32[]{:S(2)}, u32[]{:S(2)}) collective-permute-start(bf16[1,256,256]{2,1,0:T(8,128)(2,1)S(1)} %slice.267), channel_id=1, source_target_pairs={{1,0},{2,1},{3,2},{0,3},{5,4},{6,5},{7,6},{4,7},{9,8},{10,9},{11,1... | collective-permute-start | bytes 393224 | tf_op jit(solution)/shard_map/ppermute | solution.py:192
